TPU v7x, 16 devices: a whole 2x2x2 slice. The times are simulated.
16 devices in a mesh: dp: 4 (over z, y), tp: 4 (over x, core).
Axes of the slice: x: 2, y: 2, z: 2, core: 2. Of those that a mesh axis runs over, the one named last changes fastest.
Arguments:
- y_one: float32 [16, 256, 768], P('dp'), parts along dimension 0
- y_two: float32 [16, 256, 768], P('dp'), parts along dimension 0
- dy_one: float32 [16, 256, 768], P('dp'), parts along dimension 0
- dy_two: float32 [16, 256, 768], P('dp'), parts along dimension 0
- saved_one: float32 [4, 16, 256, 768], P(None, 'dp'), parts along dimension 1
- saved_two: float32 [4, 16, 256, 768], P(None, 'dp'), parts along dimension 1
- w_qkv: bfloat16 [9, 768, 3, 12, 64], P(None, None, None, 'tp')
- w_o: bfloat16 [9, 12, 64, 768], P(None, 'tp')
- w_in: bfloat16 [9, 768, 3072], P(None, None, 'tp')
- w_out: bfloat16 [9, 3072, 768], P(None, 'tp')
Outputs:
- output 1: float32 [16, 256, 768], P('dp'), parts along dimension 0
- output 2: float32 [16, 256, 768], P('dp'), parts along dimension 0
- output 3: float32 [16, 256, 768], P('dp'), parts along dimension 0
- output 4: float32 [16, 256, 768], P('dp'), parts along dimension 0
- output 5: float32 [36, 768, 3, 12, 64], P('dp', None, None, 'tp'), parts along dimension 0
- output 6: float32 [36, 12, 64, 768], P('dp', 'tp'), parts along dimension 0
- output 7: float32 [36, 768, 3072], P('dp', None, 'tp'), parts along dimension 0
- output 8: float32 [36, 3072, 768], P('dp', 'tp'), parts along dimension 0
There are 4 independent parts. A program takes and returns all parts, laid end to end along the dimension named above; an argument that names none is the same for every part.
All inputs are finite; a program needn't handle non-finite values.
Results may differ from a plain program's by a relative error of at most 0.0148571.
Values are sent between devices in bfloat16 or wider.
A program may use at most 1 GiB of HBM per device.

v0:
```python
import jax
import jax.numpy as jnp
from jax import lax
from jax.sharding import PartitionSpec as P

EPS = 1e-6


def rms_norm(state):
    return state * lax.rsqrt(jnp.mean(state * state, axis=-1, keepdims=True) + EPS)


def gelu_tanh(hidden):
    return jax.nn.gelu(hidden, approximate=True)


def attn_forward(normed, w_qkv):
    head_dim = w_qkv.shape[-1]
    qkv_all = jnp.einsum("bsh,hkne->kbsne", normed, w_qkv, preferred_element_type=jnp.float32).astype(jnp.bfloat16)
    scores = jnp.einsum("bqne,bkne->bnqk", qkv_all[0], qkv_all[1], preferred_element_type=jnp.float32) * head_dim ** -0.5
    attn_probs = jax.nn.softmax(scores, axis=-1)
    probs_bf = attn_probs.astype(jnp.bfloat16)
    heads_out = jnp.einsum("bnqk,bkne->bqne", probs_bf, qkv_all[2], preferred_element_type=jnp.float32).astype(jnp.bfloat16)
    return qkv_all, attn_probs, probs_bf, heads_out


def attn_backward(normed, w_qkv, w_o, attn_cache, d_out):
    qkv_all, attn_probs, probs_bf, heads_out = attn_cache
    head_dim = w_qkv.shape[-1]
    d_bf = d_out.astype(jnp.bfloat16)
    d_wo = jnp.einsum("bqne,bqh->neh", heads_out, d_bf, preferred_element_type=jnp.float32)
    d_heads = jnp.einsum("bqh,neh->bqne", d_bf, w_o, preferred_element_type=jnp.float32).astype(jnp.bfloat16)
    d_v = jnp.einsum("bnqk,bqne->bkne", probs_bf, d_heads, preferred_element_type=jnp.float32)
    d_probs = jnp.einsum("bqne,bkne->bnqk", d_heads, qkv_all[2], preferred_element_type=jnp.float32)
    d_scores = attn_probs * (d_probs - jnp.sum(d_probs * attn_probs, axis=-1, keepdims=True)) * head_dim ** -0.5
    ds_bf = d_scores.astype(jnp.bfloat16)
    d_q = jnp.einsum("bnqk,bkne->bqne", ds_bf, qkv_all[1], preferred_element_type=jnp.float32)
    d_k = jnp.einsum("bnqk,bqne->bkne", ds_bf, qkv_all[0], preferred_element_type=jnp.float32)
    d_qkv = jnp.stack([d_q.astype(jnp.bfloat16), d_k.astype(jnp.bfloat16), d_v.astype(jnp.bfloat16)], axis=2)
    d_wqkv = jnp.einsum("bsh,bskne->hkne", normed, d_qkv, preferred_element_type=jnp.float32)
    d_normed = jnp.einsum("bskne,hkne->bsh", d_qkv, w_qkv, preferred_element_type=jnp.float32)
    return d_normed, d_wqkv, d_wo


def mlp_forward(normed, w_in):
    hidden = jnp.einsum("bsh,hf->bsf", normed, w_in, preferred_element_type=jnp.float32)
    gelu_out, gelu_pull = jax.vjp(gelu_tanh, hidden)
    return gelu_out.astype(jnp.bfloat16), gelu_pull


def mlp_backward(normed, w_in, w_out, act_bf, gelu_pull, d_out):
    d_bf = d_out.astype(jnp.bfloat16)
    d_wout = jnp.einsum("bsf,bsh->fh", act_bf, d_bf, preferred_element_type=jnp.float32)
    d_act = jnp.einsum("bsh,fh->bsf", d_bf, w_out, preferred_element_type=jnp.float32)
    d_hidden = gelu_pull(d_act)[0].astype(jnp.bfloat16)
    d_win = jnp.einsum("bsh,bsf->hf", normed, d_hidden, preferred_element_type=jnp.float32)
    d_normed = jnp.einsum("bsf,hf->bsh", d_hidden, w_in, preferred_element_type=jnp.float32)
    return d_normed, d_win, d_wout


def reversible_block(block_w, y_one, y_two, d_one, d_two, want_x_one):
    w_qkv, w_o, w_in, w_out = block_w
    g_norm, g_norm_pull = jax.vjp(rms_norm, y_one)
    g_in = g_norm.astype(jnp.bfloat16)
    act_bf, gelu_pull = mlp_forward(g_in, w_in)
    g_part = jnp.einsum("bsf,fh->bsh", act_bf, w_out, preferred_element_type=jnp.float32)
    x_two = y_two - lax.psum(g_part, "tp")
    g_back, d_win, d_wout = mlp_backward(g_in, w_in, w_out, act_bf, gelu_pull, d_two)
    d_one = d_one + g_norm_pull(lax.psum(g_back, "tp"))[0]
    f_norm, f_norm_pull = jax.vjp(rms_norm, x_two)
    f_in = f_norm.astype(jnp.bfloat16)
    attn_cache = attn_forward(f_in, w_qkv)
    x_one = None
    if want_x_one:
        f_part = jnp.einsum("bqne,neh->bqh", attn_cache[3], w_o, preferred_element_type=jnp.float32)
        x_one = y_one - lax.psum(f_part, "tp")
    f_back, d_wqkv, d_wo = attn_backward(f_in, w_qkv, w_o, attn_cache, d_one)
    d_two = d_two + f_norm_pull(lax.psum(f_back, "tp"))[0]
    return x_one, x_two, d_one, d_two, (d_wqkv, d_wo, d_win, d_wout)


def plain_block(block_w, x_one, x_two, d_one, d_two):
    w_qkv, w_o, w_in, w_out = block_w
    f_norm, f_norm_pull = jax.vjp(rms_norm, x_two)
    f_in = f_norm.astype(jnp.bfloat16)
    attn_cache = attn_forward(f_in, w_qkv)
    f_back, d_wqkv, d_wo = attn_backward(f_in, w_qkv, w_o, attn_cache, d_one)
    g_norm, g_norm_pull = jax.vjp(rms_norm, x_one)
    g_in = g_norm.astype(jnp.bfloat16)
    act_bf, gelu_pull = mlp_forward(g_in, w_in)
    g_back, d_win, d_wout = mlp_backward(g_in, w_in, w_out, act_bf, gelu_pull, d_two)
    new_one = d_one + g_norm_pull(lax.psum(g_back, "tp"))[0]
    new_two = d_two + f_norm_pull(lax.psum(f_back, "tp"))[0]
    return new_one, new_two, (d_wqkv, d_wo, d_win, d_wout)


def solution(mesh):
    act_spec = P("dp", None, None)
    saved_spec = P(None, "dp", None, None)
    weight_specs = (P(None, None, None, "tp", None), P(None, "tp", None, None), P(None, None, "tp"), P(None, "tp", None))
    grad_specs = (P("dp", None, None, "tp", None), P("dp", "tp", None, None), P("dp", None, "tp"), P("dp", "tp", None))

    def per_device(y_one, y_two, dy_one, dy_two, saved_one, saved_two, w_qkv, w_o, w_in, w_out):
        all_w = (w_qkv, w_o, w_in, w_out)
        n_layers = w_qkv.shape[0]
        n_pairs = saved_one.shape[0]
        grad_list = [None] * n_layers
        top_w = tuple(weight[n_layers - 1] for weight in all_w)
        x_one, x_two, d_one, d_two, top_grads = reversible_block(top_w, y_one, y_two, dy_one, dy_two, n_pairs == 0)
        grad_list[n_layers - 1] = top_grads
        for pair_idx in reversed(range(n_pairs)):
            plain_w = tuple(weight[2 * pair_idx + 1] for weight in all_w)
            d_one, d_two, plain_grads = plain_block(plain_w, saved_one[pair_idx], saved_two[pair_idx], d_one, d_two)
            grad_list[2 * pair_idx + 1] = plain_grads
            rev_w = tuple(weight[2 * pair_idx] for weight in all_w)
            x_one, x_two, d_one, d_two, rev_grads = reversible_block(rev_w, saved_one[pair_idx], saved_two[pair_idx], d_one, d_two, pair_idx == 0)
            grad_list[2 * pair_idx] = rev_grads
        stacked = tuple(jnp.stack([entry[slot_idx] for entry in grad_list]) for slot_idx in range(4))
        return (x_one, x_two, d_one, d_two) + stacked

    return jax.shard_map(
        per_device,
        mesh=mesh,
        in_specs=(act_spec,) * 4 + (saved_spec,) * 2 + weight_specs,
        out_specs=(act_spec,) * 4 + grad_specs,
        check_vma=False,
    )
```

profile of v0, /device:TPU:0, one launch (start us, length us, event | category | flops | bytes accessed | tf_op | source)
XLA Modules:
  0.0 1912.5 jit_solution(12940328331144147934)
XLA Ops:
  12.8 6.0 fusion.766
  42.3 104.9 %all-reduce.39.cloned.1.call-done = (f32[4,256,768]{2,1,0:T(8,128)}, f32[4,256,768]{2,1,0:T(8,128)}) async-done(((f32[4,256,768]{2,1,0:T(8,128)}, f32[4,256,768]{2,1,0:T(8,128)}), (f32[4,256,768]{2,1,0:T(8,128)}, f32[4,256,768]{2,1,0:T(8,128)})) %all-reduce.39.cloned.1.call-update) | async-done | bytes 6291472 | tf_op jit(solution)/shard_map/psum | solution.py:67
  187.4 6.7 fusion.676
  211.3 6.5 fusion.759
  222.9 98.4 %all-reduce.37.cloned.1.call-done = (f32[4,256,768]{2,1,0:T(8,128)}, f32[4,256,768]{2,1,0:T(8,128)}) async-done(((f32[4,256,768]{2,1,0:T(8,128)}, f32[4,256,768]{2,1,0:T(8,128)}), (f32[4,256,768]{2,1,0:T(8,128)}, f32[4,256,768]{2,1,0:T(8,128)})) %all-reduce.37.cloned.1.call-update) | async-done | bytes 6291472 | tf_op jit(solution)/shard_map/psum | solution.py:78
  324.1 5.9 fusion.120
  333.7 5.3 fusion.45
  364.6 155.6 %all-reduce.35.cloned.1.call-done = (f32[4,256,768]{2,1,0:T(8,128)}, f32[4,256,768]{2,1,0:T(8,128)}, f32[4,256,768]{2,1,0:T(8,128)}) async-done(((f32[4,256,768]{2,1,0:T(8,128)}, f32[4,256,768]{2,1,0:T(8,128)}, f32[4,256,768]{2,1,0:T(8,128)}), (f32[4,256,768]{2,1,0:T(8,128)}, f32[4,256,768]{2,1,0:T(8,128)}, f32[4,256,768]{2,1,0:T(8,128)})) %all-reduce.35.cloned.1.call-update) | async-done | bytes 9437200 | tf_op jit(solution)/shard_map/psum | solution.py:92
  520.3 7.3 fusion.102
  548.7 6.6 fusion.679
  555.3 6.6 fusion.682
  568.5 6.6 fusion.685
  575.1 6.6 fusion.688
  599.4 6.4 fusion.747
  610.7 100.3 %all-reduce.33.cloned.1.call-done = (f32[4,256,768]{2,1,0:T(8,128)}, f32[4,256,768]{2,1,0:T(8,128)}) async-done(((f32[4,256,768]{2,1,0:T(8,128)}, f32[4,256,768]{2,1,0:T(8,128)}), (f32[4,256,768]{2,1,0:T(8,128)}, f32[4,256,768]{2,1,0:T(8,128)})) %all-reduce.33.cloned.1.call-update) | async-done | bytes 6291472 | tf_op jit(solution)/shard_map/psum | solution.py:78
  720.7 5.3 fusion.59
  750.5 156.7 %all-reduce.31.cloned.1.call-done = (f32[4,256,768]{2,1,0:T(8,128)}, f32[4,256,768]{2,1,0:T(8,128)}, f32[4,256,768]{2,1,0:T(8,128)}) async-done(((f32[4,256,768]{2,1,0:T(8,128)}, f32[4,256,768]{2,1,0:T(8,128)}, f32[4,256,768]{2,1,0:T(8,128)}), (f32[4,256,768]{2,1,0:T(8,128)}, f32[4,256,768]{2,1,0:T(8,128)}, f32[4,256,768]{2,1,0:T(8,128)})) %all-reduce.31.cloned.1.call-update) | async-done | bytes 9437200 | tf_op jit(solution)/shard_map/psum | solution.py:67
  946.6 6.6 fusion.691
  953.2 6.6 fusion.694
  977.3 6.5 fusion.735
  988.7 100.2 %all-reduce.29.cloned.1.call-done = (f32[4,256,768]{2,1,0:T(8,128)}, f32[4,256,768]{2,1,0:T(8,128)}) async-done(((f32[4,256,768]{2,1,0:T(8,128)}, f32[4,256,768]{2,1,0:T(8,128)}), (f32[4,256,768]{2,1,0:T(8,128)}, f32[4,256,768]{2,1,0:T(8,128)})) %all-reduce.29.cloned.1.call-update) | async-done | bytes 6291472 | tf_op jit(solution)/shard_map/psum | solution.py:78
  1098.7 5.3 fusion.73
  1128.5 156.7 %all-reduce.27.cloned.1.call-done = (f32[4,256,768]{2,1,0:T(8,128)}, f32[4,256,768]{2,1,0:T(8,128)}, f32[4,256,768]{2,1,0:T(8,128)}) async-done(((f32[4,256,768]{2,1,0:T(8,128)}, f32[4,256,768]{2,1,0:T(8,128)}, f32[4,256,768]{2,1,0:T(8,128)}), (f32[4,256,768]{2,1,0:T(8,128)}, f32[4,256,768]{2,1,0:T(8,128)}, f32[4,256,768]{2,1,0:T(8,128)})) %all-reduce.27.cloned.1.call-update) | async-done | bytes 9437200 | tf_op jit(solution)/shard_map/psum | solution.py:92
  1285.2 6.2 fusion.103
  1325.4 6.6 fusion.703
  1332.0 6.6 fusion.706
  1356.0 6.4 fusion.723
  1367.4 100.2 %all-reduce.25.cloned.1.call-done = (f32[4,256,768]{2,1,0:T(8,128)}, f32[4,256,768]{2,1,0:T(8,128)}) async-done(((f32[4,256,768]{2,1,0:T(8,128)}, f32[4,256,768]{2,1,0:T(8,128)}), (f32[4,256,768]{2,1,0:T(8,128)}, f32[4,256,768]{2,1,0:T(8,128)})) %all-reduce.25.cloned.1.call-update) | async-done | bytes 6291472 | tf_op jit(solution)/shard_map/psum | solution.py:78
  1564.3 133.5 %all-reduce.23.cloned.1.call-done = (f32[4,256,768]{2,1,0:T(8,128)}, f32[4,256,768]{2,1,0:T(8,128)}, f32[4,256,768]{2,1,0:T(8,128)}) async-done(((f32[4,256,768]{2,1,0:T(8,128)}, f32[4,256,768]{2,1,0:T(8,128)}, f32[4,256,768]{2,1,0:T(8,128)}), (f32[4,256,768]{2,1,0:T(8,128)}, f32[4,256,768]{2,1,0:T(8,128)}, f32[4,256,768]{2,1,0:T(8,128)})) %all-reduce.23.cloned.1.call-update) | async-done | bytes 9437200 | tf_op jit(solution)/shard_map/psum | solution.py:67
  1722.2 6.6 fusion.718
  1728.8 6.6 fusion.715
  1807.1 89.0 %all-reduce.21.cloned.1.call-done = (f32[4,256,768]{2,1,0:T(8,128)}, f32[4,256,768]{2,1,0:T(8,128)}) async-done(((f32[4,256,768]{2,1,0:T(8,128)}, f32[4,256,768]{2,1,0:T(8,128)}), (f32[4,256,768]{2,1,0:T(8,128)}, f32[4,256,768]{2,1,0:T(8,128)})) %all-reduce.21.cloned.1.call-update) | async-done | bytes 6291472 | tf_op jit(solution)/shard_map/psum | solution.py:76
  (667 shorter events, 560.6 us)
Async XLA Ops:
  7.2 140.0 %all-reduce.39.cloned.1.call-start = ((), (), s32[]{:S(2)}) async-start(), calls=%async_computation.9 | async-start | bytes 12582912 | tf_op jit(solution)/shard_map/psum | solution.py:67
  10.0 141.8 %copy-start.132 = (f32[4,256]{1,0:T(4,128)}, f32[4,256]{1,0:T(4,128)S(1)}, u32[]{:S(2)}) copy-start(f32[4,256]{1,0:T(4,128)S(1)} %fusion.930) | copy-start | bytes 12292
  28.6 292.7 %all-reduce.37.cloned.1.call-start = ((), (), s32[]{:S(2)}) async-start(), calls=%async_computation.8 | async-start | bytes 12582912 | tf_op jit(solution)/shard_map/psum | solution.py:78
  187.4 8.4 copy-start.48
  205.2 315.1 %all-reduce.35.cloned.1.call-start = ((), (), s32[]{:S(2)}) async-start(), calls=%async_computation.7 | async-start | bytes 18874368 | tf_op jit(solution)/shard_map/psum | solution.py:92
  207.6 320.0 %copy-start.125 = (f32[4,256]{1,0:T(4,128)}, f32[4,256]{1,0:T(4,128)S(1)}, u32[]{:S(2)}) copy-start(f32[4,256]{1,0:T(4,128)S(1)} %fusion.932) | copy-start | bytes 12292
  217.8 103.5 %copy-start.3 = (f32[4,256,768]{2,1,0:T(8,128)S(1)}, f32[4,256,768]{2,1,0:T(8,128)}, u32[]{:S(2)}) copy-start(f32[4,256,768]{2,1,0:T(8,128)} %copy-done.2) | copy-start | bytes 9437188
  330.1 24.0 %copy-start.139 = (f32[4,256]{1,0:T(4,128)}, f32[4,256]{1,0:T(4,128)S(1)}, u32[]{:S(2)}) copy-start(f32[4,256]{1,0:T(4,128)S(1)} %get-tuple-element.13) | copy-start | bytes 12292
  333.7 10.3 copy-start.84
  354.0 357.0 %all-reduce.33.cloned.1.call-start = ((), (), s32[]{:S(2)}) async-start(), calls=%async_computation.6 | async-start | bytes 12582912 | tf_op jit(solution)/shard_map/psum | solution.py:78
  520.3 7.3 copy-start.19
  520.3 7.4 copy-start.22
  520.3 8.3 copy-start.23
  539.2 177.3 %copy-start.6 = (f32[4,256,768]{2,1,0:T(8,128)}, f32[4,256,768]{2,1,0:T(8,128)S(1)}, u32[]{:S(2)}) copy-start(f32[4,256,768]{2,1,0:T(8,128)S(1)} %get-tuple-element.64) | copy-start | bytes 9437188
  595.0 312.2 %all-reduce.31.cloned.1.call-start = ((), (), s32[]{:S(2)}) async-start(), calls=%async_computation.5 | async-start | bytes 18874368 | tf_op jit(solution)/shard_map/psum | solution.py:67
  595.7 316.1 %copy-start.127 = (f32[4,256]{1,0:T(4,128)}, f32[4,256]{1,0:T(4,128)S(1)}, u32[]{:S(2)}) copy-start(f32[4,256]{1,0:T(4,128)S(1)} %fusion.935) | copy-start | bytes 12292
  720.7 10.3 copy-start.87
  740.9 348.0 %all-reduce.29.cloned.1.call-start = ((), (), s32[]{:S(2)}) async-start(), calls=%async_computation.4 | async-start | bytes 12582912 | tf_op jit(solution)/shard_map/psum | solution.py:78
  937.7 156.7 %copy-start.8 = (f32[4,256,768]{2,1,0:T(8,128)}, f32[4,256,768]{2,1,0:T(8,128)S(1)}, u32[]{:S(2)}) copy-start(f32[4,256,768]{2,1,0:T(8,128)S(1)} %get-tuple-element.58) | copy-start | bytes 9437188
  972.9 312.2 %all-reduce.27.cloned.1.call-start = ((), (), s32[]{:S(2)}) async-start(), calls=%async_computation.3 | async-start | bytes 18874368 | tf_op jit(solution)/shard_map/psum | solution.py:92
  973.6 317.8 %copy-start.129 = (f32[4,256]{1,0:T(4,128)}, f32[4,256]{1,0:T(4,128)S(1)}, u32[]{:S(2)}) copy-start(f32[4,256]{1,0:T(4,128)S(1)} %fusion.938) | copy-start | bytes 12292
  1098.6 10.3 copy-start.90
  1118.9 348.8 %all-reduce.25.cloned.1.call-start = ((), (), s32[]{:S(2)}) async-start(), calls=%async_computation.2 | async-start | bytes 12582912 | tf_op jit(solution)/shard_map/psum | solution.py:78
  1285.2 7.4 copy-start.46
  1316.5 156.6 %copy-start.10 = (f32[4,256,768]{2,1,0:T(8,128)}, f32[4,256,768]{2,1,0:T(8,128)S(1)}, u32[]{:S(2)}) copy-start(f32[4,256,768]{2,1,0:T(8,128)S(1)} %get-tuple-element.52) | copy-start | bytes 9437188
  1351.7 346.2 %all-reduce.23.cloned.1.call-start = ((), (), s32[]{:S(2)}) async-start(), calls=%async_computation.1 | async-start | bytes 18874368 | tf_op jit(solution)/shard_map/psum | solution.py:67
  1477.4 17.9 copy-start.92
  1504.2 15.1 slice-start
  1509.2 10.1 slice-start.1
  1531.5 364.6 %all-reduce.21.cloned.1.call-start = ((), (), s32[]{:S(2)}) async-start(), calls=%async_computation | async-start | bytes 12582912 | tf_op jit(solution)/shard_map/psum | solution.py:76
  1701.2 200.3 %copy-start.5 = (f32[4,256,768]{2,1,0:T(8,128)}, f32[4,256,768]{2,1,0:T(8,128)S(1)}, u32[]{:S(2)}) copy-start(f32[4,256,768]{2,1,0:T(8,128)S(1)} %get-tuple-element.48) | copy-start | bytes 9437188
  1784.1 9.2 copy-start.198
  (202 other events, 737.2 us)
Sparse Core Ops, SparseCore 0:
  28.7 118.4 all-reduce.38
  205.3 115.8 all-reduce.36
  354.1 166.1 all-reduce.34
  595.1 115.8 all-reduce.32
  741.0 166.1 all-reduce.30
  973.1 115.8 all-reduce.28
  1119.0 166.1 all-reduce.26
  1351.8 115.8 all-reduce.24
  1531.6 166.1 all-reduce.22
  1780.3 115.8 all-reduce.20
where the time goes:
time: 1920 us; the launch traced here: 1910 us
  waiting for transfers between devices  1200 us (62%)
  matrix products  513 us (27%)
  other arithmetic  146 us (8%)
  local copies, waits for them, and re-layouts  39.7 us (2%)
    psum x4, waiting for transfers between devices, reversible_block(): d_two = d_two + f_norm_pull(lax.psum(f_back, 'tp'))[0]  399 us
    psum x3, waiting for transfers between devices, reversible_block(): x_two = y_two - lax.psum(g_part, 'tp')  395 us
    psum x2, waiting for transfers between devices, plain_block(): new_one = d_one + g_norm_pull(lax.psum(g_back, 'tp'))[0]  312 us
    psum x1, waiting for transfers between devices, reversible_block(): x_one = y_one - lax.psum(f_part, 'tp')  89 us
    dot_general x9, matrix products, attn_backward(): jnp.einsum('bnqk,bkne->bqne', ds_bf, qkv_all[1], preferred_element_type=j...  53.9 us
    dot_general x9, matrix products, attn_backward(): jnp.einsum('bnqk,bqne->bkne', ds_bf, qkv_all[0], preferred_element_type=j...  52.1 us
    dot_general x9, matrix products, mlp_forward(): jnp.einsum('bsh,hf->bsf', normed, w_in, preferred_element_type=jnp.float32)  43.2 us
    dot_general x9, matrix products, mlp_backward(): jnp.einsum('bsh,fh->bsf', d_bf, w_out, preferred_element_type=jnp.float32)  42.9 us
  transfers between devices with their start and end apart: 10, of which 10 were waited for; matrix products, arithmetic and copies ran while one was open for 8% of the time, Pallas kernels for 0%

commit v1 on v0

--- a/solution.py
+++ b/solution.py
@@ -66,7 +66,7 @@
     g_part = jnp.einsum("bsf,fh->bsh", act_bf, w_out, preferred_element_type=jnp.float32)
     x_two = y_two - lax.psum(g_part, "tp")
     g_back, d_win, d_wout = mlp_backward(g_in, w_in, w_out, act_bf, gelu_pull, d_two)
-    d_one = d_one + g_norm_pull(lax.psum(g_back, "tp"))[0]
+    d_one = d_one + g_norm_pull(lax.psum(g_back.astype(jnp.bfloat16), "tp").astype(jnp.float32))[0]
     f_norm, f_norm_pull = jax.vjp(rms_norm, x_two)
     f_in = f_norm.astype(jnp.bfloat16)
     attn_cache = attn_forward(f_in, w_qkv)
@@ -75,7 +75,7 @@
         f_part = jnp.einsum("bqne,neh->bqh", attn_cache[3], w_o, preferred_element_type=jnp.float32)
         x_one = y_one - lax.psum(f_part, "tp")
     f_back, d_wqkv, d_wo = attn_backward(f_in, w_qkv, w_o, attn_cache, d_one)
-    d_two = d_two + f_norm_pull(lax.psum(f_back, "tp"))[0]
+    d_two = d_two + f_norm_pull(lax.psum(f_back.astype(jnp.bfloat16), "tp").astype(jnp.float32))[0]
     return x_one, x_two, d_one, d_two, (d_wqkv, d_wo, d_win, d_wout)
 
 
@@ -89,8 +89,8 @@
     g_in = g_norm.astype(jnp.bfloat16)
     act_bf, gelu_pull = mlp_forward(g_in, w_in)
     g_back, d_win, d_wout = mlp_backward(g_in, w_in, w_out, act_bf, gelu_pull, d_two)
-    new_one = d_one + g_norm_pull(lax.psum(g_back, "tp"))[0]
-    new_two = d_two + f_norm_pull(lax.psum(f_back, "tp"))[0]
+    new_one = d_one + g_norm_pull(lax.psum(g_back.astype(jnp.bfloat16), "tp").astype(jnp.float32))[0]
+    new_two = d_two + f_norm_pull(lax.psum(f_back.astype(jnp.bfloat16), "tp").astype(jnp.float32))[0]
     return new_one, new_two, (d_wqkv, d_wo, d_win, d_wout)
 
 

time: 1920 us -> 1440 us (0.75)
  waiting for transfers between devices: 1200 us -> 710 us
    psum x6 -> x10, waiting for transfers between devices: 711 us -> 458 us  [the longest x4 225 us: plain_block(): lax.psum(g_back.astype(jnp.bfloat16), 'tp').astype(jnp.float32)]
    psum x3, waiting for transfers between devices: 395 us -> 170 us  [reversible_block(): x_two = y_two - lax.psum(g_part, 'tp')]
    unnamed x448 -> x494, local copies, waits for them, and re-layouts: 39.7 us -> 52.9 us
  transfers between devices with their start and end apart: 10 -> 14, of which waited for: 10 -> 13; matrix products, arithmetic and copies ran while one was open for 8% -> 17% of each run, Pallas kernels for 0% -> 0%
where the time goes in v1:
time: 1440 us; the launch traced here: 1430 us
  waiting for transfers between devices  710 us (49%)
  matrix products  507 us (35%)
  other arithmetic  145 us (10%)
  local copies, waits for them, and re-layouts  52.9 us (4%)
  between operations  16.7 us (1%)
    psum x4, waiting for transfers between devices, plain_block(): lax.psum(g_back.astype(jnp.bfloat16), 'tp').astype(jnp.float32)  225 us
    psum x5, waiting for transfers between devices, reversible_block(): lax.psum(f_back.astype(jnp.bfloat16), 'tp').astype(jnp.float32)  214 us
    psum x3, waiting for transfers between devices, reversible_block(): x_two = y_two - lax.psum(g_part, 'tp')  170 us
    psum x1, waiting for transfers between devices, reversible_block(): x_one = y_one - lax.psum(f_part, 'tp')  81.1 us
    dot_general x9, matrix products, attn_backward(): jnp.einsum('bnqk,bkne->bqne', ds_bf, qkv_all[1], preferred_element_type=j...  57.7 us
    dot_general x9, matrix products, attn_backward(): jnp.einsum('bnqk,bqne->bkne', ds_bf, qkv_all[0], preferred_element_type=j...  55.7 us
    unnamed x494, local copies, waits for them, and re-layouts  52.9 us
    dot_general x9, matrix products, mlp_backward(): jnp.einsum('bsh,fh->bsf', d_bf, w_out, preferred_element_type=jnp.float32)  43.2 us
  transfers between devices with their start and end apart: 14, of which 13 were waited for; matrix products, arithmetic and copies ran while one was open for 17% of the time, Pallas kernels for 0%

profile of v1, /device:TPU:0, one launch (start us, length us, event | category | flops | bytes accessed | tf_op | source)
XLA Modules:
  0.0 1432.0 jit_solution(8595072071141704347)
XLA Ops:
  45.7 19.5 %all-reduce.27.cloned.1.call-done = bf16[4,256,768]{2,1,0:T(8,128)(2,1)} async-done(((bf16[4,256,768]{2,1,0:T(8,128)(2,1)}), bf16[4,256,768]{2,1,0:T(8,128)(2,1)}) %all-reduce.27.cloned.1.call-update) | async-done | bytes 1572880 | tf_op jit(solution)/shard_map/psum | solution.py:69
  74.9 6.6 fusion.679
  81.5 6.6 fusion.682
  96.2 36.5 %all-reduce.29.cloned.1.call-done = f32[4,256,768]{2,1,0:T(8,128)} async-done(((f32[4,256,768]{2,1,0:T(8,128)}), f32[4,256,768]{2,1,0:T(8,128)}) %all-reduce.29.cloned.1.call-update) | async-done | bytes 3145744 | tf_op jit(solution)/shard_map/psum | solution.py:67
  144.9 6.6 fusion.673
  151.5 6.7 fusion.676
  171.3 6.5 fusion.758
  182.7 49.0 %all-reduce.51.cloned.1.call-done = (bf16[4,256,768]{2,1,0:T(8,128)(2,1)}, bf16[4,256,768]{2,1,0:T(8,128)(2,1)}) async-done(((bf16[4,256,768]{2,1,0:T(8,128)(2,1)}, bf16[4,256,768]{2,1,0:T(8,128)(2,1)}), (bf16[4,256,768]{2,1,0:T(8,128)(2,1)}, bf16[4,256,768]{2,1,0:T(8,128)(2,1)})) %all-reduce.51.cloned.1.call-update) | async-done | bytes 3145744 | tf_op jit(solution)/shard_map/psum | solution.py:78
  234.7 5.9 fusion.129
  274.8 53.9 %all-reduce.49.cloned.1.call-done = (bf16[4,256,768]{2,1,0:T(8,128)(2,1)}, bf16[4,256,768]{2,1,0:T(8,128)(2,1)}) async-done(((bf16[4,256,768]{2,1,0:T(8,128)(2,1)}, bf16[4,256,768]{2,1,0:T(8,128)(2,1)}), (bf16[4,256,768]{2,1,0:T(8,128)(2,1)}, bf16[4,256,768]{2,1,0:T(8,128)(2,1)})) %all-reduce.49.cloned.1.call-update) | async-done | bytes 3145744 | tf_op jit(solution)/shard_map/psum | solution.py:92
  328.7 6.3 fusion.119
  366.3 6.7 fusion.694
  379.2 82.0 %all-reduce.35.cloned.1.call-done = (f32[4,256,768]{2,1,0:T(8,128)}, f32[4,256,768]{2,1,0:T(8,128)}) async-done(((f32[4,256,768]{2,1,0:T(8,128)}, f32[4,256,768]{2,1,0:T(8,128)}), (f32[4,256,768]{2,1,0:T(8,128)}, f32[4,256,768]{2,1,0:T(8,128)})) %all-reduce.35.cloned.1.call-update) | async-done | bytes 6291472 | tf_op jit(solution)/shard_map/psum | solution.py:67
  461.2 7.7 multiply_reduce_fusion.6
  477.8 6.6 fusion.685
  484.4 6.6 fusion.688
  512.6 52.1 %all-reduce.47.cloned.1.call-done = (bf16[4,256,768]{2,1,0:T(8,128)(2,1)}, bf16[4,256,768]{2,1,0:T(8,128)(2,1)}) async-done(((bf16[4,256,768]{2,1,0:T(8,128)(2,1)}, bf16[4,256,768]{2,1,0:T(8,128)(2,1)}), (bf16[4,256,768]{2,1,0:T(8,128)(2,1)}, bf16[4,256,768]{2,1,0:T(8,128)(2,1)})) %all-reduce.47.cloned.1.call-update) | async-done | bytes 3145744 | tf_op jit(solution)/shard_map/psum | solution.py:78
  603.9 53.1 %all-reduce.45.cloned.1.call-done = (bf16[4,256,768]{2,1,0:T(8,128)(2,1)}, bf16[4,256,768]{2,1,0:T(8,128)(2,1)}) async-done(((bf16[4,256,768]{2,1,0:T(8,128)(2,1)}, bf16[4,256,768]{2,1,0:T(8,128)(2,1)}), (bf16[4,256,768]{2,1,0:T(8,128)(2,1)}, bf16[4,256,768]{2,1,0:T(8,128)(2,1)})) %all-reduce.45.cloned.1.call-update) | async-done | bytes 3145744 | tf_op jit(solution)/shard_map/psum | solution.py:92
  673.2 6.6 fusion.700
  679.8 6.6 fusion.697
  689.8 6.6 fusion.706
  696.4 6.6 fusion.703
  726.3 53.5 %all-reduce.43.cloned.1.call-done = (bf16[4,256,768]{2,1,0:T(8,128)(2,1)}, bf16[4,256,768]{2,1,0:T(8,128)(2,1)}) async-done(((bf16[4,256,768]{2,1,0:T(8,128)(2,1)}, bf16[4,256,768]{2,1,0:T(8,128)(2,1)}), (bf16[4,256,768]{2,1,0:T(8,128)(2,1)}, bf16[4,256,768]{2,1,0:T(8,128)(2,1)})) %all-reduce.43.cloned.1.call-update) | async-done | bytes 3145744 | tf_op jit(solution)/shard_map/psum | solution.py:78
  807.6 64.6 %all-reduce.41.cloned.1.call-done = (bf16[4,256,768]{2,1,0:T(8,128)(2,1)}, bf16[4,256,768]{2,1,0:T(8,128)(2,1)}) async-done(((bf16[4,256,768]{2,1,0:T(8,128)(2,1)}, bf16[4,256,768]{2,1,0:T(8,128)(2,1)}), (bf16[4,256,768]{2,1,0:T(8,128)(2,1)}, bf16[4,256,768]{2,1,0:T(8,128)(2,1)})) %all-reduce.41.cloned.1.call-update) | async-done | bytes 3145744 | tf_op jit(solution)/shard_map/psum | solution.py:92
  900.6 51.3 %all-reduce.25.cloned.1.call-done = f32[4,256,768]{2,1,0:T(8,128)} async-done(((f32[4,256,768]{2,1,0:T(8,128)}), f32[4,256,768]{2,1,0:T(8,128)}) %all-reduce.25.cloned.1.call-update) | async-done | bytes 3145744 | tf_op jit(solution)/shard_map/psum | solution.py:67
  1002.4 81.1 %all-reduce.33.cloned.1.call-done = (f32[4,256,768]{2,1,0:T(8,128)}, f32[4,256,768]{2,1,0:T(8,128)}) async-done(((f32[4,256,768]{2,1,0:T(8,128)}, f32[4,256,768]{2,1,0:T(8,128)}), (f32[4,256,768]{2,1,0:T(8,128)}, f32[4,256,768]{2,1,0:T(8,128)})) %all-reduce.33.cloned.1.call-update) | async-done | bytes 6291472 | tf_op jit(solution)/shard_map/psum | solution.py:76
  1095.6 6.6 fusion.709
  1102.2 6.6 fusion.712
  1123.7 58.9 %all-reduce.39.cloned.1.call-done = (bf16[4,256,768]{2,1,0:T(8,128)(2,1)}, bf16[4,256,768]{2,1,0:T(8,128)(2,1)}) async-done(((bf16[4,256,768]{2,1,0:T(8,128)(2,1)}, bf16[4,256,768]{2,1,0:T(8,128)(2,1)}), (bf16[4,256,768]{2,1,0:T(8,128)(2,1)}, bf16[4,256,768]{2,1,0:T(8,128)(2,1)})) %all-reduce.39.cloned.1.call-update) | async-done | bytes 3145744 | tf_op jit(solution)/shard_map/psum | solution.py:78
  1273.1 53.6 %all-reduce.37.cloned.1.call-done = (bf16[4,256,768]{2,1,0:T(8,128)(2,1)}, bf16[4,256,768]{2,1,0:T(8,128)(2,1)}) async-done(((bf16[4,256,768]{2,1,0:T(8,128)(2,1)}, bf16[4,256,768]{2,1,0:T(8,128)(2,1)}), (bf16[4,256,768]{2,1,0:T(8,128)(2,1)}, bf16[4,256,768]{2,1,0:T(8,128)(2,1)})) %all-reduce.37.cloned.1.call-update) | async-done | bytes 3145744 | tf_op jit(solution)/shard_map/psum | solution.py:92
  1344.1 6.7 fusion.724
  1350.8 6.6 fusion.721
  (723 shorter events, 580.5 us)
Async XLA Ops:
  7.2 58.0 %all-reduce.27.cloned.1.call-start = ((), (), s32[]{:S(2)}) async-start(), calls=%async_computation.1 | async-start | bytes 3145728 | tf_op jit(solution)/shard_map/psum | solution.py:69
  10.0 57.2 %copy-start.127 = (f32[4,256]{1,0:T(4,128)}, f32[4,256]{1,0:T(4,128)S(1)}, u32[]{:S(2)}) copy-start(f32[4,256]{1,0:T(4,128)S(1)} %fusion.927) | copy-start | bytes 12292
  23.1 109.6 %all-reduce.29.cloned.1.call-start = ((), (), s32[]{:S(2)}) async-start(), calls=%async_computation.2 | async-start | bytes 6291456 | tf_op jit(solution)/shard_map/psum | solution.py:67
  29.1 202.7 %all-reduce.51.cloned.1.call-start = ((), (), s32[]{:S(2)}) async-start(), calls=%async_computation.13 | async-start | bytes 6291456 | tf_op jit(solution)/shard_map/psum | solution.py:78
  167.0 161.7 %all-reduce.49.cloned.1.call-start = ((), (), s32[]{:S(2)}) async-start(), calls=%async_computation.12 | async-start | bytes 6291456 | tf_op jit(solution)/shard_map/psum | solution.py:92
  167.6 182.3 %copy-start.130 = (f32[4,256]{1,0:T(4,128)}, f32[4,256]{1,0:T(4,128)S(1)}, u32[]{:S(2)}) copy-start(f32[4,256]{1,0:T(4,128)S(1)} %fusion.929) | copy-start | bytes 12292
  182.7 51.9 %copy-start.152 = (f32[4,256]{1,0:T(4,128)S(1)}, f32[4,256]{1,0:T(4,128)}, u32[]{:S(2)}) copy-start(f32[4,256]{1,0:T(4,128)} %copy-done.151) | copy-start | bytes 12292
  240.6 23.3 %copy-start.161 = (f32[4,256]{1,0:T(4,128)}, f32[4,256]{1,0:T(4,128)S(1)}, u32[]{:S(2)}) copy-start(f32[4,256]{1,0:T(4,128)S(1)} %get-tuple-element.13) | copy-start | bytes 12292
  241.7 103.7 %copy-start.176 = (f32[4,256]{1,0:T(4,128)}, f32[4,256]{1,0:T(4,128)S(1)}, u32[]{:S(2)}) copy-start(f32[4,256]{1,0:T(4,128)S(1)} %fusion.936) | copy-start | bytes 12292
  244.8 9.7 copy-start.89
  263.9 197.3 %all-reduce.35.cloned.1.call-start = ((), (), s32[]{:S(2)}) async-start(), calls=%async_computation.5 | async-start | bytes 12582912 | tf_op jit(solution)/shard_map/psum | solution.py:67
  345.3 219.5 %all-reduce.47.cloned.1.call-start = ((), (), s32[]{:S(2)}) async-start(), calls=%async_computation.11 | async-start | bytes 6291456 | tf_op jit(solution)/shard_map/psum | solution.py:78
  468.9 100.3 %copy-start.8 = (f32[4,256,768]{2,1,0:T(8,128)}, f32[4,256,768]{2,1,0:T(8,128)S(1)}, u32[]{:S(2)}) copy-start(f32[4,256,768]{2,1,0:T(8,128)S(1)} %get-tuple-element.70) | copy-start | bytes 9437188
  499.9 157.1 %all-reduce.45.cloned.1.call-start = ((), (), s32[]{:S(2)}) async-start(), calls=%async_computation.10 | async-start | bytes 6291456 | tf_op jit(solution)/shard_map/psum | solution.py:92
  512.6 54.0 %copy-start.164 = (f32[4,256]{1,0:T(4,128)S(1)}, f32[4,256]{1,0:T(4,128)}, u32[]{:S(2)}) copy-start(f32[4,256]{1,0:T(4,128)} %copy-done.163) | copy-start | bytes 12292
  573.1 9.7 copy-start.92
  592.2 187.7 %all-reduce.43.cloned.1.call-start = ((), (), s32[]{:S(2)}) async-start(), calls=%async_computation.9 | async-start | bytes 6291456 | tf_op jit(solution)/shard_map/psum | solution.py:78
  600.7 59.9 %copy-start.126 = (f32[4,3,256]{2,1,0:T(4,128)}, f32[4,3,256]{2,1,0:T(4,128)S(1)}, u32[]{:S(2)}) copy-start(f32[4,3,256]{2,1,0:T(4,128)S(1)} %get-tuple-element.87) | copy-start | bytes 36868
  715.1 157.1 %all-reduce.41.cloned.1.call-start = ((), (), s32[]{:S(2)}) async-start(), calls=%async_computation.8 | async-start | bytes 6291456 | tf_op jit(solution)/shard_map/psum | solution.py:92
  715.7 257.2 %copy-start.137 = (f32[4,256]{1,0:T(4,128)}, f32[4,256]{1,0:T(4,128)S(1)}, u32[]{:S(2)}) copy-start(f32[4,256]{1,0:T(4,128)S(1)} %fusion.935) | copy-start | bytes 12292
  726.3 55.5 %copy-start.160 = (f32[4,256]{1,0:T(4,128)S(1)}, f32[4,256]{1,0:T(4,128)}, u32[]{:S(2)}) copy-start(f32[4,256]{1,0:T(4,128)} %get-tuple-element.53) | copy-start | bytes 12292
  784.4 109.5 %copy-start.167 = (f32[4,256]{1,0:T(4,128)}, f32[4,256]{1,0:T(4,128)S(1)}, u32[]{:S(2)}) copy-start(f32[4,256]{1,0:T(4,128)S(1)} %get-tuple-element.98) | copy-start | bytes 12292
  788.2 9.7 copy-start.95
  807.4 144.5 %all-reduce.25.cloned.1.call-start = ((), (), s32[]{:S(2)}) async-start(), calls=%async_computation | async-start | bytes 6291456 | tf_op jit(solution)/shard_map/psum | solution.py:67
  887.1 196.4 %all-reduce.33.cloned.1.call-start = ((), (), s32[]{:S(2)}) async-start(), calls=%async_computation.4 | async-start | bytes 12582912 | tf_op jit(solution)/shard_map/psum | solution.py:76
  967.6 215.1 %all-reduce.39.cloned.1.call-start = ((), (), s32[]{:S(2)}) async-start(), calls=%async_computation.7 | async-start | bytes 6291456 | tf_op jit(solution)/shard_map/psum | solution.py:78
  1086.8 100.4 %copy-start.5 = (f32[4,256,768]{2,1,0:T(8,128)}, f32[4,256,768]{2,1,0:T(8,128)S(1)}, u32[]{:S(2)}) copy-start(f32[4,256,768]{2,1,0:T(8,128)S(1)} %get-tuple-element.46) | copy-start | bytes 9437188
  1117.8 208.9 %all-reduce.37.cloned.1.call-start = ((), (), s32[]{:S(2)}) async-start(), calls=%async_computation.6 | async-start | bytes 6291456 | tf_op jit(solution)/shard_map/psum | solution.py:92
  1123.7 60.9 %copy-start.154 = (f32[4,256]{1,0:T(4,128)S(1)}, f32[4,256]{1,0:T(4,128)}, u32[]{:S(2)}) copy-start(f32[4,256]{1,0:T(4,128)} %copy-done.153) | copy-start | bytes 12292
  1191.0 17.3 %copy-start.97 = (bf16[4,256,768]{2,1,0:T(8,128)(2,1)}, bf16[4,256,768]{2,1,0:T(8,128)(2,1)S(1)}, u32[]{:S(2)}) copy-start(bf16[4,256,768]{2,1,0:T(8,128)(2,1)S(1)} %get-tuple-element.44) | copy-start | bytes 4718596
  1261.9 155.3 %all-reduce.31.cloned.1.call-start = ((), (), s32[]{:S(2)}) async-start(), calls=%async_computation.3 | async-start | bytes 3145728 | tf_op jit(solution)/shard_map/psum | solution.py:78
  1336.3 21.0 %copy-start.7 = (f32[4,256,768]{2,1,0:T(8,128)}, f32[4,256,768]{2,1,0:T(8,128)S(1)}, u32[]{:S(2)}) copy-start(f32[4,256,768]{2,1,0:T(8,128)S(1)} %get-tuple-element.67) | copy-start | bytes 9437188
  (229 other events, 761.9 us)
Sparse Core Ops, SparseCore 0:
  23.2 41.9 all-reduce.26
  68.2 64.5 all-reduce.28
  167.1 64.6 all-reduce.50
  264.0 64.6 all-reduce.48
  345.4 115.7 all-reduce.34
  500.0 64.7 all-reduce.46
  592.3 64.6 all-reduce.44
  715.2 64.6 all-reduce.42
  807.5 64.6 all-reduce.40
  887.2 64.6 all-reduce.24
  967.7 115.7 all-reduce.32
  1117.9 64.7 all-reduce.38
  1262.0 64.6 all-reduce.36
  1366.4 39.2 all-reduce.30

commit v2 on v1

v2 whole, which is shorter than its diff:
```python
import functools

import jax
import jax.numpy as jnp
from jax import lax
from jax.experimental import pallas as pl
from jax.experimental.pallas import tpu as pltpu
from jax.sharding import PartitionSpec as P

EPS = 1e-6
BF = jnp.bfloat16
F32 = jnp.float32
MESH = pl.DeviceIdType.MESH
GELU_C = 0.7978845608028654
GELU_A = 0.044715

NN = (((1,), (0,)), ((), ()))
NT = (((1,), (1,)), ((), ()))
TN = (((0,), (0,)), ((), ()))


def dot(lhs, rhs, dims):
    return lax.dot_general(lhs, rhs, dims, preferred_element_type=F32)


def rms_scale(state):
    return lax.rsqrt(jnp.mean(state * state, axis=-1, keepdims=True) + EPS)


def rms_pull(state, grad):
    scale = rms_scale(state)
    normed = state * scale
    return scale * (grad - normed * jnp.mean(normed * grad, axis=-1, keepdims=True))


def gelu_parts(hidden, want_grad):
    sq = hidden * hidden
    tanh = jnp.tanh(GELU_C * (hidden + GELU_A * (sq * hidden)))
    half = 0.5 * (1.0 + tanh)
    value = hidden * half
    if not want_grad:
        return value, None
    grad = half + 0.5 * hidden * (1.0 - tanh * tanh) * (GELU_C * (1.0 + 3.0 * GELU_A * sq))
    return value, grad


def chain_kernel(
    seq, hid, heads, hdim, n_pairs,
    y1, y2, dy1, dy2, s1, s2, wq_h, wo_h, wi_h, wu_h,
    ox1, ox2, od1, od2, gq, go, gi, gu,
    wq, wo, wi, wu, a_g, act, gp, dhb, finp, finr, qkvt, dqkvt, pt, ot,
    d1b, d2b, d1f, d2f, vbuf, x2r, xl, pbuf, e1r, xs, xr, gbuf, g1r, g2r, stage,
    e1s_s, e1r_s, e2s_s, e2r_s, e3s_s, e3r_s, g1s_s, g1r_s, g2s_s, g2r_s, g3s_s, g3r_s,
    os_s, or_s, ol_s, w_s, xl_s, v_s, x2_s, st_s, d_s, gcred,
):
    me = lax.axis_index("tp")
    dp = lax.axis_index("dp")
    ci = lax.rem(me, 2)
    core_peer = (dp, me + 1 - 2 * ci)
    x_peer = (dp, lax.rem(me + 2, 4))
    qw = heads * hdim
    npc = 4
    prow = seq // npc

    barrier = pltpu.get_barrier_semaphore()
    pl.semaphore_signal(barrier, inc=1, device_id=core_peer, device_id_type=MESH)
    pl.semaphore_signal(barrier, inc=1, device_id=x_peer, device_id_type=MESH)
    pl.semaphore_wait(barrier, 2)

    def rows(seq_idx):
        return pl.ds(pl.multiple_of(seq_idx * seq, seq), seq)

    def mine(c):
        return 2 * c + ci

    def theirs(c):
        return 2 * c + 1 - ci

    def local(src, dst, sem):
        return pltpu.make_async_copy(src, dst, sem)

    def remote(src, dst, ssem, rsem, dev):
        return pltpu.make_async_remote_copy(src_ref=src, dst_ref=dst, send_sem=ssem, recv_sem=rsem, device_id=dev, device_id_type=MESH)

    def weight_copies(slot, blk, which):
        pairs = {"q": (wq_h, wq), "o": (wo_h, wo), "i": (wi_h, wi), "u": (wu_h, wu)}
        return [local(pairs[k][0].at[blk], pairs[k][1].at[slot], w_s.at[slot, "qoiu".index(k)]) for k in which]

    def w_start(slot, blk, which):
        for cp in weight_copies(slot, blk, which):
            cp.start()

    def w_wait(slot, which):
        for cp in weight_copies(slot, 0, which):
            cp.wait()

    def state_start(first, one, pair, rws, dst, sem):
        top, saved = (y1, s1) if one else (y2, s2)
        if first is True:
            local(top.at[rws], dst, sem).start()
        elif first is False:
            local(saved.at[pair, rws], dst, sem).start()
        else:
            @pl.when(first)
            def _():
                local(top.at[rws], dst, sem).start()

            @pl.when(jnp.logical_not(first))
            def _():
                local(saved.at[jnp.minimum(pair, n_pairs - 1), rws], dst, sem).start()

    def state_wait(dst, sem):
        local(y1.at[rows(0)], dst, sem).wait()

    def each_seq(first, one, pair, body, order=lambda i: i):
        for i in (0, 1):
            state_start(first, one, pair, rows(order(i)), xl.at[i], xl_s.at[i])

        @pl.loop(0, 4)
        def _(i):
            slot = lax.rem(i, 2)
            state_wait(xl.at[slot], xl_s.at[slot])
            body(i, order(i), xl[slot])

            @pl.when(i < 2)
            def _():
                state_start(first, one, pair, rows(order(i + 2)), xl.at[slot], xl_s.at[slot])

    def mlp_fwd(slot, first, pair):
        def body(i, s, state):
            normed = (state * rms_scale(state)).astype(BF)
            a_g[rows(s), :] = normed
            value, grad = gelu_parts(dot(normed, wi[slot], NN), True)
            act[rows(s), :] = value.astype(BF)
            gp[rows(s), :] = grad
        each_seq(first, True, pair, body)

    def attn_fwd_seq(slot, fin, s):
        cols = rows(s)
        qkv = dot(wq[slot], fin[cols, :], NT).astype(BF)
        qkvt[:, cols] = qkv
        for h in range(heads):
            q_t = qkv[h * hdim:(h + 1) * hdim]
            k_t = qkv[qw + h * hdim:qw + (h + 1) * hdim]
            v_t = qkv[2 * qw + h * hdim:2 * qw + (h + 1) * hdim]
            sc = dot(k_t, q_t, TN) * (hdim ** -0.5)
            ex = jnp.exp(sc - jnp.max(sc, axis=0, keepdims=True))
            prob = ex * (1.0 / jnp.sum(ex, axis=0, keepdims=True))
            pt[s * heads + h] = prob
            ot[h * hdim:(h + 1) * hdim, cols] = dot(v_t, prob.astype(BF), NN).astype(BF)

    def attn_fwd_plain(pair):
        def body(i, s, state):
            finp[rows(s), :] = (state * rms_scale(state)).astype(BF)
            attn_fwd_seq(0, finp, s)
        each_seq(False, False, pair, body)

    def attn_fwd_rev():
        @pl.loop(0, 4)
        def _(s):
            attn_fwd_seq(1, finr, s)

    def e1(slot, c):
        return remote(pbuf.at[c, 0], e1r.at[slot, c], e1s_s.at[slot, c], e1r_s.at[slot, c], core_peer)

    def e2(t, c):
        return remote(xs.at[t, c], xr.at[t, c], e2s_s.at[t, c], e2r_s.at[t, c], x_peer)

    def part_g(slot, ver, t, c):
        @pl.loop(0, 2)
        def _(i):
            s = 2 * c + jnp.where(i == 0, 1 - ci, ci)
            d_act = dot(d2b[ver, rows(s), :], wu[slot], NT)
            dh = (d_act * gp[rows(s), :]).astype(BF)
            dhb[rows(s), :] = dh
            pbuf[c, i] = dot(dh, wi[slot], NT)

            @pl.when(i == 0)
            def _():
                e1(t % 2, c).start()

    def part_f(slot, t, c):
        @pl.loop(0, 2)
        def _(i):
            s = 2 * c + jnp.where(i == 0, 1 - ci, ci)
            cols = rows(s)
            do_t = dot(wo[slot], d1b[cols, :], NT).astype(BF)
            for h in range(heads):
                lo = h * hdim
                do_h = do_t[lo:lo + hdim]
                prob = pt[s * heads + h]
                q_t = qkvt[lo:lo + hdim, cols]
                k_t = qkvt[qw + lo:qw + lo + hdim, cols]
                v_t = qkvt[2 * qw + lo:2 * qw + lo + hdim, cols]
                dqkvt[2 * qw + lo:2 * qw + lo + hdim, cols] = dot(do_h, prob.astype(BF), NT).astype(BF)
                dp_t = dot(v_t, do_h, TN)
                inner = jnp.sum(prob * dp_t, axis=0, keepdims=True)
                ds = (prob * (dp_t - inner) * (hdim ** -0.5)).astype(BF)
                dqkvt[lo:lo + hdim, cols] = dot(k_t, ds, NN).astype(BF)
                dqkvt[qw + lo:qw + lo + hdim, cols] = dot(q_t, ds, NT).astype(BF)
            pbuf[c, i] = dot(dqkvt[:, cols], wq[slot], TN)

            @pl.when(i == 0)
            def _():
                e1(t % 2, c).start()

    def to_x(t, c):
        e1(t % 2, c).wait()
        xs[t, c] = (pbuf[c, 1] + e1r[t % 2, c]).astype(BF)
        e2(t, c).start()

    def summed(t, c):
        e2(t, c).wait()
        return xs[t, c].astype(F32) + xr[t, c].astype(F32)

    def e3(kind, c):
        ref = d1b.at[rows(mine(c))] if kind == 0 else d2b.at[kind - 1, rows(mine(c))]
        return remote(ref, ref, e3s_s.at[kind, c], e3r_s.at[kind, c], core_peer)

    def finish(t, c, kind, acc, state):
        total = acc[c] + rms_pull(state, summed(t, c))
        acc[c] = total
        if kind is not None:
            if kind == 0:
                d1b[rows(mine(c)), :] = total.astype(BF)
            else:
                d2b[kind - 1, rows(mine(c)), :] = total.astype(BF)
            e3(kind, c).start()

    def g1(c):
        return remote(gbuf.at[c, 0], g1r.at[c], g1s_s.at[c], g1r_s.at[c], core_peer)

    def g2(k):
        c, q = k // npc, k % npc
        rws = pl.ds(q * prow, prow)
        return remote(gbuf.at[c, 1, rws], g2r.at[c, rws], g2s_s.at[k], g2r_s.at[k], x_peer)

    def g_order(i):
        return 2 * (i // 2) + jnp.where(lax.rem(i, 2) == 0, 1 - ci, ci)

    def g_send_core(i):
        for c in (0, 1):
            @pl.when(i == 2 * c)
            def _():
                g1(c).start()

    def g_part(slot, first, pair):
        def body(i, s, state):
            normed = (state * rms_scale(state)).astype(BF)
            value, _ = gelu_parts(dot(normed, wi[slot], NN), False)
            gbuf[i // 2, lax.rem(i, 2)] = dot(value.astype(BF), wu[slot], NN)
            g_send_core(i)
        each_seq(first, True, pair, body, g_order)

    def f_part(slot):
        @pl.loop(0, 4)
        def _(i):
            gbuf[i // 2, lax.rem(i, 2)] = dot(ot[:, rows(g_order(i))], wo[slot], TN)
            g_send_core(i)

    def g_chip(c):
        g1(c).wait()
        gbuf[c, 1] = gbuf[c, 1] + g1r[c]

    def g_send(*ks):
        for k in ks:
            g2(k).start()

    def g_total(c):
        for q in range(npc):
            g2(c * npc + q).wait()
        return gbuf[c, 1] + g2r[c]

    def g3(c):
        ref = finr.at[rows(mine(c))]
        return remote(ref, ref, g3s_s.at[c], g3r_s.at[c], core_peer)

    def g_finish(c):
        state_wait(x2r.at[c], x2_s.at[c])
        state = x2r[c] - g_total(c)
        x2r[c] = state
        finr[rows(mine(c)), :] = (state * rms_scale(state)).astype(BF)
        g3(c).start()

    def g_credit():
        pl.semaphore_signal(gcred, inc=1, device_id=x_peer, device_id_type=MESH)

    def put(pending, tile, dst, value):
        slot = tile % 3
        height = value.shape[0]
        if pending[slot] is not None:
            pending[slot].wait()
        stage[slot, :height] = value
        cp = local(stage.at[slot, pl.ds(0, height)], dst, st_s.at[slot])
        cp.start()
        pending[slot] = cp

    def flush(pending):
        for cp in pending:
            if cp is not None:
                cp.wait()

    def mlp_grads(blk, ver):
        pending = [None] * 3
        n_t = hid // 256
        for k in range(n_t):
            put(pending, k, gu.at[blk, pl.ds(256 * k, 256)], dot(act[:, 256 * k:256 * (k + 1)], d2b[ver], TN))
        for k in range(n_t):
            put(pending, k, gi.at[blk, pl.ds(256 * k, 256)], dot(a_g[:, 256 * k:256 * (k + 1)], dhb[...], TN))
        flush(pending)

    def attn_grads(blk, fin):
        pending = [None] * 3
        for k in range(3):
            put(pending, k, gq.at[blk, pl.ds(qw * k, qw)], dot(dqkvt[qw * k:qw * (k + 1), :], fin[...], NN))
        put(pending, 3, go.at[blk], dot(ot[...], d1b[...], NN))
        flush(pending)

    def v_start(first, one, pair, c):
        state_start(first, one, pair, rows(mine(c)), vbuf.at[c], v_s.at[c])

    def v_wait(c):
        state_wait(vbuf.at[c], v_s.at[c])

    top = 2 * n_pairs
    w_start(1, top, "iuqo")
    for c in (0, 1):
        local(dy1.at[rows(mine(c))], d1f.at[c], d_s.at[0, c]).start()
        local(dy2.at[rows(mine(c))], d2f.at[c], d_s.at[1, c]).start()
        state_start(True, False, 0, rows(mine(c)), x2r.at[c], x2_s.at[c])
        v_start(True, True, 0, c)
    w_wait(1, "iu")
    g_part(1, True, 0)
    g_chip(0)
    g_send(*range(npc))
    g_chip(1)
    g_send(*range(npc, 2 * npc))
    for i in range(4):
        local(dy2.at[rows(i)], xl.at[i % 2], xl_s.at[i % 2]).start()
        state_wait(xl.at[i % 2], xl_s.at[i % 2])
        d2b[1, rows(i), :] = xl[i % 2].astype(BF)
    for c in (0, 1):
        local(dy1.at[rows(mine(c))], d1f.at[c], d_s.at[0, c]).wait()
        local(dy2.at[rows(mine(c))], d2f.at[c], d_s.at[1, c]).wait()

    @pl.loop(0, n_pairs + 1)
    def _(it):
        pair = n_pairs - it
        is_top = it == 0
        rev = 2 * pair
        plain = 2 * pair + 1

        @pl.when(it > 0)
        def _():
            part_f(0, 0, 0)
            to_x(0, 0)
            g_send(3, 4)
            part_f(0, 0, 1)
            to_x(0, 1)
            g_send(5)
            for c in (0, 1):
                finish(3, c, 1, d2f, x2r[c])
                state_start(False, False, pair, rows(mine(c)), x2r.at[c], x2_s.at[c])
            attn_grads(plain, finp)
            for c in (0, 1):
                e3(1, c).wait()
                part_g(0, 0, 1, c)
                to_x(1, c)
                g_send(6 + c)

            @pl.when(it < n_pairs)
            def _():
                w_start(0, plain - 2, "qoiu")
            mlp_grads(plain, 0)

        mlp_fwd(1, is_top, pair)

        @pl.when(it > 0)
        def _():
            for c in (0, 1):
                v_wait(c)
                finish(0, c, 2, d2f, vbuf[c])
                v_start(False, True, pair, c)
                e3(2, c).wait()
                part_g(1, 1, 2, c)
                to_x(2, c)

        @pl.when(is_top)
        def _():
            for c in (0, 1):
                part_g(1, 1, 2, c)
                to_x(2, c)
            w_wait(1, "qo")

        @pl.when(it < n_pairs)
        def _():
            w_start(1, rev - 2, "iu")

        for c in (0, 1):
            g_finish(c)
        g_credit()
        for c in (0, 1):
            g3(c).wait()

        @pl.when(it > 0)
        def _():
            w_wait(1, "qo")
        attn_fwd_rev()

        @pl.when(it > 0)
        def _():
            for c in (0, 1):
                v_wait(c)
                finish(1, c, None, d1f, vbuf[c])
        mlp_grads(rev, 1)

        @pl.when(it < n_pairs)
        def _():
            w_wait(1, "iu")
            g_part(1, False, pair - 1)

        @pl.when(it == n_pairs)
        def _():
            f_part(1)

        for c in (0, 1):
            @pl.when(is_top)
            def _():
                v_wait(c)
            finish(2, c, 0, d1f, vbuf[c])
            e3(0, c).wait()
            part_f(1, 3, c)
            to_x(3, c)
            g_chip(c)
            if c == 0:
                pl.semaphore_wait(gcred, 1)
                g_send(0)
            else:
                g_send(1, 2)

        @pl.when(it < n_pairs)
        def _():
            for c in (0, 1):
                v_start(False, False, pair - 1, c)
            w_start(1, rev - 2, "qo")

            @pl.when(is_top)
            def _():
                w_start(0, plain - 2, "qoiu")
        attn_grads(rev, finr)

        @pl.when(it < n_pairs)
        def _():
            w_wait(0, "qoiu")
            attn_fwd_plain(pair - 1)
            mlp_fwd(0, False, pair - 1)

    g_send(*range(3, 2 * npc))
    outs = []

    def emit(idx, ref, c, out):
        outs.append(local(ref.at[c], out.at[rows(mine(c))], ol_s.at[idx, c]))
        outs.append(remote(ref.at[c], out.at[rows(mine(c))], os_s.at[idx, c], or_s.at[idx, c], core_peer))
        outs[-2].start()
        outs[-1].start()

    for c in (0, 1):
        finish(3, c, None, d2f, x2r[c])
        emit(3, d2f, c, od2)
        emit(2, d1f, c, od1)
        emit(1, x2r, c, ox2)
    for c in (0, 1):
        v_start(False, True, 0, c)
    for c in (0, 1):
        v_wait(c)
        vbuf[c] = vbuf[c] - g_total(c)
        emit(0, vbuf, c, ox1)
    for cp in outs:
        cp.wait()


def solution(mesh):
    act_spec = P("dp", None, None)
    saved_spec = P(None, "dp", None, None)
    weight_specs = (P(None, None, None, "tp", None), P(None, "tp", None, None), P(None, None, "tp"), P(None, "tp", None))
    grad_specs = (P("dp", None, None, "tp", None), P("dp", "tp", None, None), P("dp", None, "tp"), P("dp", "tp", None))

    def per_device(y_one, y_two, dy_one, dy_two, saved_one, saved_two, w_qkv, w_o, w_in, w_out):
        n_seq, seq, hid = y_one.shape
        n_layers, _, _, heads, hdim = w_qkv.shape
        n_pairs = saved_one.shape[0]
        ff = w_in.shape[-1]
        tok = n_seq * seq
        qkv_w = 3 * heads * hdim
        flat = lambda arr: arr.reshape(arr.shape[:-3] + (tok, hid))
        wq_t = jnp.transpose(w_qkv, (0, 2, 3, 4, 1)).reshape(n_layers, qkv_w, hid)
        wo_t = w_o.reshape(n_layers, heads * hdim, hid)
        sds = jax.ShapeDtypeStruct
        vm = pltpu.VMEM
        dma = pltpu.SemaphoreType.DMA
        half = (2, seq, hid)
        scratch = [
            vm((2, qkv_w, hid), BF), vm((2, heads * hdim, hid), BF), vm((2, hid, ff), BF), vm((2, ff, hid), BF),
            vm((tok, hid), BF), vm((tok, ff), BF), vm((tok, ff), F32), vm((tok, ff), BF),
            vm((tok, hid), BF), vm((tok, hid), BF), vm((qkv_w, tok), BF), vm((qkv_w, tok), BF),
            vm((n_seq * heads, seq, seq), F32), vm((heads * hdim, tok), BF),
            vm((tok, hid), BF), vm((2, tok, hid), BF), vm(half, F32), vm(half, F32),
            vm(half, F32), vm(half, F32), vm(half, F32),
            vm((2,) + half, F32), vm((2,) + half, F32), vm((4,) + half, BF), vm((4,) + half, BF),
            vm((2,) + half, F32), vm(half, F32), vm(half, F32), vm((3, 256, hid), F32),
            dma((2, 2)), dma((2, 2)), dma((4, 2)), dma((4, 2)), dma((3, 2)), dma((3, 2)),
            dma((2,)), dma((2,)), dma((8,)), dma((8,)), dma((2,)), dma((2,)),
            dma((4, 2)), dma((4, 2)), dma((4, 2)), dma((2, 4)), dma((2,)), dma((2,)), dma((2,)), dma((3,)), dma((2, 2)),
            pltpu.SemaphoreType.REGULAR,
        ]
        anyspec = pl.BlockSpec(memory_space=pl.ANY)
        outs = pl.pallas_call(
            functools.partial(chain_kernel, seq, hid, heads, hdim, n_pairs),
            out_shape=[sds((tok, hid), F32)] * 4
            + [sds((n_layers, qkv_w, hid), F32), sds((n_layers, heads * hdim, hid), F32), sds((n_layers, hid, ff), F32), sds((n_layers, ff, hid), F32)],
            in_specs=[anyspec] * 10,
            out_specs=[anyspec] * 8,
            scratch_shapes=scratch,
            name="chain",
            compiler_params=pltpu.CompilerParams(collective_id=0, has_side_effects=True, vmem_limit_bytes=67043328),
        )(flat(y_one), flat(y_two), flat(dy_one), flat(dy_two), flat(saved_one), flat(saved_two), wq_t, wo_t, w_in, w_out)
        states = tuple(out.reshape(n_seq, seq, hid) for out in outs[:4])
        d_qkv = jnp.transpose(outs[4].reshape(n_layers, 3, heads, hdim, hid), (0, 4, 1, 2, 3))
        d_o = outs[5].reshape(n_layers, heads, hdim, hid)
        return states + (d_qkv, d_o, outs[6], outs[7])

    return jax.shard_map(
        per_device,
        mesh=mesh,
        in_specs=(act_spec,) * 4 + (saved_spec,) * 2 + weight_specs,
        out_specs=(act_spec,) * 4 + grad_specs,
        check_vma=False,
    )
```

time: 1440 us -> 621 us (0.43)
  waiting for transfers between devices: 710 us -> 0 us
  Pallas kernels: 0 us -> 569 us
  matrix products: 507 us -> 0 us
  other arithmetic: 145 us -> 0.01 us
  between operations: 16.7 us -> 0.75 us
    psum x14 -> x0, waiting for transfers between devices: 709 us -> none  [the longest x4 225 us: plain_block(): lax.psum(g_back.astype(jnp.bfloat16), 'tp').astype(jnp.float32)]
    pallas_call x0 -> x1, Pallas kernels: none -> 569 us  [per_device(): pl.pallas_call(functools.partial(chain_kernel, seq, hid, heads, hdim, n_p...]
    dot_general x142 -> x0, matrix products: 507 us -> none  [the longest x9 57.7 us: attn_backward(): jnp.einsum('bnqk,bkne->bqne', ds_bf, qkv_all[1], preferred_element_type=j...]
    reduce_sum x21 -> x0, other arithmetic: 69.6 us -> none  [the longest x9 37 us: rms_norm(): jnp.mean(state * state, axis=-1, keepdims=True) + EPS]
    convert_element_type x12 -> x0, other arithmetic: 28.8 us -> none  [the longest x4 14.6 us: attn_backward(): d_bf = d_out.astype(jnp.bfloat16)]
    sub x9 -> x0, other arithmetic: 24.5 us -> none  [attn_forward(): attn_probs = jax.nn.softmax(scores, axis=-1)]
    add x6 -> x0, other arithmetic: 21.6 us -> none  [the longest x4 12.4 us: plain_block(): d_two + f_norm_pull(lax.psum(f_back.astype(jnp.bfloat16), 'tp').astype(jn...]
    unnamed x494 -> x36, local copies, waits for them, and re-layouts: 52.9 us -> 50.8 us
  transfers between devices with their start and end apart: 14 -> 0, of which waited for: 13 -> 0; matrix products, arithmetic and copies ran while one was open for 17% -> 0% of each run, Pallas kernels for 0% -> 0%
where the time goes in v2:
time: 621 us; the launch traced here: 620 us
  Pallas kernels  569 us (92%)
  local copies, waits for them, and re-layouts  50.8 us (8%)
    pallas_call x1, Pallas kernels, per_device(): pl.pallas_call(functools.partial(chain_kernel, seq, hid, heads, hdim, n_p...  569 us
    unnamed x36, local copies, waits for them, and re-layouts  50.8 us

profile of v2, /device:TPU:0, one launch (start us, length us, event | category | flops | bytes accessed | tf_op | source)
XLA Modules:
  0.0 620.2 jit_solution(12533034623339212810)
XLA Ops:
  0.6 568.7 %chain.1 = (f32[1024,768]{1,0:T(8,128)}, f32[1024,768]{1,0:T(8,128)}, f32[1024,768]{1,0:T(8,128)}, f32[1024,768]{1,0:T(8,128)}, f32[9,576,768]{2,1,0:T(8,128)}, ...) custom-call(f32[1024,768]{1,0:T(8,128)} %bitcast.27, f32[1024,768]{1,0:T(8,128)} %bitcast.28, ...), custom_call_target="tpu_custom_call" | custom-call | tf_op jit(solution)/shard_map/chain/pallas_call | solution.py:517
  569.3 0.0 copy-start.1
  569.3 0.0 copy-start
  569.3 0.0 slice-start.6
  569.3 4.0 copy.26
  573.4 0.0 slice-start.7
  573.4 4.7 copy.27
  578.0 0.0 copy-done.1
  578.0 1.7 copy.28
  579.7 0.0 slice-start.8
  579.7 4.7 copy.29
  584.4 0.0 copy-done
  584.5 8.1 %copy.30 = f32[9,768,3,3,64]{1,4,3,2,0:T(8,128)} copy(f32[9,768,3,3,64]{1,4,3,2,0:T(8,128)S(1)} %bitcast.22) | data formatting | bytes 31850496
  592.5 6.5 %copy.31 = f32[9,3,64,768]{3,2,1,0:T(8,128)} copy(f32[9,3,64,768]{3,2,1,0:T(8,128)} %bitcast.26) | data formatting | bytes 10616832
  599.0 0.0 slice-done.6
  599.0 0.0 slice-done.7
  599.0 0.0 slice-done.8
  599.0 0.0 slice-done.9
  599.0 0.0 slice-done.10
  599.0 0.0 slice-done.11
  599.1 0.0 slice-start.2
  599.1 0.0 slice-start.3
  599.1 0.0 slice-start.4
  599.1 0.0 slice-start.5
  599.1 10.8 %copy.32 = f32[9,768,768]{2,1,0:T(8,128)} copy(f32[9,768,768]{2,1,0:T(8,128)S(1)} %bitcast.21) | data formatting | bytes 42467328
  609.8 0.0 slice-done
  609.8 0.0 slice-done.1
  609.9 0.0 slice-done.2
  609.9 0.0 slice-done.3
  609.9 1.5 slice-done.4
  611.4 1.2 slice-done.5
  612.6 7.6 %copy.33 = f32[9,768,768]{2,1,0:T(8,128)} copy(f32[9,768,768]{2,1,0:T(8,128)S(1)} %bitcast.19) | data formatting | bytes 42467328
  (7 shorter events, 0.0 us)
Async XLA Ops:
  569.3 8.7 %copy-start.1 = (f32[1024,768]{1,0:T(8,128)S(1)}, f32[1024,768]{1,0:T(8,128)}, u32[]{:S(2)}) copy-start(f32[1024,768]{1,0:T(8,128)} %get-tuple-element.18) | copy-start | bytes 9437188
  569.3 15.1 %copy-start = (f32[9,576,768]{2,1,0:T(8,128)S(1)}, f32[9,576,768]{2,1,0:T(8,128)}, u32[]{:S(2)}) copy-start(f32[9,576,768]{2,1,0:T(8,128)} %get-tuple-element.20) | copy-start | bytes 47775748
  569.3 29.7 %slice-start.6 = ((s8[21233664]{0:T(1024)(128)(4,1)}), s8[4194304]{0:T(1024)(128)(4,1)S(1)}, s32[]{:S(2)}) async-start(s8[21233664]{0:T(1024)(128)(4,1)} %bitcast.20), calls=%async_computation.6 | async-start | bytes 8388608
  573.4 25.6 %slice-start.7 = ((s8[21233664]{0:T(1024)(128)(4,1)}), s8[4194304]{0:T(1024)(128)(4,1)S(1)}, s32[]{:S(2)}) async-start(s8[21233664]{0:T(1024)(128)(4,1)} %bitcast.20), calls=%async_computation.7 | async-start | bytes 8388608
  579.7 19.3 %slice-start.8 = ((s8[21233664]{0:T(1024)(128)(4,1)}), s8[4194304]{0:T(1024)(128)(4,1)S(1)}, s32[]{:S(2)}) async-start(s8[21233664]{0:T(1024)(128)(4,1)} %bitcast.20), calls=%async_computation.8 | async-start | bytes 8388608
  584.5 14.6 %slice-start.9 = ((s8[21233664]{0:T(1024)(128)(4,1)}), s8[4194304]{0:T(1024)(128)(4,1)S(1)}, s32[]{:S(2)}) async-start(s8[21233664]{0:T(1024)(128)(4,1)} %bitcast.20), calls=%async_computation.9 | async-start | bytes 8388608
  584.5 14.6 %slice-start.10 = ((s8[21233664]{0:T(1024)(128)(4,1)}), s8[4194304]{0:T(1024)(128)(4,1)S(1)}, s32[]{:S(2)}) async-start(s8[21233664]{0:T(1024)(128)(4,1)} %bitcast.20), calls=%async_computation.10 | async-start | bytes 8388608
  584.5 14.6 %slice-start.11 = ((s8[21233664]{0:T(1024)(128)(4,1)}), s8[262144]{0:T(1024)(128)(4,1)S(1)}, s32[]{:S(2)}) async-start(s8[21233664]{0:T(1024)(128)(4,1)} %bitcast.20), calls=%async_computation.11 | async-start | bytes 524288
  592.5 17.3 %slice-start = ((s8[21233664]{0:T(1024)(128)(4,1)}), s8[262144]{0:T(1024)(128)(4,1)S(1)}, s32[]{:S(2)}) async-start(s8[21233664]{0:T(1024)(128)(4,1)} %bitcast.18), calls=%async_computation | async-start | bytes 524288
  592.5 17.3 %slice-start.1 = ((s8[21233664]{0:T(1024)(128)(4,1)}), s8[4194304]{0:T(1024)(128)(4,1)S(1)}, s32[]{:S(2)}) async-start(s8[21233664]{0:T(1024)(128)(4,1)} %bitcast.18), calls=%async_computation.1 | async-start | bytes 8388608
  599.1 10.8 %slice-start.2 = ((s8[21233664]{0:T(1024)(128)(4,1)}), s8[4194304]{0:T(1024)(128)(4,1)S(1)}, s32[]{:S(2)}) async-start(s8[21233664]{0:T(1024)(128)(4,1)} %bitcast.18), calls=%async_computation.2 | async-start | bytes 8388608
  599.1 10.8 %slice-start.3 = ((s8[21233664]{0:T(1024)(128)(4,1)}), s8[4194304]{0:T(1024)(128)(4,1)S(1)}, s32[]{:S(2)}) async-start(s8[21233664]{0:T(1024)(128)(4,1)} %bitcast.18), calls=%async_computation.3 | async-start | bytes 8388608
  599.1 12.3 %slice-start.4 = ((s8[21233664]{0:T(1024)(128)(4,1)}), s8[4194304]{0:T(1024)(128)(4,1)S(1)}, s32[]{:S(2)}) async-start(s8[21233664]{0:T(1024)(128)(4,1)} %bitcast.18), calls=%async_computation.4 | async-start | bytes 8388608
  599.1 13.5 %slice-start.5 = ((s8[21233664]{0:T(1024)(128)(4,1)}), s8[4194304]{0:T(1024)(128)(4,1)S(1)}, s32[]{:S(2)}) async-start(s8[21233664]{0:T(1024)(128)(4,1)} %bitcast.18), calls=%async_computation.5 | async-start | bytes 8388608

commit v3 on v2

--- a/solution.py
+++ b/solution.py
@@ -166,20 +166,21 @@
     def e2(t, c):
         return remote(xs.at[t, c], xr.at[t, c], e2s_s.at[t, c], e2r_s.at[t, c], x_peer)
 
-    def part_g(slot, ver, t, c):
+    def part_g(slot, ver, c, mode, e1_slot=None):
         @pl.loop(0, 2)
         def _(i):
             s = 2 * c + jnp.where(i == 0, 1 - ci, ci)
             d_act = dot(d2b[ver, rows(s), :], wu[slot], NT)
             dh = (d_act * gp[rows(s), :]).astype(BF)
             dhb[rows(s), :] = dh
-            pbuf[c, i] = dot(dh, wi[slot], NT)
-
-            @pl.when(i == 0)
-            def _():
-                e1(t % 2, c).start()
-
-    def part_f(slot, t, c):
+            part = dot(dh, wi[slot], NT)
+            pbuf[c, i] = pbuf[c, i] + part if mode == "add" else part
+            if mode != "hold":
+                @pl.when(i == 0)
+                def _():
+                    e1(e1_slot, c).start()
+
+    def part_f(slot, c, e1_slot):
         @pl.loop(0, 2)
         def _(i):
             s = 2 * c + jnp.where(i == 0, 1 - ci, ci)
@@ -202,11 +203,11 @@
 
             @pl.when(i == 0)
             def _():
-                e1(t % 2, c).start()
-
-    def to_x(t, c):
-        e1(t % 2, c).wait()
-        xs[t, c] = (pbuf[c, 1] + e1r[t % 2, c]).astype(BF)
+                e1(e1_slot, c).start()
+
+    def to_x(t, c, e1_slot):
+        e1(e1_slot, c).wait()
+        xs[t, c] = (pbuf[c, 1] + e1r[e1_slot, c]).astype(BF)
         e2(t, c).start()
 
     def summed(t, c):
@@ -349,24 +350,23 @@
         is_top = it == 0
         rev = 2 * pair
         plain = 2 * pair + 1
+        even, odd = lax.rem(it, 2), lax.rem(it + 1, 2)
 
         @pl.when(it > 0)
         def _():
-            part_f(0, 0, 0)
-            to_x(0, 0)
+            part_f(0, 0, even)
+            to_x(0, 0, even)
             g_send(3, 4)
-            part_f(0, 0, 1)
-            to_x(0, 1)
-            g_send(5)
+            part_f(0, 1, even)
+            to_x(0, 1, even)
+            g_send(5, 6, 7)
             for c in (0, 1):
-                finish(3, c, 1, d2f, x2r[c])
+                finish(2, c, 1, d2f, x2r[c])
                 state_start(False, False, pair, rows(mine(c)), x2r.at[c], x2_s.at[c])
             attn_grads(plain, finp)
             for c in (0, 1):
                 e3(1, c).wait()
-                part_g(0, 0, 1, c)
-                to_x(1, c)
-                g_send(6 + c)
+                part_g(0, 0, c, "hold")
 
             @pl.when(it < n_pairs)
             def _():
@@ -382,14 +382,14 @@
                 finish(0, c, 2, d2f, vbuf[c])
                 v_start(False, True, pair, c)
                 e3(2, c).wait()
-                part_g(1, 1, 2, c)
-                to_x(2, c)
+                part_g(1, 1, c, "add", odd)
+                to_x(1, c, odd)
 
         @pl.when(is_top)
         def _():
             for c in (0, 1):
-                part_g(1, 1, 2, c)
-                to_x(2, c)
+                part_g(1, 1, c, "first", odd)
+                to_x(1, c, odd)
             w_wait(1, "qo")
 
         @pl.when(it < n_pairs)
@@ -407,11 +407,6 @@
             w_wait(1, "qo")
         attn_fwd_rev()
 
-        @pl.when(it > 0)
-        def _():
-            for c in (0, 1):
-                v_wait(c)
-                finish(1, c, None, d1f, vbuf[c])
         mlp_grads(rev, 1)
 
         @pl.when(it < n_pairs)
@@ -424,13 +419,11 @@
             f_part(1)
 
         for c in (0, 1):
-            @pl.when(is_top)
-            def _():
-                v_wait(c)
-            finish(2, c, 0, d1f, vbuf[c])
+            v_wait(c)
+            finish(1, c, 0, d1f, vbuf[c])
             e3(0, c).wait()
-            part_f(1, 3, c)
-            to_x(3, c)
+            part_f(1, c, even)
+            to_x(2, c, even)
             g_chip(c)
             if c == 0:
                 pl.semaphore_wait(gcred, 1)
@@ -465,7 +458,7 @@
         outs[-1].start()
 
     for c in (0, 1):
-        finish(3, c, None, d2f, x2r[c])
+        finish(2, c, None, d2f, x2r[c])
         emit(3, d2f, c, od2)
         emit(2, d1f, c, od1)
         emit(1, x2r, c, ox2)
@@ -506,9 +499,9 @@
             vm((n_seq * heads, seq, seq), F32), vm((heads * hdim, tok), BF),
             vm((tok, hid), BF), vm((2, tok, hid), BF), vm(half, F32), vm(half, F32),
             vm(half, F32), vm(half, F32), vm(half, F32),
-            vm((2,) + half, F32), vm((2,) + half, F32), vm((4,) + half, BF), vm((4,) + half, BF),
+            vm((2,) + half, F32), vm((2,) + half, F32), vm((3,) + half, BF), vm((3,) + half, BF),
             vm((2,) + half, F32), vm(half, F32), vm(half, F32), vm((3, 256, hid), F32),
-            dma((2, 2)), dma((2, 2)), dma((4, 2)), dma((4, 2)), dma((3, 2)), dma((3, 2)),
+            dma((2, 2)), dma((2, 2)), dma((3, 2)), dma((3, 2)), dma((3, 2)), dma((3, 2)),
             dma((2,)), dma((2,)), dma((8,)), dma((8,)), dma((2,)), dma((2,)),
             dma((4, 2)), dma((4, 2)), dma((4, 2)), dma((2, 4)), dma((2,)), dma((2,)), dma((2,)), dma((3,)), dma((2, 2)),
             pltpu.SemaphoreType.REGULAR,

time: 621 us -> 550 us (0.89)
  Pallas kernels: 569 us -> 498 us
    pallas_call x1, Pallas kernels: 569 us -> 498 us  [per_device(): pl.pallas_call(functools.partial(chain_kernel, seq, hid, heads, hdim, n_p...]
where the time goes in v3:
time: 550 us; the launch traced here: 549 us
  Pallas kernels  498 us (91%)
  local copies, waits for them, and re-layouts  50.8 us (9%)
    pallas_call x1, Pallas kernels, per_device(): pl.pallas_call(functools.partial(chain_kernel, seq, hid, heads, hdim, n_p...  498 us
    unnamed x36, local copies, waits for them, and re-layouts  50.8 us

profile of v3, /device:TPU:0, one launch (start us, length us, event | category | flops | bytes accessed | tf_op | source)
XLA Modules:
  0.0 549.1 jit_solution(2804586153654690181)
XLA Ops:
  0.6 497.6 %chain.1 = (f32[1024,768]{1,0:T(8,128)}, f32[1024,768]{1,0:T(8,128)}, f32[1024,768]{1,0:T(8,128)}, f32[1024,768]{1,0:T(8,128)}, f32[9,576,768]{2,1,0:T(8,128)}, ...) custom-call(f32[1024,768]{1,0:T(8,128)} %bitcast.27, f32[1024,768]{1,0:T(8,128)} %bitcast.28, ...), custom_call_target="tpu_custom_call" | custom-call | tf_op jit(solution)/shard_map/chain/pallas_call | solution.py:510
  498.2 0.0 copy-start.1
  498.2 0.0 copy-start
  498.2 0.0 slice-start.6
  498.3 4.0 copy.26
  502.3 0.0 slice-start.7
  502.3 4.7 copy.27
  506.9 0.0 copy-done.1
  506.9 1.7 copy.28
  508.6 0.0 slice-start.8
  508.6 4.7 copy.29
  513.4 0.0 copy-done
  513.4 8.1 %copy.30 = f32[9,768,3,3,64]{1,4,3,2,0:T(8,128)} copy(f32[9,768,3,3,64]{1,4,3,2,0:T(8,128)S(1)} %bitcast.22) | data formatting | bytes 31850496
  521.4 6.5 %copy.31 = f32[9,3,64,768]{3,2,1,0:T(8,128)} copy(f32[9,3,64,768]{3,2,1,0:T(8,128)} %bitcast.26) | data formatting | bytes 10616832
  527.9 0.0 slice-done.6
  527.9 0.0 slice-done.7
  527.9 0.0 slice-done.8
  527.9 0.0 slice-done.9
  527.9 0.0 slice-done.10
  527.9 0.0 slice-done.11
  528.0 0.0 slice-start.2
  528.0 0.0 slice-start.3
  528.0 0.0 slice-start.4
  528.0 0.0 slice-start.5
  528.0 10.8 %copy.32 = f32[9,768,768]{2,1,0:T(8,128)} copy(f32[9,768,768]{2,1,0:T(8,128)S(1)} %bitcast.21) | data formatting | bytes 42467328
  538.8 0.0 slice-done
  538.8 0.0 slice-done.1
  538.8 0.0 slice-done.2
  538.8 0.0 slice-done.3
  538.8 1.5 slice-done.4
  540.3 1.2 slice-done.5
  541.5 7.6 %copy.33 = f32[9,768,768]{2,1,0:T(8,128)} copy(f32[9,768,768]{2,1,0:T(8,128)S(1)} %bitcast.19) | data formatting | bytes 42467328
  (7 shorter events, 0.0 us)
Async XLA Ops:
  498.2 8.7 %copy-start.1 = (f32[1024,768]{1,0:T(8,128)S(1)}, f32[1024,768]{1,0:T(8,128)}, u32[]{:S(2)}) copy-start(f32[1024,768]{1,0:T(8,128)} %get-tuple-element.18) | copy-start | bytes 9437188
  498.2 15.1 %copy-start = (f32[9,576,768]{2,1,0:T(8,128)S(1)}, f32[9,576,768]{2,1,0:T(8,128)}, u32[]{:S(2)}) copy-start(f32[9,576,768]{2,1,0:T(8,128)} %get-tuple-element.20) | copy-start | bytes 47775748
  498.2 29.7 %slice-start.6 = ((s8[21233664]{0:T(1024)(128)(4,1)}), s8[4194304]{0:T(1024)(128)(4,1)S(1)}, s32[]{:S(2)}) async-start(s8[21233664]{0:T(1024)(128)(4,1)} %bitcast.20), calls=%async_computation.6 | async-start | bytes 8388608
  502.3 25.6 %slice-start.7 = ((s8[21233664]{0:T(1024)(128)(4,1)}), s8[4194304]{0:T(1024)(128)(4,1)S(1)}, s32[]{:S(2)}) async-start(s8[21233664]{0:T(1024)(128)(4,1)} %bitcast.20), calls=%async_computation.7 | async-start | bytes 8388608
  508.6 19.3 %slice-start.8 = ((s8[21233664]{0:T(1024)(128)(4,1)}), s8[4194304]{0:T(1024)(128)(4,1)S(1)}, s32[]{:S(2)}) async-start(s8[21233664]{0:T(1024)(128)(4,1)} %bitcast.20), calls=%async_computation.8 | async-start | bytes 8388608
  513.4 14.6 %slice-start.9 = ((s8[21233664]{0:T(1024)(128)(4,1)}), s8[4194304]{0:T(1024)(128)(4,1)S(1)}, s32[]{:S(2)}) async-start(s8[21233664]{0:T(1024)(128)(4,1)} %bitcast.20), calls=%async_computation.9 | async-start | bytes 8388608
  513.4 14.6 %slice-start.10 = ((s8[21233664]{0:T(1024)(128)(4,1)}), s8[4194304]{0:T(1024)(128)(4,1)S(1)}, s32[]{:S(2)}) async-start(s8[21233664]{0:T(1024)(128)(4,1)} %bitcast.20), calls=%async_computation.10 | async-start | bytes 8388608
  513.4 14.6 %slice-start.11 = ((s8[21233664]{0:T(1024)(128)(4,1)}), s8[262144]{0:T(1024)(128)(4,1)S(1)}, s32[]{:S(2)}) async-start(s8[21233664]{0:T(1024)(128)(4,1)} %bitcast.20), calls=%async_computation.11 | async-start | bytes 524288
  521.4 17.3 %slice-start = ((s8[21233664]{0:T(1024)(128)(4,1)}), s8[262144]{0:T(1024)(128)(4,1)S(1)}, s32[]{:S(2)}) async-start(s8[21233664]{0:T(1024)(128)(4,1)} %bitcast.18), calls=%async_computation | async-start | bytes 524288
  521.4 17.3 %slice-start.1 = ((s8[21233664]{0:T(1024)(128)(4,1)}), s8[4194304]{0:T(1024)(128)(4,1)S(1)}, s32[]{:S(2)}) async-start(s8[21233664]{0:T(1024)(128)(4,1)} %bitcast.18), calls=%async_computation.1 | async-start | bytes 8388608
  528.0 10.8 %slice-start.2 = ((s8[21233664]{0:T(1024)(128)(4,1)}), s8[4194304]{0:T(1024)(128)(4,1)S(1)}, s32[]{:S(2)}) async-start(s8[21233664]{0:T(1024)(128)(4,1)} %bitcast.18), calls=%async_computation.2 | async-start | bytes 8388608
  528.0 10.8 %slice-start.3 = ((s8[21233664]{0:T(1024)(128)(4,1)}), s8[4194304]{0:T(1024)(128)(4,1)S(1)}, s32[]{:S(2)}) async-start(s8[21233664]{0:T(1024)(128)(4,1)} %bitcast.18), calls=%async_computation.3 | async-start | bytes 8388608
  528.0 12.3 %slice-start.4 = ((s8[21233664]{0:T(1024)(128)(4,1)}), s8[4194304]{0:T(1024)(128)(4,1)S(1)}, s32[]{:S(2)}) async-start(s8[21233664]{0:T(1024)(128)(4,1)} %bitcast.18), calls=%async_computation.4 | async-start | bytes 8388608
  528.0 13.5 %slice-start.5 = ((s8[21233664]{0:T(1024)(128)(4,1)}), s8[4194304]{0:T(1024)(128)(4,1)S(1)}, s32[]{:S(2)}) async-start(s8[21233664]{0:T(1024)(128)(4,1)} %bitcast.18), calls=%async_computation.5 | async-start | bytes 8388608

commit v4 on v3

--- a/solution.py
+++ b/solution.py
@@ -126,14 +126,12 @@
             def _():
                 state_start(first, one, pair, rows(order(i + 2)), xl.at[slot], xl_s.at[slot])
 
-    def mlp_fwd(slot, first, pair):
-        def body(i, s, state):
-            normed = (state * rms_scale(state)).astype(BF)
-            a_g[rows(s), :] = normed
-            value, grad = gelu_parts(dot(normed, wi[slot], NN), True)
+    def mlp_fwd(slot):
+        @pl.loop(0, 4)
+        def _(s):
+            value, grad = gelu_parts(dot(a_g[rows(s), :], wi[slot], NN), True)
             act[rows(s), :] = value.astype(BF)
             gp[rows(s), :] = grad
-        each_seq(first, True, pair, body)
 
     def attn_fwd_seq(slot, fin, s):
         cols = rows(s)
@@ -245,11 +243,16 @@
             def _():
                 g1(c).start()
 
-    def g_part(slot, first, pair):
+    def g_part(slot, first, pair, keep):
         def body(i, s, state):
             normed = (state * rms_scale(state)).astype(BF)
-            value, _ = gelu_parts(dot(normed, wi[slot], NN), False)
-            gbuf[i // 2, lax.rem(i, 2)] = dot(value.astype(BF), wu[slot], NN)
+            a_g[rows(s), :] = normed
+            value, grad = gelu_parts(dot(normed, wi[slot], NN), keep)
+            value = value.astype(BF)
+            if keep:
+                act[rows(s), :] = value
+                gp[rows(s), :] = grad
+            gbuf[i // 2, lax.rem(i, 2)] = dot(value, wu[slot], NN)
             g_send_core(i)
         each_seq(first, True, pair, body, g_order)
 
@@ -326,16 +329,16 @@
     top = 2 * n_pairs
     w_start(1, top, "iuqo")
     for c in (0, 1):
+        v_start(True, True, 0, c)
+        state_start(True, False, 0, rows(mine(c)), x2r.at[c], x2_s.at[c])
         local(dy1.at[rows(mine(c))], d1f.at[c], d_s.at[0, c]).start()
         local(dy2.at[rows(mine(c))], d2f.at[c], d_s.at[1, c]).start()
-        state_start(True, False, 0, rows(mine(c)), x2r.at[c], x2_s.at[c])
-        v_start(True, True, 0, c)
     w_wait(1, "iu")
-    g_part(1, True, 0)
-    g_chip(0)
-    g_send(*range(npc))
-    g_chip(1)
-    g_send(*range(npc, 2 * npc))
+    g_part(1, True, 0, True)
+    for c in (0, 1):
+        g_chip(c)
+        g_send(*range(npc * c, npc * (c + 1)))
+    w_start(0, top - 1, "qoiu")
     for i in range(4):
         local(dy2.at[rows(i)], xl.at[i % 2], xl_s.at[i % 2]).start()
         state_wait(xl.at[i % 2], xl_s.at[i % 2])
@@ -348,32 +351,15 @@
     def _(it):
         pair = n_pairs - it
         is_top = it == 0
+        more = it < n_pairs
         rev = 2 * pair
-        plain = 2 * pair + 1
         even, odd = lax.rem(it, 2), lax.rem(it + 1, 2)
 
-        @pl.when(it > 0)
-        def _():
-            part_f(0, 0, even)
-            to_x(0, 0, even)
-            g_send(3, 4)
-            part_f(0, 1, even)
-            to_x(0, 1, even)
-            g_send(5, 6, 7)
+        @pl.when(is_top)
+        def _():
             for c in (0, 1):
-                finish(2, c, 1, d2f, x2r[c])
-                state_start(False, False, pair, rows(mine(c)), x2r.at[c], x2_s.at[c])
-            attn_grads(plain, finp)
-            for c in (0, 1):
-                e3(1, c).wait()
-                part_g(0, 0, c, "hold")
-
-            @pl.when(it < n_pairs)
-            def _():
-                w_start(0, plain - 2, "qoiu")
-            mlp_grads(plain, 0)
-
-        mlp_fwd(1, is_top, pair)
+                part_g(1, 1, c, "first", odd)
+                to_x(1, c, odd)
 
         @pl.when(it > 0)
         def _():
@@ -385,38 +371,17 @@
                 part_g(1, 1, c, "add", odd)
                 to_x(1, c, odd)
 
-        @pl.when(is_top)
-        def _():
-            for c in (0, 1):
-                part_g(1, 1, c, "first", odd)
-                to_x(1, c, odd)
-            w_wait(1, "qo")
-
-        @pl.when(it < n_pairs)
+        @pl.when(more)
         def _():
             w_start(1, rev - 2, "iu")
 
         for c in (0, 1):
             g_finish(c)
         g_credit()
+        w_wait(1, "qo")
         for c in (0, 1):
             g3(c).wait()
-
-        @pl.when(it > 0)
-        def _():
-            w_wait(1, "qo")
         attn_fwd_rev()
-
-        mlp_grads(rev, 1)
-
-        @pl.when(it < n_pairs)
-        def _():
-            w_wait(1, "iu")
-            g_part(1, False, pair - 1)
-
-        @pl.when(it == n_pairs)
-        def _():
-            f_part(1)
 
         for c in (0, 1):
             v_wait(c)
@@ -424,31 +389,52 @@
             e3(0, c).wait()
             part_f(1, c, even)
             to_x(2, c, even)
-            g_chip(c)
-            if c == 0:
-                pl.semaphore_wait(gcred, 1)
-                g_send(0)
-            else:
-                g_send(1, 2)
-
-        @pl.when(it < n_pairs)
-        def _():
+        attn_grads(rev, finr)
+
+        @pl.when(more)
+        def _():
+            w_start(1, rev - 2, "qo")
             for c in (0, 1):
                 v_start(False, False, pair - 1, c)
-            w_start(1, rev - 2, "qo")
-
-            @pl.when(is_top)
+            w_wait(0, "qo")
+            attn_fwd_plain(pair - 1)
+            for c in (0, 1):
+                part_f(0, c, odd)
+                to_x(0, c, odd)
+        mlp_grads(rev, 1)
+
+        @pl.when(more)
+        def _():
+            w_wait(1, "iu")
+            g_part(1, False, pair - 1, False)
+
+        @pl.when(jnp.logical_not(more))
+        def _():
+            f_part(1)
+
+        pl.semaphore_wait(gcred, 1)
+        for c in (0, 1):
+            g_chip(c)
+            g_send(*range(npc * c, npc * (c + 1)))
+
+        @pl.when(more)
+        def _():
+            w_wait(0, "iu")
+            mlp_fwd(0)
+            for c in (0, 1):
+                finish(2, c, 1, d2f, x2r[c])
+                state_start(False, False, pair - 1, rows(mine(c)), x2r.at[c], x2_s.at[c])
+            for c in (0, 1):
+                e3(1, c).wait()
+                part_g(0, 0, c, "hold")
+
+            @pl.when(it < n_pairs - 1)
             def _():
-                w_start(0, plain - 2, "qoiu")
-        attn_grads(rev, finr)
-
-        @pl.when(it < n_pairs)
-        def _():
-            w_wait(0, "qoiu")
-            attn_fwd_plain(pair - 1)
-            mlp_fwd(0, False, pair - 1)
-
-    g_send(*range(3, 2 * npc))
+                w_start(0, rev - 3, "qoiu")
+            mlp_grads(rev - 1, 0)
+            attn_grads(rev - 1, finp)
+            mlp_fwd(1)
+
     outs = []
 
     def emit(idx, ref, c, out):

time: 550 us -> 534 us (0.971)
  Pallas kernels: 498 us -> 482 us
    pallas_call x1, Pallas kernels: 498 us -> 482 us  [per_device(): pl.pallas_call(functools.partial(chain_kernel, seq, hid, heads, hdim, n_p...]
where the time goes in v4:
time: 534 us
  Pallas kernels  482 us (90%)
  local copies, waits for them, and re-layouts  50.8 us (10%)
    pallas_call x1, Pallas kernels, per_device(): pl.pallas_call(functools.partial(chain_kernel, seq, hid, heads, hdim, n_p...  482 us
    unnamed x36, local copies, waits for them, and re-layouts  50.8 us

profile of v4, /device:TPU:0, one launch (start us, length us, event | category | flops | bytes accessed | tf_op | source)
XLA Modules:
  0.0 533.8 jit_solution(12927636476615512648)
XLA Ops:
  0.6 482.2 %chain.1 = (f32[1024,768]{1,0:T(8,128)}, f32[1024,768]{1,0:T(8,128)}, f32[1024,768]{1,0:T(8,128)}, f32[1024,768]{1,0:T(8,128)}, f32[9,576,768]{2,1,0:T(8,128)}, ...) custom-call(f32[1024,768]{1,0:T(8,128)} %bitcast.27, f32[1024,768]{1,0:T(8,128)} %bitcast.28, ...), custom_call_target="tpu_custom_call" | custom-call | tf_op jit(solution)/shard_map/chain/pallas_call | solution.py:496
  482.9 0.0 copy-start.1
  482.9 0.0 copy-start
  482.9 0.0 slice-start.6
  482.9 4.0 copy.26
  486.9 0.0 slice-start.7
  486.9 4.7 copy.27
  491.6 0.0 copy-done.1
  491.6 1.7 copy.28
  493.3 0.0 slice-start.8
  493.3 4.7 copy.29
  498.0 0.0 copy-done
  498.0 8.1 %copy.30 = f32[9,768,3,3,64]{1,4,3,2,0:T(8,128)} copy(f32[9,768,3,3,64]{1,4,3,2,0:T(8,128)S(1)} %bitcast.22) | data formatting | bytes 31850496
  506.1 6.5 %copy.31 = f32[9,3,64,768]{3,2,1,0:T(8,128)} copy(f32[9,3,64,768]{3,2,1,0:T(8,128)} %bitcast.26) | data formatting | bytes 10616832
  512.6 0.0 slice-done.6
  512.6 0.0 slice-done.7
  512.6 0.0 slice-done.8
  512.6 0.0 slice-done.9
  512.6 0.0 slice-done.10
  512.6 0.0 slice-done.11
  512.6 0.0 slice-start.2
  512.6 0.0 slice-start.3
  512.6 0.0 slice-start.4
  512.7 0.0 slice-start.5
  512.7 10.8 %copy.32 = f32[9,768,768]{2,1,0:T(8,128)} copy(f32[9,768,768]{2,1,0:T(8,128)S(1)} %bitcast.21) | data formatting | bytes 42467328
  523.4 0.0 slice-done
  523.4 0.0 slice-done.1
  523.4 0.0 slice-done.2
  523.4 0.0 slice-done.3
  523.4 1.5 slice-done.4
  525.0 1.2 slice-done.5
  526.2 7.6 %copy.33 = f32[9,768,768]{2,1,0:T(8,128)} copy(f32[9,768,768]{2,1,0:T(8,128)S(1)} %bitcast.19) | data formatting | bytes 42467328
  (7 shorter events, 0.0 us)
Async XLA Ops:
  482.9 8.7 %copy-start.1 = (f32[1024,768]{1,0:T(8,128)S(1)}, f32[1024,768]{1,0:T(8,128)}, u32[]{:S(2)}) copy-start(f32[1024,768]{1,0:T(8,128)} %get-tuple-element.18) | copy-start | bytes 9437188
  482.9 15.1 %copy-start = (f32[9,576,768]{2,1,0:T(8,128)S(1)}, f32[9,576,768]{2,1,0:T(8,128)}, u32[]{:S(2)}) copy-start(f32[9,576,768]{2,1,0:T(8,128)} %get-tuple-element.20) | copy-start | bytes 47775748
  482.9 29.7 %slice-start.6 = ((s8[21233664]{0:T(1024)(128)(4,1)}), s8[4194304]{0:T(1024)(128)(4,1)S(1)}, s32[]{:S(2)}) async-start(s8[21233664]{0:T(1024)(128)(4,1)} %bitcast.20), calls=%async_computation.6 | async-start | bytes 8388608
  486.9 25.6 %slice-start.7 = ((s8[21233664]{0:T(1024)(128)(4,1)}), s8[4194304]{0:T(1024)(128)(4,1)S(1)}, s32[]{:S(2)}) async-start(s8[21233664]{0:T(1024)(128)(4,1)} %bitcast.20), calls=%async_computation.7 | async-start | bytes 8388608
  493.3 19.3 %slice-start.8 = ((s8[21233664]{0:T(1024)(128)(4,1)}), s8[4194304]{0:T(1024)(128)(4,1)S(1)}, s32[]{:S(2)}) async-start(s8[21233664]{0:T(1024)(128)(4,1)} %bitcast.20), calls=%async_computation.8 | async-start | bytes 8388608
  498.0 14.6 %slice-start.9 = ((s8[21233664]{0:T(1024)(128)(4,1)}), s8[4194304]{0:T(1024)(128)(4,1)S(1)}, s32[]{:S(2)}) async-start(s8[21233664]{0:T(1024)(128)(4,1)} %bitcast.20), calls=%async_computation.9 | async-start | bytes 8388608
  498.0 14.6 %slice-start.10 = ((s8[21233664]{0:T(1024)(128)(4,1)}), s8[4194304]{0:T(1024)(128)(4,1)S(1)}, s32[]{:S(2)}) async-start(s8[21233664]{0:T(1024)(128)(4,1)} %bitcast.20), calls=%async_computation.10 | async-start | bytes 8388608
  498.0 14.6 %slice-start.11 = ((s8[21233664]{0:T(1024)(128)(4,1)}), s8[262144]{0:T(1024)(128)(4,1)S(1)}, s32[]{:S(2)}) async-start(s8[21233664]{0:T(1024)(128)(4,1)} %bitcast.20), calls=%async_computation.11 | async-start | bytes 524288
  506.1 17.3 %slice-start = ((s8[21233664]{0:T(1024)(128)(4,1)}), s8[262144]{0:T(1024)(128)(4,1)S(1)}, s32[]{:S(2)}) async-start(s8[21233664]{0:T(1024)(128)(4,1)} %bitcast.18), calls=%async_computation | async-start | bytes 524288
  506.1 17.3 %slice-start.1 = ((s8[21233664]{0:T(1024)(128)(4,1)}), s8[4194304]{0:T(1024)(128)(4,1)S(1)}, s32[]{:S(2)}) async-start(s8[21233664]{0:T(1024)(128)(4,1)} %bitcast.18), calls=%async_computation.1 | async-start | bytes 8388608
  512.6 10.8 %slice-start.2 = ((s8[21233664]{0:T(1024)(128)(4,1)}), s8[4194304]{0:T(1024)(128)(4,1)S(1)}, s32[]{:S(2)}) async-start(s8[21233664]{0:T(1024)(128)(4,1)} %bitcast.18), calls=%async_computation.2 | async-start | bytes 8388608
  512.6 10.8 %slice-start.3 = ((s8[21233664]{0:T(1024)(128)(4,1)}), s8[4194304]{0:T(1024)(128)(4,1)S(1)}, s32[]{:S(2)}) async-start(s8[21233664]{0:T(1024)(128)(4,1)} %bitcast.18), calls=%async_computation.3 | async-start | bytes 8388608
  512.6 12.3 %slice-start.4 = ((s8[21233664]{0:T(1024)(128)(4,1)}), s8[4194304]{0:T(1024)(128)(4,1)S(1)}, s32[]{:S(2)}) async-start(s8[21233664]{0:T(1024)(128)(4,1)} %bitcast.18), calls=%async_computation.4 | async-start | bytes 8388608
  512.7 13.5 %slice-start.5 = ((s8[21233664]{0:T(1024)(128)(4,1)}), s8[4194304]{0:T(1024)(128)(4,1)S(1)}, s32[]{:S(2)}) async-start(s8[21233664]{0:T(1024)(128)(4,1)} %bitcast.18), calls=%async_computation.5 | async-start | bytes 8388608

commit v5 on v4

--- a/solution.py
+++ b/solution.py
@@ -47,7 +47,7 @@
 def chain_kernel(
     seq, hid, heads, hdim, n_pairs,
     y1, y2, dy1, dy2, s1, s2, wq_h, wo_h, wi_h, wu_h,
-    ox1, ox2, od1, od2, gq, go, gi, gu,
+    fsum, ox2, od1, od2, gq, go, gi, gu,
     wq, wo, wi, wu, a_g, act, gp, dhb, finp, finr, qkvt, dqkvt, pt, ot,
     d1b, d2b, d1f, d2f, vbuf, x2r, xl, pbuf, e1r, xs, xr, gbuf, g1r, g2r, stage,
     e1s_s, e1r_s, e2s_s, e2r_s, e3s_s, e3r_s, g1s_s, g1r_s, g2s_s, g2r_s, g3s_s, g3r_s,
@@ -286,6 +286,9 @@
         finr[rows(mine(c)), :] = (state * rms_scale(state)).astype(BF)
         g3(c).start()
 
+    def f_out(c):
+        return local(gbuf.at[c, 1], fsum.at[c], ol_s.at[0, c])
+
     def g_credit():
         pl.semaphore_signal(gcred, inc=1, device_id=x_peer, device_id_type=MESH)
 
@@ -377,7 +380,10 @@
 
         for c in (0, 1):
             g_finish(c)
-        g_credit()
+
+        @pl.when(more)
+        def _():
+            g_credit()
         w_wait(1, "qo")
         for c in (0, 1):
             g3(c).wait()
@@ -412,13 +418,18 @@
         def _():
             f_part(1)
 
-        pl.semaphore_wait(gcred, 1)
         for c in (0, 1):
             g_chip(c)
-            g_send(*range(npc * c, npc * (c + 1)))
+
+        @pl.when(jnp.logical_not(more))
+        def _():
+            for c in (0, 1):
+                f_out(c).start()
 
         @pl.when(more)
         def _():
+            pl.semaphore_wait(gcred, 1)
+            g_send(*range(2 * npc))
             w_wait(0, "iu")
             mlp_fwd(0)
             for c in (0, 1):
@@ -449,13 +460,80 @@
         emit(2, d1f, c, od1)
         emit(1, x2r, c, ox2)
     for c in (0, 1):
-        v_start(False, True, 0, c)
-    for c in (0, 1):
-        v_wait(c)
-        vbuf[c] = vbuf[c] - g_total(c)
-        emit(0, vbuf, c, ox1)
+        f_out(c).wait()
     for cp in outs:
         cp.wait()
+
+
+def move_kernel(depth, chunk, *refs):
+    count = (len(refs) - 3) // 2
+    buf, in_s, out_s = refs[-3:]
+    jobs = []
+    for src, dst in zip(refs[:count], refs[count:2 * count]):
+        for lo in range(0, src.shape[0], chunk):
+            rws = pl.ds(lo, min(chunk, src.shape[0] - lo))
+            slot = len(jobs) % depth
+            part = buf.at[slot, pl.ds(0, rws.size)]
+            jobs.append((
+                pltpu.make_async_copy(src.at[rws], part, in_s.at[slot]),
+                pltpu.make_async_copy(part, dst.at[rws], out_s.at[slot]),
+            ))
+    for load, _ in jobs[:depth]:
+        load.start()
+    lag = depth // 2
+    for k in range(len(jobs)):
+        jobs[k][0].wait()
+        jobs[k][1].start()
+        if k >= lag:
+            jobs[k - lag][1].wait()
+            if k - lag + depth < len(jobs):
+                jobs[k - lag + depth][0].start()
+    for k in range(max(len(jobs) - lag, 0), len(jobs)):
+        jobs[k][1].wait()
+
+
+def move(arrays, name, depth=12, chunk=576):
+    width = arrays[0].shape[-1]
+    size = sum(arr.size for arr in arrays)
+    depth = min(depth, sum(-(-arr.shape[0] // chunk) for arr in arrays))
+    anyspec = pl.BlockSpec(memory_space=pl.ANY)
+    return pl.pallas_call(
+        functools.partial(move_kernel, depth, chunk),
+        out_shape=[jax.ShapeDtypeStruct(arr.shape, arr.dtype) for arr in arrays],
+        in_specs=[anyspec] * len(arrays),
+        out_specs=[anyspec] * len(arrays),
+        scratch_shapes=[pltpu.VMEM((depth, chunk, width), F32), pltpu.SemaphoreType.DMA((depth,)), pltpu.SemaphoreType.DMA((depth,))],
+        name=name,
+        cost_estimate=pl.CostEstimate(flops=400 * size, bytes_accessed=8 * size, transcendentals=0),
+        compiler_params=pltpu.CompilerParams(vmem_limit_bytes=60 * 2 ** 20),
+    )(*arrays)
+
+
+def join_kernel(y_ref, own_ref, peer_ref, out_ref):
+    odd = lax.rem(pl.program_id(0) + lax.axis_index("tp"), 2)
+
+    @pl.when(odd == 0)
+    def _():
+        out_ref[...] = y_ref[...] - own_ref[...]
+
+    @pl.when(odd != 0)
+    def _():
+        out_ref[...] = y_ref[...] - peer_ref[...]
+
+
+def join(y_all, own, peer):
+    _, n_seq, seq, hid = y_all.shape
+    bottom = pl.BlockSpec((None, 1, seq, hid), lambda s: (0, s, 0, 0))
+    whole = pl.BlockSpec((1, seq, hid), lambda s: (s, 0, 0))
+    half = pl.BlockSpec((1, seq, hid), lambda s: (s // 2, 0, 0))
+    return pl.pallas_call(
+        join_kernel,
+        out_shape=jax.ShapeDtypeStruct(y_all.shape[1:], F32),
+        grid=(n_seq,),
+        in_specs=[bottom, half, half],
+        out_specs=whole,
+        name="join",
+    )(y_all, own, peer)
 
 
 def solution(mesh):
@@ -495,7 +573,7 @@
         anyspec = pl.BlockSpec(memory_space=pl.ANY)
         outs = pl.pallas_call(
             functools.partial(chain_kernel, seq, hid, heads, hdim, n_pairs),
-            out_shape=[sds((tok, hid), F32)] * 4
+            out_shape=[sds(half, F32)] + [sds((tok, hid), F32)] * 3
             + [sds((n_layers, qkv_w, hid), F32), sds((n_layers, heads * hdim, hid), F32), sds((n_layers, hid, ff), F32), sds((n_layers, ff, hid), F32)],
             in_specs=[anyspec] * 10,
             out_specs=[anyspec] * 8,
@@ -503,10 +581,17 @@
             name="chain",
             compiler_params=pltpu.CompilerParams(collective_id=0, has_side_effects=True, vmem_limit_bytes=67043328),
         )(flat(y_one), flat(y_two), flat(dy_one), flat(dy_two), flat(saved_one), flat(saved_two), wq_t, wo_t, w_in, w_out)
-        states = tuple(out.reshape(n_seq, seq, hid) for out in outs[:4])
-        d_qkv = jnp.transpose(outs[4].reshape(n_layers, 3, heads, hdim, hid), (0, 4, 1, 2, 3))
-        d_o = outs[5].reshape(n_layers, heads, hdim, hid)
-        return states + (d_qkv, d_o, outs[6], outs[7])
+        f_own = outs[0]
+        f_other = lax.ppermute(f_own, "tp", [(0, 2), (2, 0), (1, 3), (3, 1)])
+        grads = move([out.reshape(-1, hid) for out in outs[4:]], "move_grads")
+        f_other, grads = lax.optimization_barrier((f_other, grads))
+        f_sum = f_own + f_other
+        f_peer = lax.ppermute(f_sum, "tp", [(0, 1), (1, 0), (2, 3), (3, 2)])
+        states = [out.reshape(n_seq, seq, hid) for out in move(outs[1:4], "move_states")]
+        x_one = join(saved_one, f_sum, f_peer)
+        d_qkv = jnp.transpose(grads[0].reshape(n_layers, 3, heads, hdim, hid), (0, 4, 1, 2, 3))
+        d_o = grads[1].reshape(n_layers, heads, hdim, hid)
+        return (x_one, *states, d_qkv, d_o, grads[2].reshape(n_layers, hid, ff), grads[3].reshape(n_layers, ff, hid))
 
     return jax.shard_map(
         per_device,

time: 534 us -> 514 us (0.963)
  local copies, waits for them, and re-layouts: 50.8 us -> 1.16 us
  Pallas kernels: 482 us -> 507 us
    pallas_call x0 -> x3, Pallas kernels: none -> 55.3 us  [the longest x2 50.2 us: move(): pl.pallas_call(functools.partial(move_kernel, depth, chunk), out_shape=[j...]
    unnamed x36 -> x6, local copies, waits for them, and re-layouts: 50.8 us -> 1.16 us
    pallas_call x1, Pallas kernels: 482 us -> 452 us  [per_device(): pl.pallas_call(functools.partial(chain_kernel, seq, hid, heads, hdim, n_p...]
  transfers between devices with their start and end apart: 0 -> 2, of which waited for: 0 -> 0; matrix products, arithmetic and copies ran while one was open for 0% -> 0% of each run, Pallas kernels for 0% -> 10%
where the time goes in v5:
time: 514 us; the launch traced here: 513 us
  Pallas kernels  507 us (99%)
    pallas_call x1, Pallas kernels, per_device(): pl.pallas_call(functools.partial(chain_kernel, seq, hid, heads, hdim, n_p...  452 us
    pallas_call x2, Pallas kernels, move(): pl.pallas_call(functools.partial(move_kernel, depth, chunk), out_shape=[j...  50.2 us
  transfers between devices with their start and end apart: 2, of which 0 were waited for; matrix products, arithmetic and copies ran while one was open for 0% of the time, Pallas kernels for 10%

profile of v5, /device:TPU:0, one launch (start us, length us, event | category | flops | bytes accessed | tf_op | source)
XLA Modules:
  0.0 513.5 jit_solution(6209155890075160024)
XLA Ops:
  0.6 452.1 %chain.1 = (f32[2,256,768]{2,1,0:T(8,128)}, f32[1024,768]{1,0:T(8,128)}, f32[1024,768]{1,0:T(8,128)}, f32[1024,768]{1,0:T(8,128)}, f32[9,576,768]{2,1,0:T(8,128)...) custom-call(f32[1024,768]{1,0:T(8,128)} %bitcast.30, f32[1024,768]{1,0:T(8,128)} %bitcast.31, ...), custom_call_target="tpu_custom_call" | custom-call | tf_op jit(solution)/shard_map/chain/pallas_call | solution.py:574
  452.7 2.5 collective-permute-start
  455.3 0.0 copy-start.2
  455.3 42.4 %move_grads.1 = (f32[5184,768]{1,0:T(8,128)}, f32[1728,768]{1,0:T(8,128)}, f32[6912,768]{1,0:T(8,128)}, f32[6912,768]{1,0:T(8,128)}) custom-call(f32[5184,768]{1,0:T(8,128)} %bitcast.26, f32[1728,768]{1,0:T(8,128)} %bitcast.29, f32[6912,768]{1,0:T(8,128)} %bitcast.24, f32[6912,768]{1,0:T(8,128)} %bitcast.25), custom_call_target="tpu_custom_call" | custom-call | flops 6370099200 | bytes 127401984 | tf_op jit(solution)/shard_map/move_grads/pallas_call | solution.py:500
  497.7 0.0 collective-permute-done
  497.7 0.0 copy-done.2
  497.7 1.6 add.3.own_ref
  499.3 0.0 copy-start
  499.3 0.0 collective-permute-start.1
  499.3 7.8 %move_states.1 = (f32[1024,768]{1,0:T(8,128)}, f32[1024,768]{1,0:T(8,128)}, f32[1024,768]{1,0:T(8,128)}) custom-call(f32[1024,768]{1,0:T(8,128)} %get-tuple-element.38.refs_0_, f32[1024,768]{1,0:T(8,128)} %get-tuple-element.39.refs_1_, f32[1024,768]{1,0:T(8,128)} %get-tuple-element.40.refs_2_), custom_call_target="tpu_custom_call" | custom-call | flops 943718400 | bytes 18874368 | tf_op jit(solution)/shard_map/move_states/pallas_call | solution.py:500
  507.2 0.0 copy-done
  507.2 0.0 collective-permute-done.1.peer_ref
  507.2 0.0 copy-start.1
  507.2 1.1 copy-done.1
  508.3 5.1 %join.1 = f32[4,256,768]{2,1,0:T(8,128)} custom-call(f32[4,4,256,768]{3,2,1,0:T(8,128)} %y_ref.1, f32[2,256,768]{2,1,0:T(8,128)} %copy-done, f32[2,256,768]{2,1,0:T(8,128)} %copy-done.1), custom_call_target="tpu_custom_call" | custom-call | tf_op jit(solution)/shard_map/join/pallas_call | solution.py:529
Async XLA Ops:
  452.7 44.9 %collective-permute-start = (f32[2,256,768]{2,1,0:T(8,128)}, f32[2,256,768]{2,1,0:T(8,128)}, u32[]{:S(2)}, u32[]{:S(2)}) collective-permute-start(f32[2,256,768]{2,1,0:T(8,128)} %get-tuple-element.28), channel_id=1, source_target_pairs={{0,2},{2,0},{1,3},{3,1},{4,6},{6,4},{5,7},{7,5},{8,10},{10,8},{9,1... | collective-permute-start | bytes 4718600 | tf_op jit(solution)/shard_map/ppermute | solution.py:585
  455.3 42.4 %copy-start.2 = (f32[2,256,768]{2,1,0:T(8,128)S(1)}, f32[2,256,768]{2,1,0:T(8,128)}, u32[]{:S(2)}) copy-start(f32[2,256,768]{2,1,0:T(8,128)} %get-tuple-element.28) | copy-start | bytes 4718596
  499.3 7.9 %copy-start = (f32[2,256,768]{2,1,0:T(8,128)}, f32[2,256,768]{2,1,0:T(8,128)S(1)}, u32[]{:S(2)}) copy-start(f32[2,256,768]{2,1,0:T(8,128)S(1)} %add.3.own_ref) | copy-start | bytes 4718596
  499.3 7.9 %collective-permute-start.1 = (f32[2,256,768]{2,1,0:T(8,128)S(1)}, f32[2,256,768]{2,1,0:T(8,128)S(1)}, u32[]{:S(2)}, u32[]{:S(2)}) collective-permute-start(f32[2,256,768]{2,1,0:T(8,128)S(1)} %add.3.own_ref), channel_id=1, source_target_pairs={{0,1},{1,0},{2,3},{3,2},{4,5},{5,4},{6,7},{7,6},{8,9},{9,8},{10,11... | collective-permute-start | bytes 4718600 | tf_op jit(solution)/shard_map/ppermute | solution.py:589
  507.2 1.2 copy-start.1

commit v6 on v5

--- a/solution.py
+++ b/solution.py
@@ -137,15 +137,14 @@
         cols = rows(s)
         qkv = dot(wq[slot], fin[cols, :], NT).astype(BF)
         qkvt[:, cols] = qkv
+        part = lambda j, h: qkv[j * qw + h * hdim:j * qw + (h + 1) * hdim]
+        scores = [dot(part(1, h), part(0, h), TN) * (hdim ** -0.5) for h in range(heads)]
+        exps = [jnp.exp(sc - jnp.max(sc, axis=0, keepdims=True)) for sc in scores]
+        probs = [ex * (1.0 / jnp.sum(ex, axis=0, keepdims=True)) for ex in exps]
         for h in range(heads):
-            q_t = qkv[h * hdim:(h + 1) * hdim]
-            k_t = qkv[qw + h * hdim:qw + (h + 1) * hdim]
-            v_t = qkv[2 * qw + h * hdim:2 * qw + (h + 1) * hdim]
-            sc = dot(k_t, q_t, TN) * (hdim ** -0.5)
-            ex = jnp.exp(sc - jnp.max(sc, axis=0, keepdims=True))
-            prob = ex * (1.0 / jnp.sum(ex, axis=0, keepdims=True))
-            pt[s * heads + h] = prob
-            ot[h * hdim:(h + 1) * hdim, cols] = dot(v_t, prob.astype(BF), NN).astype(BF)
+            pt[s * heads + h] = probs[h]
+        for h in range(heads):
+            ot[h * hdim:(h + 1) * hdim, cols] = dot(part(2, h), probs[h].astype(BF), NN).astype(BF)
 
     def attn_fwd_plain(pair):
         def body(i, s, state):
@@ -165,42 +164,35 @@
         return remote(xs.at[t, c], xr.at[t, c], e2s_s.at[t, c], e2r_s.at[t, c], x_peer)
 
     def part_g(slot, ver, c, mode, e1_slot=None):
-        @pl.loop(0, 2)
-        def _(i):
-            s = 2 * c + jnp.where(i == 0, 1 - ci, ci)
+        for i, s in enumerate((theirs(c), mine(c))):
             d_act = dot(d2b[ver, rows(s), :], wu[slot], NT)
             dh = (d_act * gp[rows(s), :]).astype(BF)
             dhb[rows(s), :] = dh
             part = dot(dh, wi[slot], NT)
             pbuf[c, i] = pbuf[c, i] + part if mode == "add" else part
-            if mode != "hold":
-                @pl.when(i == 0)
-                def _():
-                    e1(e1_slot, c).start()
+            if mode != "hold" and i == 0:
+                e1(e1_slot, c).start()
 
     def part_f(slot, c, e1_slot):
-        @pl.loop(0, 2)
-        def _(i):
-            s = 2 * c + jnp.where(i == 0, 1 - ci, ci)
+        each = range(heads)
+        for i, s in enumerate((theirs(c), mine(c))):
             cols = rows(s)
             do_t = dot(wo[slot], d1b[cols, :], NT).astype(BF)
-            for h in range(heads):
-                lo = h * hdim
-                do_h = do_t[lo:lo + hdim]
-                prob = pt[s * heads + h]
-                q_t = qkvt[lo:lo + hdim, cols]
-                k_t = qkvt[qw + lo:qw + lo + hdim, cols]
-                v_t = qkvt[2 * qw + lo:2 * qw + lo + hdim, cols]
-                dqkvt[2 * qw + lo:2 * qw + lo + hdim, cols] = dot(do_h, prob.astype(BF), NT).astype(BF)
-                dp_t = dot(v_t, do_h, TN)
-                inner = jnp.sum(prob * dp_t, axis=0, keepdims=True)
-                ds = (prob * (dp_t - inner) * (hdim ** -0.5)).astype(BF)
-                dqkvt[lo:lo + hdim, cols] = dot(k_t, ds, NN).astype(BF)
-                dqkvt[qw + lo:qw + lo + hdim, cols] = dot(q_t, ds, NT).astype(BF)
-            pbuf[c, i] = dot(dqkvt[:, cols], wq[slot], TN)
-
-            @pl.when(i == 0)
-            def _():
+            do = [do_t[h * hdim:(h + 1) * hdim] for h in each]
+            part = lambda j, h: qkvt[j * qw + h * hdim:j * qw + (h + 1) * hdim, cols]
+            probs = [pt[s * heads + h] for h in each]
+            dps = [dot(part(2, h), do[h], TN) for h in each]
+            dv = [dot(do[h], probs[h].astype(BF), NT).astype(BF) for h in each]
+            ds = []
+            for h in each:
+                inner = jnp.sum(probs[h] * dps[h], axis=0, keepdims=True)
+                ds.append((probs[h] * (dps[h] - inner) * (hdim ** -0.5)).astype(BF))
+            dq = [dot(part(1, h), ds[h], NN).astype(BF) for h in each]
+            dk = [dot(part(0, h), ds[h], NT).astype(BF) for h in each]
+            d_qkv = jnp.concatenate(dq + dk + dv, axis=0)
+            dqkvt[:, cols] = d_qkv
+            pbuf[c, i] = dot(d_qkv, wq[slot], TN)
+            if i == 0:
                 e1(e1_slot, c).start()
 
     def to_x(t, c, e1_slot):
@@ -360,13 +352,15 @@
 
         @pl.when(is_top)
         def _():
-            for c in (0, 1):
+            @pl.loop(0, 2)
+            def _(c):
                 part_g(1, 1, c, "first", odd)
                 to_x(1, c, odd)
 
         @pl.when(it > 0)
         def _():
-            for c in (0, 1):
+            @pl.loop(0, 2)
+            def _(c):
                 v_wait(c)
                 finish(0, c, 2, d2f, vbuf[c])
                 v_start(False, True, pair, c)
@@ -389,7 +383,8 @@
             g3(c).wait()
         attn_fwd_rev()
 
-        for c in (0, 1):
+        @pl.loop(0, 2)
+        def _(c):
             v_wait(c)
             finish(1, c, 0, d1f, vbuf[c])
             e3(0, c).wait()
@@ -404,7 +399,8 @@
                 v_start(False, False, pair - 1, c)
             w_wait(0, "qo")
             attn_fwd_plain(pair - 1)
-            for c in (0, 1):
+            @pl.loop(0, 2)
+            def _(c):
                 part_f(0, c, odd)
                 to_x(0, c, odd)
         mlp_grads(rev, 1)
@@ -435,7 +431,8 @@
             for c in (0, 1):
                 finish(2, c, 1, d2f, x2r[c])
                 state_start(False, False, pair - 1, rows(mine(c)), x2r.at[c], x2_s.at[c])
-            for c in (0, 1):
+            @pl.loop(0, 2)
+            def _(c):
                 e3(1, c).wait()
                 part_g(0, 0, c, "hold")
 

time: 514 us -> 503 us (0.979)
  Pallas kernels: 507 us -> 497 us
    pallas_call x1, Pallas kernels: 452 us -> 441 us  [per_device(): pl.pallas_call(functools.partial(chain_kernel, seq, hid, heads, hdim, n_p...]
where the time goes in v6:
time: 503 us
  Pallas kernels  497 us (99%)
    pallas_call x1, Pallas kernels, per_device(): pl.pallas_call(functools.partial(chain_kernel, seq, hid, heads, hdim, n_p...  441 us
    pallas_call x2, Pallas kernels, move(): pl.pallas_call(functools.partial(move_kernel, depth, chunk), out_shape=[j...  50.2 us
  transfers between devices with their start and end apart: 2, of which 0 were waited for; matrix products, arithmetic and copies ran while one was open for 0% of the time, Pallas kernels for 10%

profile of v6, /device:TPU:0, one launch (start us, length us, event | category | flops | bytes accessed | tf_op | source)
XLA Modules:
  0.0 502.9 jit_solution(12203796317782271382)
XLA Ops:
  0.6 441.5 %chain.1 = (f32[2,256,768]{2,1,0:T(8,128)}, f32[1024,768]{1,0:T(8,128)}, f32[1024,768]{1,0:T(8,128)}, f32[1024,768]{1,0:T(8,128)}, f32[9,576,768]{2,1,0:T(8,128)...) custom-call(f32[1024,768]{1,0:T(8,128)} %bitcast.30, f32[1024,768]{1,0:T(8,128)} %bitcast.31, ...), custom_call_target="tpu_custom_call" | custom-call | tf_op jit(solution)/shard_map/chain/pallas_call | solution.py:571
  442.1 2.5 collective-permute-start
  444.7 0.0 copy-start.2
  444.7 42.4 %move_grads.1 = (f32[5184,768]{1,0:T(8,128)}, f32[1728,768]{1,0:T(8,128)}, f32[6912,768]{1,0:T(8,128)}, f32[6912,768]{1,0:T(8,128)}) custom-call(f32[5184,768]{1,0:T(8,128)} %bitcast.26, f32[1728,768]{1,0:T(8,128)} %bitcast.29, f32[6912,768]{1,0:T(8,128)} %bitcast.24, f32[6912,768]{1,0:T(8,128)} %bitcast.25), custom_call_target="tpu_custom_call" | custom-call | flops 6370099200 | bytes 127401984 | tf_op jit(solution)/shard_map/move_grads/pallas_call | solution.py:497
  487.1 0.0 collective-permute-done
  487.1 0.0 copy-done.2
  487.1 1.6 add.3.own_ref
  488.7 0.0 copy-start
  488.7 0.0 collective-permute-start.1
  488.7 7.8 %move_states.1 = (f32[1024,768]{1,0:T(8,128)}, f32[1024,768]{1,0:T(8,128)}, f32[1024,768]{1,0:T(8,128)}) custom-call(f32[1024,768]{1,0:T(8,128)} %get-tuple-element.38.refs_0_, f32[1024,768]{1,0:T(8,128)} %get-tuple-element.39.refs_1_, f32[1024,768]{1,0:T(8,128)} %get-tuple-element.40.refs_2_), custom_call_target="tpu_custom_call" | custom-call | flops 943718400 | bytes 18874368 | tf_op jit(solution)/shard_map/move_states/pallas_call | solution.py:497
  496.6 0.0 copy-done
  496.6 0.0 collective-permute-done.1.peer_ref
  496.6 0.0 copy-start.1
  496.6 1.1 copy-done.1
  497.7 5.1 %join.1 = f32[4,256,768]{2,1,0:T(8,128)} custom-call(f32[4,4,256,768]{3,2,1,0:T(8,128)} %y_ref.1, f32[2,256,768]{2,1,0:T(8,128)} %copy-done, f32[2,256,768]{2,1,0:T(8,128)} %copy-done.1), custom_call_target="tpu_custom_call" | custom-call | tf_op jit(solution)/shard_map/join/pallas_call | solution.py:526
Async XLA Ops:
  442.1 44.9 %collective-permute-start = (f32[2,256,768]{2,1,0:T(8,128)}, f32[2,256,768]{2,1,0:T(8,128)}, u32[]{:S(2)}, u32[]{:S(2)}) collective-permute-start(f32[2,256,768]{2,1,0:T(8,128)} %get-tuple-element.28), channel_id=1, source_target_pairs={{0,2},{2,0},{1,3},{3,1},{4,6},{6,4},{5,7},{7,5},{8,10},{10,8},{9,1... | collective-permute-start | bytes 4718600 | tf_op jit(solution)/shard_map/ppermute | solution.py:582
  444.7 42.4 %copy-start.2 = (f32[2,256,768]{2,1,0:T(8,128)S(1)}, f32[2,256,768]{2,1,0:T(8,128)}, u32[]{:S(2)}) copy-start(f32[2,256,768]{2,1,0:T(8,128)} %get-tuple-element.28) | copy-start | bytes 4718596
  488.7 7.9 %copy-start = (f32[2,256,768]{2,1,0:T(8,128)}, f32[2,256,768]{2,1,0:T(8,128)S(1)}, u32[]{:S(2)}) copy-start(f32[2,256,768]{2,1,0:T(8,128)S(1)} %add.3.own_ref) | copy-start | bytes 4718596
  488.7 7.9 %collective-permute-start.1 = (f32[2,256,768]{2,1,0:T(8,128)S(1)}, f32[2,256,768]{2,1,0:T(8,128)S(1)}, u32[]{:S(2)}, u32[]{:S(2)}) collective-permute-start(f32[2,256,768]{2,1,0:T(8,128)S(1)} %add.3.own_ref), channel_id=1, source_target_pairs={{0,1},{1,0},{2,3},{3,2},{4,5},{5,4},{6,7},{7,6},{8,9},{9,8},{10,11... | collective-permute-start | bytes 4718600 | tf_op jit(solution)/shard_map/ppermute | solution.py:586
  496.6 1.2 copy-start.1

commit v7 on v6

--- a/solution.py
+++ b/solution.py
@@ -47,11 +47,11 @@
 def chain_kernel(
     seq, hid, heads, hdim, n_pairs,
     y1, y2, dy1, dy2, s1, s2, wq_h, wo_h, wi_h, wu_h,
-    fsum, ox2, od1, od2, gq, go, gi, gu,
+    f_own, j_own, fsum, jsum, ox2, od1, od2, gq, go, gi, gu,
     wq, wo, wi, wu, a_g, act, gp, dhb, finp, finr, qkvt, dqkvt, pt, ot,
     d1b, d2b, d1f, d2f, vbuf, x2r, xl, pbuf, e1r, xs, xr, gbuf, g1r, g2r, stage,
     e1s_s, e1r_s, e2s_s, e2r_s, e3s_s, e3r_s, g1s_s, g1r_s, g2s_s, g2r_s, g3s_s, g3r_s,
-    os_s, or_s, ol_s, w_s, xl_s, v_s, x2_s, st_s, d_s, gcred,
+    os_s, or_s, ol_s, oo_s, w_s, xl_s, v_s, x2_s, st_s, d_s, gcred,
 ):
     me = lax.axis_index("tp")
     dp = lax.axis_index("dp")
@@ -156,6 +156,26 @@
         @pl.loop(0, 4)
         def _(s):
             attn_fwd_seq(1, finr, s)
+
+    results = ((xs.at[2], jsum), (gbuf.at[:, 1], fsum), (x2r, ox2), (d1f, od1), (d2f, od2))
+
+    def emit_copies(idx, c):
+        ref, out = results[idx]
+        rws = out.at[rows(mine(c))]
+        return (
+            local(ref.at[c], rws, ol_s.at[idx, c]),
+            remote(ref.at[c], rws, os_s.at[idx, c], or_s.at[idx, c], core_peer),
+        )
+
+    def own_copy(idx, c):
+        return local(results[idx][0].at[c], (j_own, f_own)[idx].at[c], oo_s.at[idx, c])
+
+    def emit(idx, c):
+        for cp in emit_copies(idx, c):
+            cp.start()
+
+    def emit_own(idx, c):
+        own_copy(idx, c).start()
 
     def e1(slot, c):
         return remote(pbuf.at[c, 0], e1r.at[slot, c], e1s_s.at[slot, c], e1r_s.at[slot, c], core_peer)
@@ -195,10 +215,20 @@
             if i == 0:
                 e1(e1_slot, c).start()
 
-    def to_x(t, c, e1_slot):
+    def to_x(t, c, e1_slot, last=None):
         e1(e1_slot, c).wait()
         xs[t, c] = (pbuf[c, 1] + e1r[e1_slot, c]).astype(BF)
-        e2(t, c).start()
+        if last is None:
+            e2(t, c).start()
+        else:
+            @pl.when(jnp.logical_not(last))
+            def _():
+                e2(t, c).start()
+
+            @pl.when(last)
+            def _():
+                emit_own(0, c)
+                emit(0, c)
 
     def summed(t, c):
         e2(t, c).wait()
@@ -277,9 +307,6 @@
         x2r[c] = state
         finr[rows(mine(c)), :] = (state * rms_scale(state)).astype(BF)
         g3(c).start()
-
-    def f_out(c):
-        return local(gbuf.at[c, 1], fsum.at[c], ol_s.at[0, c])
 
     def g_credit():
         pl.semaphore_signal(gcred, inc=1, device_id=x_peer, device_id_type=MESH)
@@ -378,6 +405,12 @@
         @pl.when(more)
         def _():
             g_credit()
+
+        @pl.when(jnp.logical_not(more))
+        def _():
+            for c in (0, 1):
+                emit(2, c)
+                emit(4, c)
         w_wait(1, "qo")
         for c in (0, 1):
             g3(c).wait()
@@ -387,9 +420,13 @@
         def _(c):
             v_wait(c)
             finish(1, c, 0, d1f, vbuf[c])
+
+            @pl.when(jnp.logical_not(more))
+            def _():
+                emit(3, c)
             e3(0, c).wait()
             part_f(1, c, even)
-            to_x(2, c, even)
+            to_x(2, c, even, jnp.logical_not(more))
         attn_grads(rev, finr)
 
         @pl.when(more)
@@ -403,27 +440,21 @@
             def _(c):
                 part_f(0, c, odd)
                 to_x(0, c, odd)
+        @pl.when(jnp.logical_not(more))
+        def _():
+            f_part(1)
+            for c in (0, 1):
+                g_chip(c)
+                emit_own(1, c)
+                emit(1, c)
         mlp_grads(rev, 1)
 
         @pl.when(more)
         def _():
             w_wait(1, "iu")
             g_part(1, False, pair - 1, False)
-
-        @pl.when(jnp.logical_not(more))
-        def _():
-            f_part(1)
-
-        for c in (0, 1):
-            g_chip(c)
-
-        @pl.when(jnp.logical_not(more))
-        def _():
             for c in (0, 1):
-                f_out(c).start()
-
-        @pl.when(more)
-        def _():
+                g_chip(c)
             pl.semaphore_wait(gcred, 1)
             g_send(*range(2 * npc))
             w_wait(0, "iu")
@@ -443,23 +474,12 @@
             attn_grads(rev - 1, finp)
             mlp_fwd(1)
 
-    outs = []
-
-    def emit(idx, ref, c, out):
-        outs.append(local(ref.at[c], out.at[rows(mine(c))], ol_s.at[idx, c]))
-        outs.append(remote(ref.at[c], out.at[rows(mine(c))], os_s.at[idx, c], or_s.at[idx, c], core_peer))
-        outs[-2].start()
-        outs[-1].start()
-
     for c in (0, 1):
-        finish(2, c, None, d2f, x2r[c])
-        emit(3, d2f, c, od2)
-        emit(2, d1f, c, od1)
-        emit(1, x2r, c, ox2)
-    for c in (0, 1):
-        f_out(c).wait()
-    for cp in outs:
-        cp.wait()
+        for idx in (0, 1):
+            own_copy(idx, c).wait()
+        for idx in range(5):
+            for cp in emit_copies(idx, c):
+                cp.wait()
 
 
 def move_kernel(depth, chunk, *refs):
@@ -506,31 +526,42 @@
     )(*arrays)
 
 
-def join_kernel(y_ref, own_ref, peer_ref, out_ref):
+def take_kernel(finish, *refs):
+    *base, near_ref, far_ref, out_ref = refs
     odd = lax.rem(pl.program_id(0) + lax.axis_index("tp"), 2)
 
     @pl.when(odd == 0)
     def _():
-        out_ref[...] = y_ref[...] - own_ref[...]
+        out_ref[...] = finish(near_ref[...].astype(F32), *[ref[...] for ref in base])
 
     @pl.when(odd != 0)
     def _():
-        out_ref[...] = y_ref[...] - peer_ref[...]
-
-
-def join(y_all, own, peer):
-    _, n_seq, seq, hid = y_all.shape
-    bottom = pl.BlockSpec((None, 1, seq, hid), lambda s: (0, s, 0, 0))
-    whole = pl.BlockSpec((1, seq, hid), lambda s: (s, 0, 0))
-    half = pl.BlockSpec((1, seq, hid), lambda s: (s // 2, 0, 0))
+        out_ref[...] = finish(far_ref[...].astype(F32), *[ref[...] for ref in base])
+
+
+def take(finish, name, shape, base, near, far, parts=2):
+    n_seq, seq, hid = shape
+    part = seq // parts
+    whole = pl.BlockSpec((1, part, hid), lambda s, r: (s, r, 0))
+    bottom = pl.BlockSpec((None, 1, part, hid), lambda s, r: (0, s, r, 0))
+    half = pl.BlockSpec((1, part, hid), lambda s, r: (s // 2, r, 0))
     return pl.pallas_call(
-        join_kernel,
-        out_shape=jax.ShapeDtypeStruct(y_all.shape[1:], F32),
-        grid=(n_seq,),
-        in_specs=[bottom, half, half],
+        functools.partial(take_kernel, finish),
+        out_shape=jax.ShapeDtypeStruct(shape, F32),
+        grid=(n_seq, parts),
+        in_specs=[whole if arr.ndim == 3 else bottom for arr in base] + [half, half],
         out_specs=whole,
-        name="join",
-    )(y_all, own, peer)
+        name=name,
+        cost_estimate=pl.CostEstimate(flops=40_000_000, bytes_accessed=16_000_000, transcendentals=0),
+    )(*base, near, far)
+
+
+def finish_x(other, state, own):
+    return state - (own + other)
+
+
+def finish_d(other, grad, state, own):
+    return grad + rms_pull(state, own.astype(F32) + other)
 
 
 def solution(mesh):
@@ -564,31 +595,34 @@
             vm((2,) + half, F32), vm(half, F32), vm(half, F32), vm((3, 256, hid), F32),
             dma((2, 2)), dma((2, 2)), dma((3, 2)), dma((3, 2)), dma((3, 2)), dma((3, 2)),
             dma((2,)), dma((2,)), dma((8,)), dma((8,)), dma((2,)), dma((2,)),
-            dma((4, 2)), dma((4, 2)), dma((4, 2)), dma((2, 4)), dma((2,)), dma((2,)), dma((2,)), dma((3,)), dma((2, 2)),
+            dma((5, 2)), dma((5, 2)), dma((5, 2)), dma((2, 2)), dma((2, 4)), dma((2,)), dma((2,)), dma((2,)), dma((3,)), dma((2, 2)),
             pltpu.SemaphoreType.REGULAR,
         ]
         anyspec = pl.BlockSpec(memory_space=pl.ANY)
         outs = pl.pallas_call(
             functools.partial(chain_kernel, seq, hid, heads, hdim, n_pairs),
-            out_shape=[sds(half, F32)] + [sds((tok, hid), F32)] * 3
+            out_shape=[sds(half, F32), sds(half, BF), sds((tok, hid), F32), sds((tok, hid), BF)] + [sds((tok, hid), F32)] * 3
             + [sds((n_layers, qkv_w, hid), F32), sds((n_layers, heads * hdim, hid), F32), sds((n_layers, hid, ff), F32), sds((n_layers, ff, hid), F32)],
             in_specs=[anyspec] * 10,
-            out_specs=[anyspec] * 8,
+            out_specs=[anyspec] * 11,
             scratch_shapes=scratch,
             name="chain",
             compiler_params=pltpu.CompilerParams(collective_id=0, has_side_effects=True, vmem_limit_bytes=67043328),
         )(flat(y_one), flat(y_two), flat(dy_one), flat(dy_two), flat(saved_one), flat(saved_two), wq_t, wo_t, w_in, w_out)
-        f_own = outs[0]
-        f_other = lax.ppermute(f_own, "tp", [(0, 2), (2, 0), (1, 3), (3, 1)])
-        grads = move([out.reshape(-1, hid) for out in outs[4:]], "move_grads")
-        f_other, grads = lax.optimization_barrier((f_other, grads))
-        f_sum = f_own + f_other
-        f_peer = lax.ppermute(f_sum, "tp", [(0, 1), (1, 0), (2, 3), (3, 2)])
-        states = [out.reshape(n_seq, seq, hid) for out in move(outs[1:4], "move_states")]
-        x_one = join(saved_one, f_sum, f_peer)
+        f_own, j_own, f_all, j_all, x_two, d_one, d_two = outs[:7]
+        cube = lambda arr: arr.reshape(n_seq, seq, hid)
+        over_x = lambda arr: lax.ppermute(arr, "tp", [(0, 2), (2, 0), (1, 3), (3, 1)])
+        over_core = lambda arr: lax.ppermute(arr, "tp", [(0, 1), (1, 0), (2, 3), (3, 2)])
+        f_near, j_near = over_x(f_own), over_x(j_own)
+        grads = move([out.reshape(-1, hid) for out in outs[7:]], "move_grads")
+        f_near, j_near, grads = lax.optimization_barrier((f_near, j_near, grads))
+        f_far, j_far = over_core(f_near), over_core(j_near)
+        states = [cube(out) for out in move([x_two, d_one], "move_states")]
+        x_one = take(finish_x, "finish_x", (n_seq, seq, hid), [saved_one, cube(f_all)], f_near, f_far)
+        dx_two = take(finish_d, "finish_d", (n_seq, seq, hid), [cube(d_two), cube(x_two), cube(j_all)], j_near, j_far)
         d_qkv = jnp.transpose(grads[0].reshape(n_layers, 3, heads, hdim, hid), (0, 4, 1, 2, 3))
         d_o = grads[1].reshape(n_layers, heads, hdim, hid)
-        return (x_one, *states, d_qkv, d_o, grads[2].reshape(n_layers, hid, ff), grads[3].reshape(n_layers, ff, hid))
+        return (x_one, *states, dx_two, d_qkv, d_o, grads[2].reshape(n_layers, hid, ff), grads[3].reshape(n_layers, ff, hid))
 
     return jax.shard_map(
         per_device,

time: 503 us -> 512 us (1.018)
  waiting for transfers between devices: 0.01 us -> 9.63 us
    pallas_call x1 -> x2, Pallas kernels: 5.14 us -> 16.5 us  [take(): pl.pallas_call(functools.partial(take_kernel, finish), out_shape=jax.Shap...]
    ppermute x2 -> x4, waiting for transfers between devices: 0.01 us -> 9.63 us  [the longest x2 9.62 us: per_device(): lax.ppermute(arr, 'tp', [(0, 2), (2, 0), (1, 3), (3, 1)])]
    pallas_call x1, Pallas kernels: 441 us -> 433 us  [per_device(): pl.pallas_call(functools.partial(chain_kernel, seq, hid, heads, hdim, n_p...]
  transfers between devices with their start and end apart: 2 -> 4, of which waited for: 0 -> 1; matrix products, arithmetic and copies ran while one was open for 0% -> 0% of each run, Pallas kernels for 10% -> 11%
where the time goes in v7:
time: 512 us; the launch traced here: 511 us
  Pallas kernels  496 us (97%)
  waiting for transfers between devices  9.63 us (2%)
    pallas_call x1, Pallas kernels, per_device(): pl.pallas_call(functools.partial(chain_kernel, seq, hid, heads, hdim, n_p...  433 us
    pallas_call x2, Pallas kernels, move(): pl.pallas_call(functools.partial(move_kernel, depth, chunk), out_shape=[j...  47 us
    pallas_call x2, Pallas kernels, take(): pl.pallas_call(functools.partial(take_kernel, finish), out_shape=jax.Shap...  16.5 us
  transfers between devices with their start and end apart: 4, of which 1 were waited for; matrix products, arithmetic and copies ran while one was open for 0% of the time, Pallas kernels for 11%

profile of v7, /device:TPU:0, one launch (start us, length us, event | category | flops | bytes accessed | tf_op | source)
XLA Modules:
  0.0 511.0 jit_solution(13002777486963592123)
XLA Ops:
  0.6 433.0 %chain.1 = (f32[2,256,768]{2,1,0:T(8,128)}, bf16[2,256,768]{2,1,0:T(8,128)(2,1)}, f32[1024,768]{1,0:T(8,128)}, bf16[1024,768]{1,0:T(8,128)(2,1)}, f32[1024,768]{...) custom-call(f32[1024,768]{1,0:T(8,128)} %bitcast.34, ...), custom_call_target="tpu_custom_call" | custom-call | tf_op jit(solution)/shard_map/chain/pallas_call | solution.py:602
  433.6 2.5 collective-permute-start
  436.2 0.0 collective-permute-start.1
  436.2 42.1 %move_grads.1 = (f32[5184,768]{1,0:T(8,128)}, f32[1728,768]{1,0:T(8,128)}, f32[6912,768]{1,0:T(8,128)}, f32[6912,768]{1,0:T(8,128)}) custom-call(f32[5184,768]{1,0:T(8,128)} %bitcast.29, f32[1728,768]{1,0:T(8,128)} %bitcast.33, f32[6912,768]{1,0:T(8,128)} %bitcast.27, f32[6912,768]{1,0:T(8,128)} %bitcast.28), custom_call_target="tpu_custom_call" | custom-call | flops 6370099200 | bytes 127401984 | tf_op jit(solution)/shard_map/move_grads/pallas_call | solution.py:517
  478.3 9.6 %collective-permute-done.1.refs_3_ = bf16[2,256,768]{2,1,0:T(8,128)(2,1)} collective-permute-done((bf16[2,256,768]{2,1,0:T(8,128)(2,1)}, bf16[2,256,768]{2,1,0:T(8,128)(2,1)}, u32[]{:S(2)}, u32[]{:S(2)}) %collective-permute-start.1) | collective-permute-done | bytes 786464 | tf_op jit(solution)/shard_map/ppermute | solution.py:614
  487.9 0.0 collective-permute-done.refs_2_
  487.9 0.0 copy-start
  487.9 0.0 collective-permute-start.2
  488.0 0.5 collective-permute-start.3
  488.5 4.9 move_states.1
  493.4 0.0 copy-done
  493.4 0.0 collective-permute-done.3.refs_4_
  493.4 8.4 %finish_d.1 = f32[4,256,768]{2,1,0:T(8,128)} custom-call(f32[4,256,768]{2,1,0:T(8,128)} %bitcast.38, f32[4,256,768]{2,1,0:T(8,128)} %bitcast.30, bf16[4,256,768]{2,1,0:T(8,128)(2,1)} %bitcast.41, bf16[2,256,768]{2,1,0:T(8,128)(2,1)} %collective-permute-done.1.refs_3_, bf16[2,256,768]{2,1,0:T(8,128)(2,1)} %collective-permute-done.3.refs_4_), custom_call_target="tpu_custom_call" | custom-call | flops 40000000 | bytes 16000000 | tf_op jit(solution)/shard_map/finish_d/pallas_call | solution.py:548
  501.9 0.0 collective-permute-done.2.refs_3_
  501.9 0.0 copy-start.1
  501.9 1.1 copy-done.1
  503.0 8.0 %finish_x.1 = f32[4,256,768]{2,1,0:T(8,128)} custom-call(f32[4,4,256,768]{3,2,1,0:T(8,128)} %refs_0_.1, f32[4,256,768]{2,1,0:T(8,128)} %bitcast.39, f32[2,256,768]{2,1,0:T(8,128)} %copy-done, f32[2,256,768]{2,1,0:T(8,128)} %copy-done.1), custom_call_target="tpu_custom_call" | custom-call | flops 40000000 | bytes 16000000 | tf_op jit(solution)/shard_map/finish_x/pallas_call | solution.py:548
Async XLA Ops:
  433.6 54.3 %collective-permute-start = (f32[2,256,768]{2,1,0:T(8,128)}, f32[2,256,768]{2,1,0:T(8,128)S(1)}, u32[]{:S(2)}, u32[]{:S(2)}) collective-permute-start(f32[2,256,768]{2,1,0:T(8,128)} %get-tuple-element.32), channel_id=1, source_target_pairs={{0,2},{2,0},{1,3},{3,1},{4,6},{6,4},{5,7},{7,5},{8,10},{10,8},{9,1... | collective-permute-start | bytes 4718600 | tf_op jit(solution)/shard_map/ppermute | solution.py:614
  436.2 51.8 %collective-permute-start.1 = (bf16[2,256,768]{2,1,0:T(8,128)(2,1)}, bf16[2,256,768]{2,1,0:T(8,128)(2,1)}, u32[]{:S(2)}, u32[]{:S(2)}) collective-permute-start(bf16[2,256,768]{2,1,0:T(8,128)(2,1)} %get-tuple-element.33), channel_id=1, source_target_pairs={{0,2},{2,0},{1,3},{3,1},{4,6},{6,4},{5,7},{7,5},{8,10},{10,8},{9,1... | collective-permute-start | bytes 2359304 | tf_op jit(solution)/shard_map/ppermute | solution.py:614
  487.9 5.5 %copy-start = (f32[2,256,768]{2,1,0:T(8,128)}, f32[2,256,768]{2,1,0:T(8,128)S(1)}, u32[]{:S(2)}) copy-start(f32[2,256,768]{2,1,0:T(8,128)S(1)} %collective-permute-done.refs_2_) | copy-start | bytes 4718596
  487.9 13.9 %collective-permute-start.2 = (f32[2,256,768]{2,1,0:T(8,128)S(1)}, f32[2,256,768]{2,1,0:T(8,128)S(1)}, u32[]{:S(2)}, u32[]{:S(2)}) collective-permute-start(f32[2,256,768]{2,1,0:T(8,128)S(1)} %collective-permute-done.refs_2_), channel_id=1, source_target_pairs={{0,1},{1,0},{2,3},{3,2},{4,5},{5,4},{6,7},{7,6},{8,9},{9,8},{10,11... | collective-permute-start | bytes 4718600 | tf_op jit(solution)/shard_map/ppermute | solution.py:615
  488.0 5.5 %collective-permute-start.3 = (bf16[2,256,768]{2,1,0:T(8,128)(2,1)}, bf16[2,256,768]{2,1,0:T(8,128)(2,1)}, u32[]{:S(2)}, u32[]{:S(2)}) collective-permute-start(bf16[2,256,768]{2,1,0:T(8,128)(2,1)} %collective-permute-done.1.refs_3_), channel_id=1, source_target_pairs={{0,1},{1,0},{2,3},{3,2},{4,5},{5,4},{6,7},{7,6},{8,9},{9,8},{10,11... | collective-permute-start | bytes 2359304 | tf_op jit(solution)/shard_map/ppermute | solution.py:615
  501.9 1.2 copy-start.1

commit v8 on v7

--- a/solution.py
+++ b/solution.py
@@ -65,7 +65,6 @@
     barrier = pltpu.get_barrier_semaphore()
     pl.semaphore_signal(barrier, inc=1, device_id=core_peer, device_id_type=MESH)
     pl.semaphore_signal(barrier, inc=1, device_id=x_peer, device_id_type=MESH)
-    pl.semaphore_wait(barrier, 2)
 
     def rows(seq_idx):
         return pl.ds(pl.multiple_of(seq_idx * seq, seq), seq)
@@ -167,15 +166,15 @@
             remote(ref.at[c], rws, os_s.at[idx, c], or_s.at[idx, c], core_peer),
         )
 
-    def own_copy(idx, c):
-        return local(results[idx][0].at[c], (j_own, f_own)[idx].at[c], oo_s.at[idx, c])
+    def own_copy(c):
+        return local(results[0][0].at[c], j_own.at[c], oo_s.at[c]) if c is not None else local(gbuf.at[1, 1], f_own, oo_s.at[2])
 
     def emit(idx, c):
         for cp in emit_copies(idx, c):
             cp.start()
 
-    def emit_own(idx, c):
-        own_copy(idx, c).start()
+    def emit_own(c):
+        own_copy(c).start()
 
     def e1(slot, c):
         return remote(pbuf.at[c, 0], e1r.at[slot, c], e1s_s.at[slot, c], e1r_s.at[slot, c], core_peer)
@@ -227,7 +226,7 @@
 
             @pl.when(last)
             def _():
-                emit_own(0, c)
+                emit_own(c)
                 emit(0, c)
 
     def summed(t, c):
@@ -355,6 +354,7 @@
         state_start(True, False, 0, rows(mine(c)), x2r.at[c], x2_s.at[c])
         local(dy1.at[rows(mine(c))], d1f.at[c], d_s.at[0, c]).start()
         local(dy2.at[rows(mine(c))], d2f.at[c], d_s.at[1, c]).start()
+    pl.semaphore_wait(barrier, 2)
     w_wait(1, "iu")
     g_part(1, True, 0, True)
     for c in (0, 1):
@@ -402,9 +402,7 @@
         for c in (0, 1):
             g_finish(c)
 
-        @pl.when(more)
-        def _():
-            g_credit()
+        g_credit()
 
         @pl.when(jnp.logical_not(more))
         def _():
@@ -415,6 +413,16 @@
         for c in (0, 1):
             g3(c).wait()
         attn_fwd_rev()
+
+        @pl.when(jnp.logical_not(more))
+        def _():
+            f_part(1)
+            g_chip(0)
+            pl.semaphore_wait(gcred, 1)
+            g_send(*range(npc))
+            g_chip(1)
+            emit_own(None)
+            emit(1, 1)
 
         @pl.loop(0, 2)
         def _(c):
@@ -440,13 +448,6 @@
             def _(c):
                 part_f(0, c, odd)
                 to_x(0, c, odd)
-        @pl.when(jnp.logical_not(more))
-        def _():
-            f_part(1)
-            for c in (0, 1):
-                g_chip(c)
-                emit_own(1, c)
-                emit(1, c)
         mlp_grads(rev, 1)
 
         @pl.when(more)
@@ -474,9 +475,11 @@
             attn_grads(rev - 1, finp)
             mlp_fwd(1)
 
+    gbuf[0, 1] = g_total(0)
+    emit(1, 0)
+    for c in (0, 1, None):
+        own_copy(c).wait()
     for c in (0, 1):
-        for idx in (0, 1):
-            own_copy(idx, c).wait()
         for idx in range(5):
             for cp in emit_copies(idx, c):
                 cp.wait()
@@ -526,29 +529,34 @@
     )(*arrays)
 
 
-def take_kernel(finish, *refs):
+def take_kernel(finish, first, *refs):
     *base, near_ref, far_ref, out_ref = refs
-    odd = lax.rem(pl.program_id(0) + lax.axis_index("tp"), 2)
-
-    @pl.when(odd == 0)
+    seq_idx = pl.program_id(0)
+    odd = lax.rem(seq_idx + lax.axis_index("tp"), 2)
+    ready = seq_idx < first
+
+    @pl.when(ready)
+    def _():
+        out_ref[...] = finish(None, *[ref[...] for ref in base])
+
+    @pl.when(jnp.logical_not(ready) & (odd == 0))
     def _():
         out_ref[...] = finish(near_ref[...].astype(F32), *[ref[...] for ref in base])
 
-    @pl.when(odd != 0)
+    @pl.when(jnp.logical_not(ready) & (odd != 0))
     def _():
         out_ref[...] = finish(far_ref[...].astype(F32), *[ref[...] for ref in base])
 
 
-def take(finish, name, shape, base, near, far, parts=2):
+def take(finish, first, name, shape, base, near, far):
     n_seq, seq, hid = shape
-    part = seq // parts
-    whole = pl.BlockSpec((1, part, hid), lambda s, r: (s, r, 0))
-    bottom = pl.BlockSpec((None, 1, part, hid), lambda s, r: (0, s, r, 0))
-    half = pl.BlockSpec((1, part, hid), lambda s, r: (s // 2, r, 0))
+    whole = pl.BlockSpec((1, seq, hid), lambda s: (s, 0, 0))
+    bottom = pl.BlockSpec((None, 1, seq, hid), lambda s: (0, s, 0, 0))
+    half = pl.BlockSpec((1, seq, hid), lambda s: (jnp.maximum(s - first, 0) // 2, 0, 0))
     return pl.pallas_call(
-        functools.partial(take_kernel, finish),
+        functools.partial(take_kernel, finish, first),
         out_shape=jax.ShapeDtypeStruct(shape, F32),
-        grid=(n_seq, parts),
+        grid=(n_seq,),
         in_specs=[whole if arr.ndim == 3 else bottom for arr in base] + [half, half],
         out_specs=whole,
         name=name,
@@ -557,11 +565,12 @@
 
 
 def finish_x(other, state, own):
-    return state - (own + other)
+    return state - (own if other is None else own + other)
 
 
 def finish_d(other, grad, state, own):
-    return grad + rms_pull(state, own.astype(F32) + other)
+    own = own.astype(F32)
+    return grad + rms_pull(state, own if other is None else own + other)
 
 
 def solution(mesh):
@@ -595,13 +604,13 @@
             vm((2,) + half, F32), vm(half, F32), vm(half, F32), vm((3, 256, hid), F32),
             dma((2, 2)), dma((2, 2)), dma((3, 2)), dma((3, 2)), dma((3, 2)), dma((3, 2)),
             dma((2,)), dma((2,)), dma((8,)), dma((8,)), dma((2,)), dma((2,)),
-            dma((5, 2)), dma((5, 2)), dma((5, 2)), dma((2, 2)), dma((2, 4)), dma((2,)), dma((2,)), dma((2,)), dma((3,)), dma((2, 2)),
+            dma((5, 2)), dma((5, 2)), dma((5, 2)), dma((3,)), dma((2, 4)), dma((2,)), dma((2,)), dma((2,)), dma((3,)), dma((2, 2)),
             pltpu.SemaphoreType.REGULAR,
         ]
         anyspec = pl.BlockSpec(memory_space=pl.ANY)
         outs = pl.pallas_call(
             functools.partial(chain_kernel, seq, hid, heads, hdim, n_pairs),
-            out_shape=[sds(half, F32), sds(half, BF), sds((tok, hid), F32), sds((tok, hid), BF)] + [sds((tok, hid), F32)] * 3
+            out_shape=[sds(half[1:], F32), sds(half, BF), sds((tok, hid), F32), sds((tok, hid), BF)] + [sds((tok, hid), F32)] * 3
             + [sds((n_layers, qkv_w, hid), F32), sds((n_layers, heads * hdim, hid), F32), sds((n_layers, hid, ff), F32), sds((n_layers, ff, hid), F32)],
             in_specs=[anyspec] * 10,
             out_specs=[anyspec] * 11,
@@ -618,8 +627,8 @@
         f_near, j_near, grads = lax.optimization_barrier((f_near, j_near, grads))
         f_far, j_far = over_core(f_near), over_core(j_near)
         states = [cube(out) for out in move([x_two, d_one], "move_states")]
-        x_one = take(finish_x, "finish_x", (n_seq, seq, hid), [saved_one, cube(f_all)], f_near, f_far)
-        dx_two = take(finish_d, "finish_d", (n_seq, seq, hid), [cube(d_two), cube(x_two), cube(j_all)], j_near, j_far)
+        x_one = take(finish_x, 2, "finish_x", (n_seq, seq, hid), [saved_one, cube(f_all)], f_near[None], f_far[None])
+        dx_two = take(finish_d, 0, "finish_d", (n_seq, seq, hid), [cube(d_two), cube(x_two), cube(j_all)], j_near, j_far)
         d_qkv = jnp.transpose(grads[0].reshape(n_layers, 3, heads, hdim, hid), (0, 4, 1, 2, 3))
         d_o = grads[1].reshape(n_layers, heads, hdim, hid)
         return (x_one, *states, dx_two, d_qkv, d_o, grads[2].reshape(n_layers, hid, ff), grads[3].reshape(n_layers, ff, hid))

time: 512 us -> 501 us (0.979)
  waiting for transfers between devices: 9.63 us -> 0.01 us
    ppermute x2, waiting for transfers between devices: 9.62 us -> 0.01 us  [per_device(): lax.ppermute(arr, 'tp', [(0, 2), (2, 0), (1, 3), (3, 1)])]
  transfers between devices with their start and end apart: 4 -> 4, of which waited for: 1 -> 0; matrix products, arithmetic and copies ran while one was open for 0% -> 0% of each run, Pallas kernels for 11% -> 10%
where the time goes in v8:
time: 501 us
  Pallas kernels  496 us (99%)
    pallas_call x1, Pallas kernels, per_device(): pl.pallas_call(functools.partial(chain_kernel, seq, hid, heads, hdim, n_p...  437 us
    pallas_call x2, Pallas kernels, move(): pl.pallas_call(functools.partial(move_kernel, depth, chunk), out_shape=[j...  47 us
    pallas_call x2, Pallas kernels, take(): pl.pallas_call(functools.partial(take_kernel, finish, first), out_shape=j...  11.6 us
  transfers between devices with their start and end apart: 4, of which 0 were waited for; matrix products, arithmetic and copies ran while one was open for 0% of the time, Pallas kernels for 10%

profile of v8, /device:TPU:0, one launch (start us, length us, event | category | flops | bytes accessed | tf_op | source)
XLA Modules:
  0.0 500.8 jit_solution(14613443221331340722)
XLA Ops:
  0.6 437.0 %chain.1 = (f32[256,768]{1,0:T(8,128)}, bf16[2,256,768]{2,1,0:T(8,128)(2,1)}, f32[1024,768]{1,0:T(8,128)}, bf16[1024,768]{1,0:T(8,128)(2,1)}, f32[1024,768]{1,0:...) custom-call(f32[1024,768]{1,0:T(8,128)} %bitcast.36, ...), custom_call_target="tpu_custom_call" | custom-call | tf_op jit(solution)/shard_map/chain/pallas_call | solution.py:611
  437.7 0.0 collective-permute-start
  437.7 2.0 collective-permute-start.1
  439.7 42.1 %move_grads.1 = (f32[5184,768]{1,0:T(8,128)}, f32[1728,768]{1,0:T(8,128)}, f32[6912,768]{1,0:T(8,128)}, f32[6912,768]{1,0:T(8,128)}) custom-call(f32[5184,768]{1,0:T(8,128)} %bitcast.31, f32[1728,768]{1,0:T(8,128)} %bitcast.35, f32[6912,768]{1,0:T(8,128)} %bitcast.29, f32[6912,768]{1,0:T(8,128)} %bitcast.30), custom_call_target="tpu_custom_call" | custom-call | flops 6370099200 | bytes 127401984 | tf_op jit(solution)/shard_map/move_grads/pallas_call | solution.py:520
  481.9 0.0 collective-permute-done
  481.9 0.0 copy-start
  481.9 0.0 collective-permute-done.1.refs_3_
  481.9 0.0 copy-start.2
  481.9 0.0 collective-permute-start.2
  481.9 0.5 collective-permute-start.3
  482.4 4.9 move_states.1
  487.4 0.0 copy-done
  487.4 0.0 copy-done.2
  487.4 0.0 collective-permute-done.2
  487.4 0.0 copy-start.1
  487.4 0.9 copy-done.1
  488.3 5.4 %finish_x.1 = f32[4,256,768]{2,1,0:T(8,128)} custom-call(f32[4,4,256,768]{3,2,1,0:T(8,128)} %refs_0_.1, f32[4,256,768]{2,1,0:T(8,128)} %bitcast.40, f32[1,256,768]{2,1,0:T(8,128)} %bitcast.44, f32[1,256,768]{2,1,0:T(8,128)} %bitcast.45), custom_call_target="tpu_custom_call" | custom-call | flops 40000000 | bytes 16000000 | tf_op jit(solution)/shard_map/finish_x/pallas_call | solution.py:556
  493.7 0.0 collective-permute-done.3.refs_4_
  493.7 0.0 copy-start.3
  493.7 0.9 copy-done.3
  494.6 6.2 %finish_d.1 = f32[4,256,768]{2,1,0:T(8,128)} custom-call(f32[4,256,768]{2,1,0:T(8,128)} %bitcast.41, f32[4,256,768]{2,1,0:T(8,128)} %bitcast.32, bf16[4,256,768]{2,1,0:T(8,128)(2,1)} %bitcast.43, bf16[2,256,768]{2,1,0:T(8,128)(2,1)} %copy-done.2, bf16[2,256,768]{2,1,0:T(8,128)(2,1)} %copy-done.3), custom_call_target="tpu_custom_call" | custom-call | flops 40000000 | bytes 16000000 | tf_op jit(solution)/shard_map/finish_d/pallas_call | solution.py:556
Async XLA Ops:
  437.7 44.2 %collective-permute-start = (f32[256,768]{1,0:T(8,128)}, f32[256,768]{1,0:T(8,128)S(1)}, u32[]{:S(2)}, u32[]{:S(2)}) collective-permute-start(f32[256,768]{1,0:T(8,128)} %get-tuple-element.32), channel_id=1, source_target_pairs={{0,2},{2,0},{1,3},{3,1},{4,6},{6,4},{5,7},{7,5},{8,10},{10,8},{9,1... | collective-permute-start | bytes 2359304 | tf_op jit(solution)/shard_map/ppermute | solution.py:623
  437.7 44.1 %collective-permute-start.1 = (bf16[2,256,768]{2,1,0:T(8,128)(2,1)}, bf16[2,256,768]{2,1,0:T(8,128)(2,1)S(1)}, u32[]{:S(2)}, u32[]{:S(2)}) collective-permute-start(bf16[2,256,768]{2,1,0:T(8,128)(2,1)} %get-tuple-element.33), channel_id=1, source_target_pairs={{0,2},{2,0},{1,3},{3,1},{4,6},{6,4},{5,7},{7,5},{8,10},{10,8},{9,1... | collective-permute-start | bytes 2359304 | tf_op jit(solution)/shard_map/ppermute | solution.py:623
  481.9 5.5 %copy-start = (f32[256,768]{1,0:T(8,128)}, f32[256,768]{1,0:T(8,128)S(1)}, u32[]{:S(2)}) copy-start(f32[256,768]{1,0:T(8,128)S(1)} %collective-permute-done) | copy-start | bytes 2359300
  481.9 5.5 %copy-start.2 = (bf16[2,256,768]{2,1,0:T(8,128)(2,1)}, bf16[2,256,768]{2,1,0:T(8,128)(2,1)S(1)}, u32[]{:S(2)}) copy-start(bf16[2,256,768]{2,1,0:T(8,128)(2,1)S(1)} %collective-permute-done.1.refs_3_) | copy-start | bytes 2359300
  481.9 5.5 %collective-permute-start.2 = (f32[256,768]{1,0:T(8,128)S(1)}, f32[256,768]{1,0:T(8,128)S(1)}, u32[]{:S(2)}, u32[]{:S(2)}) collective-permute-start(f32[256,768]{1,0:T(8,128)S(1)} %collective-permute-done), channel_id=1, source_target_pairs={{0,1},{1,0},{2,3},{3,2},{4,5},{5,4},{6,7},{7,6},{8,9},{9,8},{10,11... | collective-permute-start | bytes 2359304 | tf_op jit(solution)/shard_map/ppermute | solution.py:624
  481.9 11.7 %collective-permute-start.3 = (bf16[2,256,768]{2,1,0:T(8,128)(2,1)S(1)}, bf16[2,256,768]{2,1,0:T(8,128)(2,1)S(1)}, u32[]{:S(2)}, u32[]{:S(2)}) collective-permute-start(bf16[2,256,768]{2,1,0:T(8,128)(2,1)S(1)} %collective-permute-done.1.refs_3_), channel_id=1, source_target_pairs={{0,1},{1,0},{2,3},{3,2},{4,5},{5,4},{6,7},{7,6},{8,9},{9,8},{10,11... | collective-permute-start | bytes 2359304 | tf_op jit(solution)/shard_map/ppermute | solution.py:624
  487.4 0.9 copy-start.1
  493.7 0.9 copy-start.3

commit v9 on v8

--- a/solution.py
+++ b/solution.py
@@ -111,10 +111,11 @@
     def state_wait(dst, sem):
         local(y1.at[rows(0)], dst, sem).wait()
 
-    def each_seq(first, one, pair, body, order=lambda i: i):
+    def seq_start(first, one, pair, order=lambda i: i):
         for i in (0, 1):
             state_start(first, one, pair, rows(order(i)), xl.at[i], xl_s.at[i])
 
+    def each_seq(first, one, pair, body, order=lambda i: i):
         @pl.loop(0, 4)
         def _(i):
             slot = lax.rem(i, 2)
@@ -125,8 +126,8 @@
             def _():
                 state_start(first, one, pair, rows(order(i + 2)), xl.at[slot], xl_s.at[slot])
 
-    def mlp_fwd(slot):
-        @pl.loop(0, 4)
+    def mlp_fwd(slot, lo=0, hi=4):
+        @pl.loop(lo, hi)
         def _(s):
             value, grad = gelu_parts(dot(a_g[rows(s), :], wi[slot], NN), True)
             act[rows(s), :] = value.astype(BF)
@@ -275,7 +276,14 @@
                 gp[rows(s), :] = grad
             gbuf[i // 2, lax.rem(i, 2)] = dot(value, wu[slot], NN)
             g_send_core(i)
+
+            @pl.when(i == 2)
+            def _():
+                g_chip(0)
+                g_send(*range(npc))
         each_seq(first, True, pair, body, g_order)
+        g_chip(1)
+        g_send(*range(npc, 2 * npc))
 
     def f_part(slot):
         @pl.loop(0, 4)
@@ -325,21 +333,18 @@
             if cp is not None:
                 cp.wait()
 
-    def mlp_grads(blk, ver):
-        pending = [None] * 3
-        n_t = hid // 256
-        for k in range(n_t):
+    def mlp_out_grads(blk, ver, pending):
+        for k in range(hid // 256):
             put(pending, k, gu.at[blk, pl.ds(256 * k, 256)], dot(act[:, 256 * k:256 * (k + 1)], d2b[ver], TN))
-        for k in range(n_t):
+
+    def mlp_in_grads(blk, pending):
+        for k in range(hid // 256):
             put(pending, k, gi.at[blk, pl.ds(256 * k, 256)], dot(a_g[:, 256 * k:256 * (k + 1)], dhb[...], TN))
-        flush(pending)
-
-    def attn_grads(blk, fin):
-        pending = [None] * 3
+
+    def attn_grads(blk, fin, pending):
         for k in range(3):
             put(pending, k, gq.at[blk, pl.ds(qw * k, qw)], dot(dqkvt[qw * k:qw * (k + 1), :], fin[...], NN))
         put(pending, 3, go.at[blk], dot(ot[...], d1b[...], NN))
-        flush(pending)
 
     def v_start(first, one, pair, c):
         state_start(first, one, pair, rows(mine(c)), vbuf.at[c], v_s.at[c])
@@ -348,7 +353,8 @@
         state_wait(vbuf.at[c], v_s.at[c])
 
     top = 2 * n_pairs
-    w_start(1, top, "iuqo")
+    w_start(1, top, "iu")
+    seq_start(True, True, 0, g_order)
     for c in (0, 1):
         v_start(True, True, 0, c)
         state_start(True, False, 0, rows(mine(c)), x2r.at[c], x2_s.at[c])
@@ -356,10 +362,8 @@
         local(dy2.at[rows(mine(c))], d2f.at[c], d_s.at[1, c]).start()
     pl.semaphore_wait(barrier, 2)
     w_wait(1, "iu")
+    w_start(1, top, "qo")
     g_part(1, True, 0, True)
-    for c in (0, 1):
-        g_chip(c)
-        g_send(*range(npc * c, npc * (c + 1)))
     w_start(0, top - 1, "qoiu")
     for i in range(4):
         local(dy2.at[rows(i)], xl.at[i % 2], xl_s.at[i % 2]).start()
@@ -391,6 +395,7 @@
                 v_wait(c)
                 finish(0, c, 2, d2f, vbuf[c])
                 v_start(False, True, pair, c)
+                mlp_fwd(1, 2 * c, 2 * c + 2)
                 e3(2, c).wait()
                 part_g(1, 1, c, "add", odd)
                 to_x(1, c, odd)
@@ -424,18 +429,27 @@
             emit_own(None)
             emit(1, 1)
 
-        @pl.loop(0, 2)
-        def _(c):
+        pending = [None] * 3
+        for c in (0, 1):
             v_wait(c)
             finish(1, c, 0, d1f, vbuf[c])
 
             @pl.when(jnp.logical_not(more))
             def _():
                 emit(3, c)
+            if c == 0:
+                mlp_out_grads(rev, 1, pending)
+            else:
+                mlp_in_grads(rev, pending)
             e3(0, c).wait()
             part_f(1, c, even)
             to_x(2, c, even, jnp.logical_not(more))
-        attn_grads(rev, finr)
+
+        @pl.when(more)
+        def _():
+            seq_start(False, False, pair - 1)
+        attn_grads(rev, finr, pending)
+        flush(pending)
 
         @pl.when(more)
         def _():
@@ -444,20 +458,15 @@
                 v_start(False, False, pair - 1, c)
             w_wait(0, "qo")
             attn_fwd_plain(pair - 1)
+            seq_start(False, True, pair - 1, g_order)
+
             @pl.loop(0, 2)
             def _(c):
                 part_f(0, c, odd)
                 to_x(0, c, odd)
-        mlp_grads(rev, 1)
-
-        @pl.when(more)
-        def _():
             w_wait(1, "iu")
+            pl.semaphore_wait(gcred, 1)
             g_part(1, False, pair - 1, False)
-            for c in (0, 1):
-                g_chip(c)
-            pl.semaphore_wait(gcred, 1)
-            g_send(*range(2 * npc))
             w_wait(0, "iu")
             mlp_fwd(0)
             for c in (0, 1):
@@ -471,9 +480,11 @@
             @pl.when(it < n_pairs - 1)
             def _():
                 w_start(0, rev - 3, "qoiu")
-            mlp_grads(rev - 1, 0)
-            attn_grads(rev - 1, finp)
-            mlp_fwd(1)
+            later = [None] * 3
+            mlp_out_grads(rev - 1, 0, later)
+            mlp_in_grads(rev - 1, later)
+            attn_grads(rev - 1, finp, later)
+            flush(later)
 
     gbuf[0, 1] = g_total(0)
     emit(1, 0)
@@ -525,7 +536,7 @@
         scratch_shapes=[pltpu.VMEM((depth, chunk, width), F32), pltpu.SemaphoreType.DMA((depth,)), pltpu.SemaphoreType.DMA((depth,))],
         name=name,
         cost_estimate=pl.CostEstimate(flops=400 * size, bytes_accessed=8 * size, transcendentals=0),
-        compiler_params=pltpu.CompilerParams(vmem_limit_bytes=60 * 2 ** 20),
+        compiler_params=pltpu.CompilerParams(vmem_limit_bytes=depth * chunk * width * 4 + 2 ** 20),
     )(*arrays)
 
 

time: 501 us -> 501 us (level)
  Pallas kernels: 496 us -> 488 us
  local copies, waits for them, and re-layouts: 1.78 us -> 8.95 us
    unnamed x8 -> x12, local copies, waits for them, and re-layouts: 1.78 us -> 8.95 us
where the time goes in v9:
time: 501 us
  Pallas kernels  488 us (97%)
  local copies, waits for them, and re-layouts  8.95 us (2%)
    pallas_call x1, Pallas kernels, per_device(): pl.pallas_call(functools.partial(chain_kernel, seq, hid, heads, hdim, n_p...  434 us
    pallas_call x2, Pallas kernels, move(): pl.pallas_call(functools.partial(move_kernel, depth, chunk), out_shape=[j...  43 us
    pallas_call x2, Pallas kernels, take(): pl.pallas_call(functools.partial(take_kernel, finish, first), out_shape=j...  11.7 us
  transfers between devices with their start and end apart: 4, of which 0 were waited for; matrix products, arithmetic and copies ran while one was open for 0% of the time, Pallas kernels for 10%

profile of v9, /device:TPU:0, one launch (start us, length us, event | category | flops | bytes accessed | tf_op | source)
XLA Modules:
  0.0 500.7 jit_solution(6370115334065246727)
XLA Ops:
  0.6 433.8 %chain.1 = (f32[256,768]{1,0:T(8,128)}, bf16[2,256,768]{2,1,0:T(8,128)(2,1)}, f32[1024,768]{1,0:T(8,128)}, bf16[1024,768]{1,0:T(8,128)(2,1)}, f32[1024,768]{1,0:...) custom-call(f32[1024,768]{1,0:T(8,128)} %bitcast.36, ...), custom_call_target="tpu_custom_call" | custom-call | tf_op jit(solution)/shard_map/chain/pallas_call | solution.py:622
  434.4 0.0 collective-permute-start
  434.5 2.0 collective-permute-start.1
  436.5 0.0 copy-start
  436.5 5.5 %copy-done = f32[9,576,768]{2,1,0:T(8,128)S(1)} copy-done((f32[9,576,768]{2,1,0:T(8,128)S(1)}, f32[9,576,768]{2,1,0:T(8,128)}, u32[]{:S(2)}) %copy-start) | copy-done | bytes 15925272
  442.0 0.0 copy-start.2
  442.0 2.5 copy-done.2
  444.5 0.0 copy-start.1
  444.5 0.0 copy-start.3
  444.5 39.2 %move_grads.1 = (f32[5184,768]{1,0:T(8,128)}, f32[1728,768]{1,0:T(8,128)}, f32[6912,768]{1,0:T(8,128)}, f32[6912,768]{1,0:T(8,128)}) custom-call(f32[5184,768]{1,0:T(8,128)S(1)} %bitcast.28, f32[1728,768]{1,0:T(8,128)S(1)} %bitcast.30, f32[6912,768]{1,0:T(8,128)} %bitcast.32, f32[6912,768]{1,0:T(8,128)} %bitcast.33), custom_call_target="tpu_custom_call" | custom-call | flops 6370099200 | bytes 127401984 | tf_op jit(solution)/shard_map/move_grads/pallas_call | solution.py:531
  483.7 0.0 collective-permute-done
  483.7 0.0 copy-start.4
  483.8 0.0 collective-permute-done.1.refs_3_
  483.8 0.0 collective-permute-start.2
  483.8 0.5 collective-permute-start.3
  484.3 0.0 copy-done.1
  484.3 0.0 copy-done.3
  484.3 3.8 move_states.1
  488.2 0.0 copy-done.4
  488.2 0.0 collective-permute-done.2
  488.2 0.0 copy-start.5
  488.2 0.9 copy-done.5
  489.1 5.4 %finish_x.1 = f32[4,256,768]{2,1,0:T(8,128)} custom-call(f32[4,4,256,768]{3,2,1,0:T(8,128)} %refs_0_.1, f32[4,256,768]{2,1,0:T(8,128)} %bitcast.40, f32[1,256,768]{2,1,0:T(8,128)} %bitcast.44, f32[1,256,768]{2,1,0:T(8,128)} %bitcast.45), custom_call_target="tpu_custom_call" | custom-call | flops 40000000 | bytes 16000000 | tf_op jit(solution)/shard_map/finish_x/pallas_call | solution.py:567
  494.5 0.0 collective-permute-done.3.refs_4_
  494.5 6.2 %finish_d.1 = f32[4,256,768]{2,1,0:T(8,128)} custom-call(f32[4,256,768]{2,1,0:T(8,128)} %bitcast.41, f32[4,256,768]{2,1,0:T(8,128)} %bitcast.29, bf16[4,256,768]{2,1,0:T(8,128)(2,1)} %bitcast.43, bf16[2,256,768]{2,1,0:T(8,128)(2,1)} %collective-permute-done.1.refs_3_, bf16[2,256,768]{2,1,0:T(8,128)(2,1)} %collective-permute-done.3.refs_4_), custom_call_target="tpu_custom_call" | custom-call | flops 40000000 | bytes 16000000 | tf_op jit(solution)/shard_map/finish_d/pallas_call | solution.py:567
Async XLA Ops:
  434.4 49.3 %collective-permute-start = (f32[256,768]{1,0:T(8,128)}, f32[256,768]{1,0:T(8,128)S(1)}, u32[]{:S(2)}, u32[]{:S(2)}) collective-permute-start(f32[256,768]{1,0:T(8,128)} %get-tuple-element.32), channel_id=1, source_target_pairs={{0,2},{2,0},{1,3},{3,1},{4,6},{6,4},{5,7},{7,5},{8,10},{10,8},{9,1... | collective-permute-start | bytes 2359304 | tf_op jit(solution)/shard_map/ppermute | solution.py:634
  434.5 49.3 %collective-permute-start.1 = (bf16[2,256,768]{2,1,0:T(8,128)(2,1)}, bf16[2,256,768]{2,1,0:T(8,128)(2,1)}, u32[]{:S(2)}, u32[]{:S(2)}) collective-permute-start(bf16[2,256,768]{2,1,0:T(8,128)(2,1)} %get-tuple-element.33), channel_id=1, source_target_pairs={{0,2},{2,0},{1,3},{3,1},{4,6},{6,4},{5,7},{7,5},{8,10},{10,8},{9,1... | collective-permute-start | bytes 2359304 | tf_op jit(solution)/shard_map/ppermute | solution.py:634
  436.5 5.5 %copy-start = (f32[9,576,768]{2,1,0:T(8,128)S(1)}, f32[9,576,768]{2,1,0:T(8,128)}, u32[]{:S(2)}) copy-start(f32[9,576,768]{2,1,0:T(8,128)} %get-tuple-element.34) | copy-start | bytes 47775748
  442.0 2.5 copy-start.2
  444.5 39.8 %copy-start.1 = (f32[1024,768]{1,0:T(8,128)S(1)}, f32[1024,768]{1,0:T(8,128)}, u32[]{:S(2)}) copy-start(f32[1024,768]{1,0:T(8,128)} %get-tuple-element.43.refs_0_) | copy-start | bytes 9437188
  444.5 39.8 %copy-start.3 = (f32[1024,768]{1,0:T(8,128)S(1)}, f32[1024,768]{1,0:T(8,128)}, u32[]{:S(2)}) copy-start(f32[1024,768]{1,0:T(8,128)} %get-tuple-element.44.refs_1_) | copy-start | bytes 9437188
  483.7 4.4 copy-start.4
  483.8 4.4 collective-permute-start.2
  483.8 10.7 %collective-permute-start.3 = (bf16[2,256,768]{2,1,0:T(8,128)(2,1)}, bf16[2,256,768]{2,1,0:T(8,128)(2,1)}, u32[]{:S(2)}, u32[]{:S(2)}) collective-permute-start(bf16[2,256,768]{2,1,0:T(8,128)(2,1)} %collective-permute-done.1.refs_3_), channel_id=1, source_target_pairs={{0,1},{1,0},{2,3},{3,2},{4,5},{5,4},{6,7},{7,6},{8,9},{9,8},{10,11... | collective-permute-start | bytes 2359304 | tf_op jit(solution)/shard_map/ppermute | solution.py:635
  488.2 0.9 copy-start.5

commit v10 on v9

--- a/solution.py
+++ b/solution.py
@@ -13,6 +13,7 @@
 MESH = pl.DeviceIdType.MESH
 GELU_C = 0.7978845608028654
 GELU_A = 0.044715
+GRANT = 40
 
 NN = (((1,), (0,)), ((), ()))
 NT = (((1,), (1,)), ((), ()))
@@ -536,7 +537,7 @@
         scratch_shapes=[pltpu.VMEM((depth, chunk, width), F32), pltpu.SemaphoreType.DMA((depth,)), pltpu.SemaphoreType.DMA((depth,))],
         name=name,
         cost_estimate=pl.CostEstimate(flops=400 * size, bytes_accessed=8 * size, transcendentals=0),
-        compiler_params=pltpu.CompilerParams(vmem_limit_bytes=depth * chunk * width * 4 + 2 ** 20),
+        compiler_params=pltpu.CompilerParams(vmem_limit_bytes=60 * 2 ** 20),
     )(*arrays)
 
 
@@ -572,6 +573,7 @@
         out_specs=whole,
         name=name,
         cost_estimate=pl.CostEstimate(flops=40_000_000, bytes_accessed=16_000_000, transcendentals=0),
+        compiler_params=pltpu.CompilerParams(vmem_limit_bytes=GRANT * 2 ** 20),
     )(*base, near, far)
 
 

time: 501 us -> 496 us (0.990)
  local copies, waits for them, and re-layouts: 8.95 us -> 0.93 us
    unnamed x12 -> x8, local copies, waits for them, and re-layouts: 8.95 us -> 0.93 us
  transfers between devices with their start and end apart: 4 -> 4, of which waited for: 0 -> 0; matrix products, arithmetic and copies ran while one was open for 0% -> 0% of each run, Pallas kernels for 10% -> 11%
where the time goes in v10:
time: 496 us; the launch traced here: 495 us
  Pallas kernels  491 us (99%)
    pallas_call x1, Pallas kernels, per_device(): pl.pallas_call(functools.partial(chain_kernel, seq, hid, heads, hdim, n_p...  434 us
    pallas_call x2, Pallas kernels, move(): pl.pallas_call(functools.partial(move_kernel, depth, chunk), out_shape=[j...  47.2 us
    pallas_call x2, Pallas kernels, take(): pl.pallas_call(functools.partial(take_kernel, finish, first), out_shape=j...  10.2 us
  transfers between devices with their start and end apart: 4, of which 0 were waited for; matrix products, arithmetic and copies ran while one was open for 0% of the time, Pallas kernels for 11%

profile of v10, /device:TPU:0, one launch (start us, length us, event | category | flops | bytes accessed | tf_op | source)
XLA Modules:
  0.0 495.4 jit_solution(820958113555190234)
XLA Ops:
  0.6 433.8 %chain.1 = (f32[256,768]{1,0:T(8,128)}, bf16[2,256,768]{2,1,0:T(8,128)(2,1)}, f32[1024,768]{1,0:T(8,128)}, bf16[1024,768]{1,0:T(8,128)(2,1)}, f32[1024,768]{1,0:...) custom-call(f32[1024,768]{1,0:T(8,128)} %bitcast.40, ...), custom_call_target="tpu_custom_call" | custom-call | tf_op jit(solution)/shard_map/chain/pallas_call | solution.py:624
  434.4 0.0 collective-permute-start
  434.5 2.0 collective-permute-start.1
  436.5 42.1 %move_grads.1 = (f32[5184,768]{1,0:T(8,128)}, f32[1728,768]{1,0:T(8,128)}, f32[6912,768]{1,0:T(8,128)}, f32[6912,768]{1,0:T(8,128)}) custom-call(f32[5184,768]{1,0:T(8,128)} %bitcast.36, f32[1728,768]{1,0:T(8,128)} %bitcast.39, f32[6912,768]{1,0:T(8,128)} %bitcast.34, f32[6912,768]{1,0:T(8,128)} %bitcast.35), custom_call_target="tpu_custom_call" | custom-call | flops 6370099200 | bytes 127401984 | tf_op jit(solution)/shard_map/move_grads/pallas_call | solution.py:532
  478.6 0.0 collective-permute-done
  478.6 0.0 collective-permute-done.1.refs_3_
  478.6 0.0 collective-permute-start.2
  478.7 0.5 collective-permute-start.3
  479.2 0.0 copy-start.1
  479.2 5.1 %move_states.1 = (f32[1024,768]{1,0:T(8,128)}, f32[1024,768]{1,0:T(8,128)}) custom-call(f32[1024,768]{1,0:T(8,128)} %get-tuple-element.43.refs_0_, f32[1024,768]{1,0:T(8,128)} %get-tuple-element.44.refs_1_), custom_call_target="tpu_custom_call" | custom-call | flops 629145600 | bytes 12582912 | tf_op jit(solution)/shard_map/move_states/pallas_call | solution.py:532
  484.2 0.0 collective-permute-done.2
  484.3 0.9 copy-done.1
  485.2 0.0 copy-start
  485.2 0.0 copy-start.2
  485.2 0.0 copy-start.3
  485.2 5.4 %finish_x.1 = f32[4,256,768]{2,1,0:T(8,128)} custom-call(f32[4,4,256,768]{3,2,1,0:T(8,128)} %refs_0_.1, f32[4,256,768]{2,1,0:T(8,128)S(1)} %bitcast.29, f32[1,256,768]{2,1,0:T(8,128)S(1)} %bitcast.32, f32[1,256,768]{2,1,0:T(8,128)} %bitcast.15.refs_3_), custom_call_target="tpu_custom_call" | custom-call | flops 40000000 | bytes 16000000 | tf_op jit(solution)/shard_map/finish_x/pallas_call | solution.py:568
  490.6 0.0 collective-permute-done.3.refs_4_
  490.6 0.0 copy-done
  490.6 0.0 copy-done.2
  490.6 0.0 copy-done.3
  490.6 4.8 finish_d.1
Async XLA Ops:
  434.4 44.2 %collective-permute-start = (f32[256,768]{1,0:T(8,128)}, f32[256,768]{1,0:T(8,128)S(1)}, u32[]{:S(2)}, u32[]{:S(2)}) collective-permute-start(f32[256,768]{1,0:T(8,128)} %get-tuple-element.32), channel_id=1, source_target_pairs={{0,2},{2,0},{1,3},{3,1},{4,6},{6,4},{5,7},{7,5},{8,10},{10,8},{9,1... | collective-permute-start | bytes 2359304 | tf_op jit(solution)/shard_map/ppermute | solution.py:636
  434.5 44.1 %collective-permute-start.1 = (bf16[2,256,768]{2,1,0:T(8,128)(2,1)}, bf16[2,256,768]{2,1,0:T(8,128)(2,1)}, u32[]{:S(2)}, u32[]{:S(2)}) collective-permute-start(bf16[2,256,768]{2,1,0:T(8,128)(2,1)} %get-tuple-element.33), channel_id=1, source_target_pairs={{0,2},{2,0},{1,3},{3,1},{4,6},{6,4},{5,7},{7,5},{8,10},{10,8},{9,1... | collective-permute-start | bytes 2359304 | tf_op jit(solution)/shard_map/ppermute | solution.py:636
  478.6 5.6 %collective-permute-start.2 = (f32[256,768]{1,0:T(8,128)S(1)}, f32[256,768]{1,0:T(8,128)}, u32[]{:S(2)}, u32[]{:S(2)}) collective-permute-start(f32[256,768]{1,0:T(8,128)S(1)} %collective-permute-done), channel_id=1, source_target_pairs={{0,1},{1,0},{2,3},{3,2},{4,5},{5,4},{6,7},{7,6},{8,9},{9,8},{10,11... | collective-permute-start | bytes 2359304 | tf_op jit(solution)/shard_map/ppermute | solution.py:637
  478.7 11.9 %collective-permute-start.3 = (bf16[2,256,768]{2,1,0:T(8,128)(2,1)}, bf16[2,256,768]{2,1,0:T(8,128)(2,1)}, u32[]{:S(2)}, u32[]{:S(2)}) collective-permute-start(bf16[2,256,768]{2,1,0:T(8,128)(2,1)} %collective-permute-done.1.refs_3_), channel_id=1, source_target_pairs={{0,1},{1,0},{2,3},{3,2},{4,5},{5,4},{6,7},{7,6},{8,9},{9,8},{10,11... | collective-permute-start | bytes 2359304 | tf_op jit(solution)/shard_map/ppermute | solution.py:637
  479.2 6.0 %copy-start.1 = (f32[1024,768]{1,0:T(8,128)S(1)}, f32[1024,768]{1,0:T(8,128)}, u32[]{:S(2)}) copy-start(f32[1024,768]{1,0:T(8,128)} %get-tuple-element.31) | copy-start | bytes 9437188
  485.2 5.4 %copy-start = (f32[1024,768]{1,0:T(8,128)S(1)}, f32[1024,768]{1,0:T(8,128)}, u32[]{:S(2)}) copy-start(f32[1024,768]{1,0:T(8,128)} %get-tuple-element.43.refs_0_) | copy-start | bytes 9437188
  485.2 5.4 %copy-start.2 = (f32[1024,768]{1,0:T(8,128)S(1)}, f32[1024,768]{1,0:T(8,128)}, u32[]{:S(2)}) copy-start(f32[1024,768]{1,0:T(8,128)} %get-tuple-element.47) | copy-start | bytes 9437188
  485.2 5.4 %copy-start.3 = (bf16[1024,768]{1,0:T(8,128)(2,1)S(1)}, bf16[1024,768]{1,0:T(8,128)(2,1)}, u32[]{:S(2)}) copy-start(bf16[1024,768]{1,0:T(8,128)(2,1)} %get-tuple-element.48) | copy-start | bytes 4718596

commit v11 on v10

--- a/solution.py
+++ b/solution.py
@@ -541,8 +541,10 @@
     )(*arrays)
 
 
-def take_kernel(finish, first, *refs):
-    *base, near_ref, far_ref, out_ref = refs
+def take_kernel(finish, first, keep, *refs):
+    *base, near_ref, far_ref, out_ref = refs[:-1] if keep else refs
+    if keep:
+        refs[-1][...] = base[1][...]
     seq_idx = pl.program_id(0)
     odd = lax.rem(seq_idx + lax.axis_index("tp"), 2)
     ready = seq_idx < first
@@ -560,17 +562,17 @@
         out_ref[...] = finish(far_ref[...].astype(F32), *[ref[...] for ref in base])
 
 
-def take(finish, first, name, shape, base, near, far):
+def take(finish, first, name, shape, base, near, far, keep=False):
     n_seq, seq, hid = shape
     whole = pl.BlockSpec((1, seq, hid), lambda s: (s, 0, 0))
     bottom = pl.BlockSpec((None, 1, seq, hid), lambda s: (0, s, 0, 0))
     half = pl.BlockSpec((1, seq, hid), lambda s: (jnp.maximum(s - first, 0) // 2, 0, 0))
     return pl.pallas_call(
-        functools.partial(take_kernel, finish, first),
-        out_shape=jax.ShapeDtypeStruct(shape, F32),
+        functools.partial(take_kernel, finish, first, keep),
+        out_shape=[jax.ShapeDtypeStruct(shape, F32)] * (1 + keep),
         grid=(n_seq,),
         in_specs=[whole if arr.ndim == 3 else bottom for arr in base] + [half, half],
-        out_specs=whole,
+        out_specs=[whole] * (1 + keep),
         name=name,
         cost_estimate=pl.CostEstimate(flops=40_000_000, bytes_accessed=16_000_000, transcendentals=0),
         compiler_params=pltpu.CompilerParams(vmem_limit_bytes=GRANT * 2 ** 20),
@@ -639,12 +641,12 @@
         grads = move([out.reshape(-1, hid) for out in outs[7:]], "move_grads")
         f_near, j_near, grads = lax.optimization_barrier((f_near, j_near, grads))
         f_far, j_far = over_core(f_near), over_core(j_near)
-        states = [cube(out) for out in move([x_two, d_one], "move_states")]
-        x_one = take(finish_x, 2, "finish_x", (n_seq, seq, hid), [saved_one, cube(f_all)], f_near[None], f_far[None])
-        dx_two = take(finish_d, 0, "finish_d", (n_seq, seq, hid), [cube(d_two), cube(x_two), cube(j_all)], j_near, j_far)
+        d_one = cube(move([d_one], "move_states")[0])
+        x_one, = take(finish_x, 2, "finish_x", (n_seq, seq, hid), [saved_one, cube(f_all)], f_near[None], f_far[None])
+        dx_two, x_two = take(finish_d, 0, "finish_d", (n_seq, seq, hid), [cube(d_two), cube(x_two), cube(j_all)], j_near, j_far, keep=True)
         d_qkv = jnp.transpose(grads[0].reshape(n_layers, 3, heads, hdim, hid), (0, 4, 1, 2, 3))
         d_o = grads[1].reshape(n_layers, heads, hdim, hid)
-        return (x_one, *states, dx_two, d_qkv, d_o, grads[2].reshape(n_layers, hid, ff), grads[3].reshape(n_layers, ff, hid))
+        return (x_one, x_two, d_one, dx_two, d_qkv, d_o, grads[2].reshape(n_layers, hid, ff), grads[3].reshape(n_layers, ff, hid))
 
     return jax.shard_map(
         per_device,

time: 496 us -> 494 us (level)
  transfers between devices with their start and end apart: 4 -> 4, of which waited for: 0 -> 0; matrix products, arithmetic and copies ran while one was open for 0% -> 0% of each run, Pallas kernels for 11% -> 10%
where the time goes in v11:
time: 494 us; the launch traced here: 493 us
  Pallas kernels  490 us (99%)
    pallas_call x1, Pallas kernels, per_device(): pl.pallas_call(functools.partial(chain_kernel, seq, hid, heads, hdim, n_p...  434 us
    pallas_call x2, Pallas kernels, move(): pl.pallas_call(functools.partial(move_kernel, depth, chunk), out_shape=[j...  45.4 us
    pallas_call x2, Pallas kernels, take(): pl.pallas_call(functools.partial(take_kernel, finish, first, keep), out_s...  10.7 us
  transfers between devices with their start and end apart: 4, of which 0 were waited for; matrix products, arithmetic and copies ran while one was open for 0% of the time, Pallas kernels for 10%

profile of v11, /device:TPU:0, one launch (start us, length us, event | category | flops | bytes accessed | tf_op | source)
XLA Modules:
  0.0 493.4 jit_solution(8476225941717970192)
XLA Ops:
  0.6 433.8 %chain.1 = (f32[256,768]{1,0:T(8,128)}, bf16[2,256,768]{2,1,0:T(8,128)(2,1)}, f32[1024,768]{1,0:T(8,128)}, bf16[1024,768]{1,0:T(8,128)(2,1)}, f32[1024,768]{1,0:...) custom-call(f32[1024,768]{1,0:T(8,128)} %bitcast.39, ...), custom_call_target="tpu_custom_call" | custom-call | tf_op jit(solution)/shard_map/chain/pallas_call | solution.py:626
  434.4 0.0 collective-permute-start
  434.5 2.0 collective-permute-start.1
  436.5 42.1 %move_grads.1 = (f32[5184,768]{1,0:T(8,128)}, f32[1728,768]{1,0:T(8,128)}, f32[6912,768]{1,0:T(8,128)}, f32[6912,768]{1,0:T(8,128)}) custom-call(f32[5184,768]{1,0:T(8,128)} %bitcast.35, f32[1728,768]{1,0:T(8,128)} %bitcast.38, f32[6912,768]{1,0:T(8,128)} %bitcast.33, f32[6912,768]{1,0:T(8,128)} %bitcast.34), custom_call_target="tpu_custom_call" | custom-call | flops 6370099200 | bytes 127401984 | tf_op jit(solution)/shard_map/move_grads/pallas_call | solution.py:532
  478.6 0.0 collective-permute-done
  478.6 0.0 collective-permute-done.1.refs_3_
  478.6 0.0 collective-permute-start.2
  478.7 0.5 collective-permute-start.3
  479.2 0.0 copy-start
  479.2 3.3 move_states.1
  482.5 0.0 collective-permute-done.2
  482.5 0.1 copy-done
  482.6 0.0 copy-start.1
  482.6 0.0 copy-start.2
  482.6 0.0 copy-start.3
  482.6 5.4 %finish_x.1 = f32[4,256,768]{2,1,0:T(8,128)} custom-call(f32[4,4,256,768]{3,2,1,0:T(8,128)} %refs_0_.1, f32[4,256,768]{2,1,0:T(8,128)S(1)} %bitcast.27, f32[1,256,768]{2,1,0:T(8,128)S(1)} %bitcast.31, f32[1,256,768]{2,1,0:T(8,128)} %bitcast.15.refs_3_), custom_call_target="tpu_custom_call" | custom-call | flops 40000000 | bytes 16000000 | tf_op jit(solution)/shard_map/finish_x/pallas_call | solution.py:570
  488.0 0.0 collective-permute-done.3.refs_4_
  488.1 0.0 copy-done.1
  488.1 0.0 copy-done.2
  488.1 0.0 copy-done.3
  488.1 5.3 %finish_d.1 = (f32[4,256,768]{2,1,0:T(8,128)}, f32[4,256,768]{2,1,0:T(8,128)}) custom-call(f32[4,256,768]{2,1,0:T(8,128)S(1)} %bitcast.29, f32[4,256,768]{2,1,0:T(8,128)S(1)} %bitcast.28, bf16[4,256,768]{2,1,0:T(8,128)(2,1)S(1)} %bitcast.30, bf16[2,256,768]{2,1,0:T(8,128)(2,1)} %collective-permute-done.1.refs_3_, ...), custom_call_target="tpu_custom_call" | custom-call | flops 40000000 | bytes 16000000 | tf_op jit(solution)/shard_map/finish_d/pallas_call | solution.py:570
Async XLA Ops:
  434.4 44.2 %collective-permute-start = (f32[256,768]{1,0:T(8,128)}, f32[256,768]{1,0:T(8,128)S(1)}, u32[]{:S(2)}, u32[]{:S(2)}) collective-permute-start(f32[256,768]{1,0:T(8,128)} %get-tuple-element.32), channel_id=1, source_target_pairs={{0,2},{2,0},{1,3},{3,1},{4,6},{6,4},{5,7},{7,5},{8,10},{10,8},{9,1... | collective-permute-start | bytes 2359304 | tf_op jit(solution)/shard_map/ppermute | solution.py:638
  434.5 44.1 %collective-permute-start.1 = (bf16[2,256,768]{2,1,0:T(8,128)(2,1)}, bf16[2,256,768]{2,1,0:T(8,128)(2,1)}, u32[]{:S(2)}, u32[]{:S(2)}) collective-permute-start(bf16[2,256,768]{2,1,0:T(8,128)(2,1)} %get-tuple-element.33), channel_id=1, source_target_pairs={{0,2},{2,0},{1,3},{3,1},{4,6},{6,4},{5,7},{7,5},{8,10},{10,8},{9,1... | collective-permute-start | bytes 2359304 | tf_op jit(solution)/shard_map/ppermute | solution.py:638
  478.6 3.9 collective-permute-start.2
  478.7 9.4 %collective-permute-start.3 = (bf16[2,256,768]{2,1,0:T(8,128)(2,1)}, bf16[2,256,768]{2,1,0:T(8,128)(2,1)}, u32[]{:S(2)}, u32[]{:S(2)}) collective-permute-start(bf16[2,256,768]{2,1,0:T(8,128)(2,1)} %collective-permute-done.1.refs_3_), channel_id=1, source_target_pairs={{0,1},{1,0},{2,3},{3,2},{4,5},{5,4},{6,7},{7,6},{8,9},{9,8},{10,11... | collective-permute-start | bytes 2359304 | tf_op jit(solution)/shard_map/ppermute | solution.py:639
  479.2 3.5 copy-start
  482.6 5.4 %copy-start.1 = (f32[1024,768]{1,0:T(8,128)S(1)}, f32[1024,768]{1,0:T(8,128)}, u32[]{:S(2)}) copy-start(f32[1024,768]{1,0:T(8,128)} %get-tuple-element.44) | copy-start | bytes 9437188
  482.6 5.4 %copy-start.2 = (f32[1024,768]{1,0:T(8,128)S(1)}, f32[1024,768]{1,0:T(8,128)}, u32[]{:S(2)}) copy-start(f32[1024,768]{1,0:T(8,128)} %get-tuple-element.43) | copy-start | bytes 9437188
  482.6 5.4 %copy-start.3 = (bf16[1024,768]{1,0:T(8,128)(2,1)S(1)}, bf16[1024,768]{1,0:T(8,128)(2,1)}, u32[]{:S(2)}) copy-start(bf16[1024,768]{1,0:T(8,128)(2,1)} %get-tuple-element.45) | copy-start | bytes 4718596
